TPU v7x, 8 devices: a whole 2x2x1 slice. The times are simulated.
8 devices in a mesh: dp: 2 (over z, y), tp: 4 (over x, core).
Axes of the slice: x: 2, y: 2, z: 1, core: 2. Of those that a mesh axis runs over, the one named last changes fastest.
Arguments:
- x: bfloat16 [1024, 2048], P('dp'), parts along dimension 0
- k_cache: bfloat16 [1024, 32, 16, 128], P('dp', None, 'tp'), parts along dimension 0
- v_cache: bfloat16 [1024, 32, 16, 128], P('dp', None, 'tp'), parts along dimension 0
- positions: int32 [1024], P('dp'), parts along dimension 0
- att_ids: int32 [1024, 2], P('dp'), parts along dimension 0
- mlp_ids: int32 [1024, 2], P('dp'), parts along dimension 0
- norm_att: float32 [2048], replicated
- w_kv: bfloat16 [2048, 16, 256], P(None, 'tp')
- router_att: bfloat16 [2048, 8], replicated
- w_query: bfloat16 [8, 2048, 2048], P(None, None, 'tp')
- w_out: bfloat16 [8, 2048, 2048], P(None, 'tp')
- norm_mlp: float32 [2048], replicated
- router_mlp: bfloat16 [2048, 8], replicated
- w_gate: bfloat16 [8, 2048, 5632], P('tp')
- w_up: bfloat16 [8, 2048, 5632], P('tp')
- w_down: bfloat16 [8, 5632, 2048], P('tp')
Outputs:
- output 1: bfloat16 [1024, 2048], P('dp'), parts along dimension 0
- output 2: bfloat16 [1024, 32, 16, 128], P('dp', None, 'tp'), parts along dimension 0
- output 3: bfloat16 [1024, 32, 16, 128], P('dp', None, 'tp'), parts along dimension 0
There are 2 independent parts. A program takes and returns all parts, laid end to end along the dimension named above; an argument that names none is the same for every part.
All inputs are finite; a program needn't handle non-finite values.
Results may differ from a plain program's by a relative error of at most 0.012235.
Values are sent between devices in bfloat16 or wider.
A program may use at most 1 GiB of HBM per device.

v0:
```python
import jax
import jax.numpy as jnp
from jax import lax
from jax.sharding import PartitionSpec as P

NORM_EPS = 1e-6
ROPE_BASE = 10000.0


def rms_norm(x, gain):
    values = x.astype(jnp.float32)
    inv_rms = lax.rsqrt(jnp.mean(values * values, axis=-1, keepdims=True) + NORM_EPS)
    return (values * inv_rms * gain).astype(jnp.bfloat16)


def rope_tables(positions, head_dim):
    half_dim = head_dim // 2
    inv_freq = ROPE_BASE ** (-(jnp.arange(half_dim, dtype=jnp.float32) * 2.0 / head_dim))
    angles = positions.astype(jnp.float32)[:, None] * inv_freq[None, :]
    return jnp.cos(angles), jnp.sin(angles)


def apply_rope(vectors, cos_table, sin_table):
    half_dim = vectors.shape[-1] // 2
    first_half = vectors[..., :half_dim]
    second_half = vectors[..., half_dim:]
    return jnp.concatenate([first_half * cos_table - second_half * sin_table, second_half * cos_table + first_half * sin_table], axis=-1)


def route_weights(logits, choice_ids, first_id, count):
    pair_gates = jax.nn.softmax(jnp.take_along_axis(logits, choice_ids, axis=1), axis=-1)
    expert_index = first_id + jnp.arange(count)
    onehot = (choice_ids[:, :, None] == expert_index[None, None, :]).astype(jnp.float32)
    dense_gates = jnp.sum(onehot * pair_gates[:, :, None], axis=1)
    return onehot, dense_gates


def attention_part(hidden, k_cache, v_cache, positions, att_ids, w_kv, router_att, w_query, w_out):
    tokens = hidden.shape[0]
    head_count = k_cache.shape[2]
    head_dim = k_cache.shape[3]
    kv_new = jnp.einsum('bd,dnc->bnc', hidden, w_kv, preferred_element_type=jnp.float32)
    cos_table, sin_table = rope_tables(positions, head_dim)
    key_new = apply_rope(kv_new[:, :, :head_dim], cos_table[:, None, :], sin_table[:, None, :]).astype(jnp.bfloat16)
    value_new = kv_new[:, :, head_dim:].astype(jnp.bfloat16)
    slot_index = jnp.arange(k_cache.shape[1])
    at_slot = (slot_index[None, :] == positions[:, None])[:, :, None, None]
    keys_all = jnp.where(at_slot, key_new[:, None, :, :], k_cache)
    values_all = jnp.where(at_slot, value_new[:, None, :, :], v_cache)
    att_logits = jnp.dot(hidden, router_att, preferred_element_type=jnp.float32)
    att_onehot, att_dense = route_weights(att_logits, att_ids, 0, w_query.shape[0])
    query_all = jnp.einsum('bd,edc->bec', hidden, w_query, preferred_element_type=jnp.float32)
    query_sel = jnp.take_along_axis(query_all, att_ids[:, :, None], axis=1).reshape(tokens, 2, head_count, head_dim)
    query_rot = apply_rope(query_sel, cos_table[:, None, None, :], sin_table[:, None, None, :]).astype(jnp.bfloat16)
    scores = jnp.einsum('bknd,bsnd->bkns', query_rot, keys_all, preferred_element_type=jnp.float32) * head_dim ** -0.5
    visible = (slot_index[None, :] <= positions[:, None])[:, None, None, :]
    weights = jax.nn.softmax(jnp.where(visible, scores, -1e30), axis=-1).astype(jnp.bfloat16)
    attended = jnp.einsum('bkns,bsnd->bknd', weights, values_all, preferred_element_type=jnp.float32).astype(jnp.bfloat16).reshape(tokens, 2, head_count * head_dim)
    out_slots = jnp.einsum('bke,bkc->bec', att_onehot.astype(jnp.bfloat16), attended, preferred_element_type=jnp.float32).astype(jnp.bfloat16)
    projected = jnp.einsum('bec,ecd->bed', out_slots, w_out, preferred_element_type=jnp.float32)
    att_part = jnp.sum(att_dense[:, :, None] * projected, axis=1)
    return att_part, keys_all, values_all


def expert_part(normed, mlp_dense, w_gate, w_up, w_down):
    gate_val = jnp.einsum('bd,edf->bef', normed, w_gate, preferred_element_type=jnp.float32)
    up_val = jnp.einsum('bd,edf->bef', normed, w_up, preferred_element_type=jnp.float32)
    activation = (jax.nn.silu(gate_val) * up_val).astype(jnp.bfloat16)
    down_out = jnp.einsum('bef,efd->bed', activation, w_down, preferred_element_type=jnp.float32)
    return jnp.sum(mlp_dense[:, :, None] * down_out, axis=1)


def solution(mesh):
    def local_step(x, k_cache, v_cache, positions, att_ids, mlp_ids, norm_att, w_kv, router_att, w_query, w_out, norm_mlp, router_mlp, w_gate, w_up, w_down):
        hidden = rms_norm(x, norm_att)
        att_part, keys_all, values_all = attention_part(hidden, k_cache, v_cache, positions, att_ids, w_kv, router_att, w_query, w_out)
        att_sum = lax.psum(att_part.astype(jnp.bfloat16), 'tp').astype(jnp.float32)
        x_mid = (x.astype(jnp.float32) + att_sum).astype(jnp.bfloat16)
        normed = rms_norm(x_mid, norm_mlp)
        mlp_logits = jnp.dot(normed, router_mlp, preferred_element_type=jnp.float32)
        local_count = w_gate.shape[0]
        _, mlp_dense = route_weights(mlp_logits, mlp_ids, lax.axis_index('tp') * local_count, local_count)
        mlp_part = expert_part(normed, mlp_dense, w_gate, w_up, w_down)
        mlp_sum = lax.psum(mlp_part.astype(jnp.bfloat16), 'tp').astype(jnp.float32)
        x_out = (x_mid.astype(jnp.float32) + mlp_sum).astype(jnp.bfloat16)
        return x_out, keys_all, values_all

    token_spec = P('dp', None)
    cache_spec = P('dp', None, 'tp', None)
    expert_spec = P('tp', None, None)
    in_specs = (token_spec, cache_spec, cache_spec, P('dp'), token_spec, token_spec, P(), P(None, 'tp', None), P(), P(None, None, 'tp'), P(None, 'tp', None), P(), P(), expert_spec, expert_spec, expert_spec)
    out_specs = (token_spec, cache_spec, cache_spec)
    return jax.shard_map(local_step, mesh=mesh, in_specs=in_specs, out_specs=out_specs, check_vma=False)
```

profile of v0, /device:TPU:0, one launch (start us, length us, event | category | flops | bytes accessed | tf_op | source)
XLA Modules:
  0.0 378.7 jit_solution(17237843874713732390)
XLA Ops:
  7.2 0.7 convert_element_type.68
  7.9 1.4 iota_compare_fusion
  9.4 2.1 fusion.8
  11.5 5.3 %fusion.17 = f32[512,4,256]{0,2,1:T(8,128)S(1)} fusion(bf16[2048,4,256]{2,1,0:T(4,128)(2,1)} %param.25, bf16[512,2048]{1,0:T(8,128)(2,1)} %param.18, f32[2048]{0:T(1024)} %param.24, f32[512]{0:T(512)S(1)} %add_rsqrt_fusion.1), kind=kOutput, calls=%fused_computation.31 | convolution fusion | flops 2151677952 | bytes 8398848 | tf_op jit(solution)/shard_map/bd,dnc->bnc/dot_general | solution.py:42
  16.8 1.3 copy-done.7
  18.1 0.9 slice.44
  19.0 0.5 multiply_cosine_fusion
  19.5 0.8 copy.89
  20.3 1.4 subtract_convert_fusion.1
  21.7 0.8 copy.90
  22.6 0.3 copy.84
  22.9 1.4 copy.83
  24.3 1.4 fusion.59
  25.7 0.2 copy.80
  25.9 0.2 reshape.244
  26.1 7.0 %gather_fusion.1 = f32[1024]{0:T(1024)S(1)} fusion(f32[512,8]{0,1:T(8,128)S(1)} %fusion.59, s32[1024]{0:T(1024)S(1)} %reshape.244), kind=kCustom, calls=%fused_computation.clone | custom fusion | bytes 16384 | tf_op jit(solution)/shard_map/jit(take_along_axis)/gather | solution.py:31
  33.1 0.2 reshape.247
  33.3 0.1 copy.81
  33.5 0.8 copy.85
  34.3 11.8 %fusion.29 = f32[512,8,512]{2,0,1:T(8,128)S(1)} fusion(bf16[8,2048,512]{2,1,0:T(8,128)(2,1)} %param.27, bf16[512,2048]{1,0:T(8,128)(2,1)S(1)} %copy-done.2, f32[2048]{0:T(1024)S(1)} %copy-done.16, f32[512]{0:T(512)S(1)} %add_rsqrt_fusion.1), kind=kOutput, calls=%fused_computation.42 | convolution fusion | flops 8594128896 | bytes 27273216 | tf_op jit(solution)/shard_map/bd,edc->bec/dot_general | solution.py:52
  46.1 8.3 %copy.87 = f32[512,8,512]{2,1,0:T(8,128)} copy(f32[512,8,512]{2,0,1:T(8,128)S(1)} %fusion.29) | data formatting | bytes 16777216 | tf_op jit(solution)/shard_map/bd,edc->bec/dot_general | solution.py:52
  54.4 18.3 %gather_fusion = f32[1024,512]{1,0:T(8,128)} fusion(f32[512,8,512]{2,1,0:T(8,128)} %copy.87, s32[1024]{0:T(1024)S(1)} %reshape.244), kind=kCustom, calls=%fused_computation.2 | custom fusion | bytes 4202496 | tf_op jit(solution)/shard_map/jit(take_along_axis)/gather | solution.py:53
  72.6 2.9 gather.10
  75.6 4.1 %copy_select_fusion = f32[512,2,4,128]{3,1,2,0:T(2,128)S(1)} fusion(f32[512,2,4,128]{3,2,1,0:T(4,128)} %gather.10, pred[512,2]{1,0:T(8,128)(4,1)} %copy.85), kind=kLoop, calls=%fused_computation.45 | loop fusion | flops 524288 | bytes 4195328 | tf_op jit(solution)/shard_map/jit(take_along_axis)/select_n | solution.py:53
  79.7 3.0 subtract_convert_fusion
  82.7 26.3 %broadcast_select_fusion = (bf16[512,32,4,128]{3,2,1,0:T(4,128)(2,1)}, bf16[512,32,4,128]{3,2,1,0:T(4,128)(2,1)}) fusion(bf16[512,32,4,128]{3,2,1,0:T(4,128)(2,1)} %param.19, pred[512,32]{1,0:T(8,128)(4,1)S(1)} %get-tuple-element.17, bf16[512,4,128]{2,1,0:T(4,128)(2,1)S(1)} %copy.84, bf16[512,32,4,128]{3,2,1,0:T(4,128)(2,1)} %param.20, ...), kind=kLoop, calls=%fused_computation.11 | loop fusion | flops 16777216 | bytes 68173824 | tf_op jit(solution)/shard_map/jit(_where)/select_n | solution.py:48
  109.0 12.6 %multiply_select_fusion = f32[512,4,32,2]{2,3,1,0:T(2,128)S(1)} fusion(pred[512,32]{1,0:T(8,128)(4,1)S(1)} %copy-done.11, bf16[512,32,4,128]{3,2,1,0:T(4,128)(2,1)} %get-tuple-element.12, bf16[512,2,4,64]{3,1,2,0:T(2,128)(2,1)S(1)} %get-tuple-element.9, bf16[512,2,4,64]{3,1,2,0:T(2,128)(2,1)S(1)} %get-tuple-element.8), kind=kOutput, calls=%fused_computation.46 | convolution fusion | flops 35913728 | bytes 18366464 | tf_op jit(solution)/shard_map/bknd,bsnd->bkns/dot_general | solution.py:55
  121.6 4.7 %fusion.62 = (f32[512,2,4]{1,2,0:T(4,128)S(1)}, f32[512,2,4,32]{3,1,2,0:T(2,128)}) fusion(f32[512,4,32,2]{2,3,1,0:T(2,128)S(1)} %multiply_select_fusion), kind=kOutput, calls=%fused_computation.92 | output fusion | flops 262175 | bytes 1064960 | tf_op jit(solution)/shard_map/sub | solution.py:57
  126.3 0.2 copy.93
  126.5 13.5 %convolution_convert_fusion = bf16[512,8,512]{2,1,0:T(8,128)(2,1)} fusion(bf16[512,2,8]{2,1,0:T(2,128)(2,1)S(1)} %copy.93, bf16[512,32,4,128]{3,2,1,0:T(4,128)(2,1)} %get-tuple-element.13, f32[512,2,4,32]{3,1,2,0:T(2,128)} %get-tuple-element.19, f32[512,2,4]{1,2,0:T(4,128)S(1)} %get-tuple-element.18), kind=kOutput, calls=%fused_computation.33 | convolution fusion | flops 44826624 | bytes 21528576 | tf_op jit(solution)/shard_map/bke,bkc->bec/dot_general | solution.py:59
  140.1 20.0 %fusion.1 = bf16[512,2048]{1,0:T(8,128)(2,1)} fusion(bf16[8,512,2048]{2,1,0:T(8,128)(2,1)} %param.28, f32[512,8]{0,1:T(8,128)S(1)} %select_reduce_fusion, bf16[512,8,512]{2,1,0:T(8,128)(2,1)} %convolution_convert_fusion), kind=kOutput, calls=%fused_computation.5 | convolution fusion | flops 8605663232 | bytes 23085056 | tf_op jit(solution)/shard_map/bec,ecd->bed/dot_general | solution.py:60
  160.1 0.0 all-reduce.5.cloned.1.call-start
  160.2 0.1 copy.95
  160.4 0.2 reshape.249
  160.5 0.5 iota_add_fusion
  161.1 47.7 %all-reduce.3.cloned.1.call-done = bf16[512,2048]{1,0:T(8,128)(2,1)} async-done(((bf16[512,2048]{1,0:T(8,128)(2,1)}), bf16[512,2048]{1,0:T(8,128)(2,1)}) %all-reduce.3.cloned.1.call-update) | async-done | bytes 2097168 | tf_op jit(solution)/shard_map/psum | solution.py:77
  208.8 2.5 fusion.12
  211.3 1.0 fusion.14
  212.4 32.4 %fusion.21 = f32[512,2,5632]{2,0,1:T(8,128)} fusion(bf16[2,2048,5632]{2,1,0:T(8,128)(2,1)} %param.31, bf16[512,2048]{1,0:T(8,128)(2,1)S(1)} %fusion.14), kind=kOutput, calls=%fused_computation.36 | convolution fusion | flops 23622320128 | bytes 71303168 | tf_op jit(solution)/shard_map/bd,edf->bef/dot_general | solution.py:66
  244.8 0.6 fusion.63
  245.4 6.5 %gather_fusion.2 = f32[1024]{0:T(1024)S(1)} fusion(f32[512,8]{0,1:T(8,128)S(1)} %fusion.63, s32[1024]{0:T(1024)S(1)} %reshape.249), kind=kCustom, calls=%fused_computation.1.clone | custom fusion | bytes 16384 | tf_op jit(solution)/shard_map/jit(take_along_axis)/gather | solution.py:31
  252.0 0.2 reshape.252
  252.2 0.1 copy.96
  252.4 33.8 %multiply_convert_fusion.6 = bf16[512,2,5632]{2,0,1:T(8,128)(2,1)} fusion(f32[512,2,5632]{2,0,1:T(8,128)} %fusion.21, bf16[2,2048,5632]{2,1,0:T(8,128)(2,1)} %param.32, bf16[512,2048]{1,0:T(8,128)(2,1)S(1)} %copy-done.6), kind=kOutput, calls=%fused_computation.6.clone.clone.clone.clone.1 | convolution fusion | flops 23656923136 | bytes 82837504 | tf_op jit(solution)/shard_map/bd,edf->bef/dot_general | solution.py:67
  286.2 0.1 fusion.49
  286.3 34.2 %fusion.7 = bf16[512,2048]{1,0:T(8,128)(2,1)} fusion(bf16[2,5632,2048]{2,1,0:T(8,128)(2,1)} %param.33, f32[512,2]{0,1:T(2,128)S(1)} %fusion.49, bf16[512,2,5632]{2,0,1:T(8,128)(2,1)} %multiply_convert_fusion.6), kind=kOutput, calls=%fused_computation.15 | convolution fusion | flops 23625465856 | bytes 59772928 | tf_op jit(solution)/shard_map/bef,efd->bed/dot_general | solution.py:69
  320.5 45.9 %all-reduce.5.cloned.1.call-done = bf16[512,2048]{1,0:T(8,128)(2,1)} async-done(((bf16[512,2048]{1,0:T(8,128)(2,1)}), bf16[512,2048]{1,0:T(8,128)(2,1)}) %all-reduce.5.cloned.1.call-update) | async-done | bytes 2097168 | tf_op jit(solution)/shard_map/psum | solution.py:84
  366.4 5.0 %fusion.15 = bf16[512,2048]{1,0:T(8,128)(2,1)} fusion(bf16[512,2048]{1,0:T(8,128)(2,1)} %all-reduce.5.cloned.1.call-done, bf16[512,2048]{1,0:T(8,128)(2,1)} %all-reduce.3.cloned.1.call-done, bf16[512,2048]{1,0:T(8,128)(2,1)S(1)} %copy-done.3), kind=kLoop, calls=%fused_computation.29 | loop fusion | flops 8388608 | bytes 8388608 | tf_op jit(solution)/shard_map/convert_element_type | solution.py:85
  (50 shorter events, 0.4 us)
Async XLA Ops:
  7.2 17.1 %copy-start = (bf16[2048,8]{0,1:T(8,128)(2,1)S(1)}, bf16[2048,8]{0,1:T(8,128)(2,1)}, u32[]{:S(2)}) copy-start(bf16[2048,8]{0,1:T(8,128)(2,1)} %param.26) | copy-start | bytes 98308
  7.2 201.6 %all-reduce.3.cloned.1.call-start = ((), (), s32[]{:S(2)}) async-start(), calls=%async_computation | async-start | bytes 4194304 | tf_op jit(solution)/shard_map/psum | solution.py:77
  11.5 11.1 %copy-start.10 = (s32[512,2]{0,1:T(2,128)S(1)}, s32[512,2]{0,1:T(2,128)}, u32[]{:S(2)}) copy-start(s32[512,2]{0,1:T(2,128)} %param.22) | copy-start | bytes 12292
  16.8 1.3 copy-start.7
  18.1 6.2 %copy-start.2 = (bf16[512,2048]{1,0:T(8,128)(2,1)S(1)}, bf16[512,2048]{1,0:T(8,128)(2,1)}, u32[]{:S(2)}) copy-start(bf16[512,2048]{1,0:T(8,128)(2,1)} %param.18) | copy-start | bytes 6291460
  26.1 8.2 %copy-start.16 = (f32[2048]{0:T(1024)S(1)}, f32[2048]{0:T(1024)}, u32[]{:S(2)}) copy-start(f32[2048]{0:T(1024)} %param.24) | copy-start | bytes 24580
  72.6 7.0 %copy-start.8 = (f32[512,64]{1,0:T(8,128)S(1)}, f32[512,64]{1,0:T(8,128)}, u32[]{:S(2)}) copy-start(f32[512,64]{1,0:T(8,128)} %copy.89) | copy-start | bytes 393220
  75.6 4.1 %copy-start.9 = (f32[512,64]{1,0:T(8,128)S(1)}, f32[512,64]{1,0:T(8,128)}, u32[]{:S(2)}) copy-start(f32[512,64]{1,0:T(8,128)} %copy.90) | copy-start | bytes 393220
  82.7 26.3 %copy-start.11 = (pred[512,32]{1,0:T(8,128)(4,1)S(1)}, pred[512,32]{1,0:T(8,128)(4,1)}, u32[]{:S(2)}) copy-start(pred[512,32]{1,0:T(8,128)(4,1)} %get-tuple-element.16) | copy-start | bytes 49156
  140.1 20.1 %copy-start.12 = (s32[512,2]{0,1:T(2,128)S(1)}, s32[512,2]{0,1:T(2,128)}, u32[]{:S(2)}) copy-start(s32[512,2]{0,1:T(2,128)} %param.23) | copy-start | bytes 12292
  160.1 51.2 %copy-start.14 = (f32[2048]{0:T(1024)S(1)}, f32[2048]{0:T(1024)}, u32[]{:S(2)}) copy-start(f32[2048]{0:T(1024)} %param.29) | copy-start | bytes 24580
  160.1 206.3 %all-reduce.5.cloned.1.call-start = ((), (), s32[]{:S(2)}) async-start(), calls=%async_computation.1 | async-start | bytes 4194304 | tf_op jit(solution)/shard_map/psum | solution.py:84
  208.8 2.5 copy-start.4
  212.3 32.4 %copy-start.5 = (bf16[512,2048]{1,0:T(8,128)(2,1)}, bf16[512,2048]{1,0:T(8,128)(2,1)S(1)}, u32[]{:S(2)}) copy-start(bf16[512,2048]{1,0:T(8,128)(2,1)S(1)} %fusion.14) | copy-start | bytes 6291460
  212.4 32.4 %copy-start.13 = (bf16[2048,8]{0,1:T(8,128)(2,1)S(1)}, bf16[2048,8]{0,1:T(8,128)(2,1)}, u32[]{:S(2)}) copy-start(bf16[2048,8]{0,1:T(8,128)(2,1)} %param.30) | copy-start | bytes 98308
  245.4 6.9 %copy-start.6 = (bf16[512,2048]{1,0:T(8,128)(2,1)S(1)}, bf16[512,2048]{1,0:T(8,128)(2,1)}, u32[]{:S(2)}) copy-start(bf16[512,2048]{1,0:T(8,128)(2,1)} %copy-done.5) | copy-start | bytes 6291460
  252.4 33.8 %copy-start.15 = (s32[2]{0:T(128)S(1)}, s32[2]{0:T(128)}, u32[]{:S(2)}) copy-start(s32[2]{0:T(128)} %iota_add_fusion) | copy-start | bytes 28
  286.3 80.1 %copy-start.3 = (bf16[512,2048]{1,0:T(8,128)(2,1)S(1)}, bf16[512,2048]{1,0:T(8,128)(2,1)}, u32[]{:S(2)}) copy-start(bf16[512,2048]{1,0:T(8,128)(2,1)} %param.18) | copy-start | bytes 6291460
  320.5 50.9 %copy-start.1 = (bf16[2048,8]{0,1:T(8,128)(2,1)S(1)}, bf16[2048,8]{0,1:T(8,128)(2,1)}, u32[]{:S(2)}) copy-start(bf16[2048,8]{0,1:T(8,128)(2,1)} %param.26) | copy-start | bytes 98308
Sparse Core Ops, SparseCore 0:
  160.2 48.4 all-reduce.2
  320.6 45.7 all-reduce.4
where the time goes:
time: 384 us; the launch traced here: 379 us
  matrix products  166 us (43%)
  waiting for transfers between devices  93.6 us (24%)
  other arithmetic  53.6 us (14%)
  local copies, waits for them, and re-layouts  50.8 us (13%)
  between operations  14.9 us (4%)
    psum x1, waiting for transfers between devices, local_step(): att_sum = lax.psum(att_part.astype(jnp.bfloat16), 'tp').astype(jnp.float32)  47.7 us
    psum x1, waiting for transfers between devices, local_step(): mlp_sum = lax.psum(mlp_part.astype(jnp.bfloat16), 'tp').astype(jnp.float32)  45.9 us
    dot_general x1, matrix products, expert_part(): jnp.einsum('bef,efd->bed', activation, w_down, preferred_element_type=jnp...  34.2 us
    dot_general x1, matrix products, expert_part(): jnp.einsum('bd,edf->bef', normed, w_up, preferred_element_type=jnp.float32)  33.8 us
    dot_general x1, matrix products, expert_part(): jnp.einsum('bd,edf->bef', normed, w_gate, preferred_element_type=jnp.floa...  32.4 us
    select_n x1, other arithmetic, attention_part(): keys_all = jnp.where(at_slot, key_new[:, None, :, :], k_cache)  26.3 us
    gather x2, local copies, waits for them, and re-layouts, attention_part(): jnp.take_along_axis(query_all, att_ids[:, :, None], axis=1)  21.2 us
    dot_general x1, matrix products, attention_part(): jnp.einsum('bec,ecd->bed', out_slots, w_out, preferred_element_type=jnp.f...  20 us
  transfers between devices with their start and end apart: 2, of which 2 were waited for; matrix products, arithmetic and copies ran while one was open for 0% of the time, Pallas kernels for 0%

commit v1 on v0

v1 whole, which is shorter than its diff:
```python
import functools

import jax
import jax.numpy as jnp
from jax import lax
from jax.experimental import pallas as pl
from jax.experimental.pallas import tpu as pltpu
from jax.sharding import PartitionSpec as P

NORM_EPS = 1e-6
ROPE_BASE = 10000.0
F32 = jnp.float32
BF16 = jnp.bfloat16
NEG = -1e30
MESH = pl.DeviceIdType.MESH
VMEM_LIMIT = 62 * 1024 * 1024

TOKENS = 512
HIDDEN = 2048
HEADS = 4
HEAD_DIM = 128
SLOTS = 32
QUERY_COLS = HEADS * HEAD_DIM
EXPERTS = 8
FFN = 5632
LOCAL = 2

BLOCK = 32
RING = 8
BLOCKS = TOKENS // BLOCK
GROUP = 8
WQ_RING = 3

COL = 256
ROWS = 256
STEPS = HIDDEN // COL
CHUNKS = STEPS // 2 * (TOKENS // ROWS)

FT = 512
F_TILES = FFN // FT
MLP_STEPS = LOCAL * F_TILES
W_RING = 4
RB = 128


def dot(a, b):
    return jnp.dot(a, b, preferred_element_type=F32)


def iota(shape, dim):
    return lax.broadcasted_iota(jnp.int32, shape, dim)


def norm_rows(x_ref, gain_ref, out_ref):
    def body(i, carry):
        rows = pl.ds(pl.multiple_of(i * 32, 32), 32)
        values = x_ref[rows, :].astype(F32)
        inv = lax.rsqrt(jnp.mean(values * values, axis=-1, keepdims=True) + NORM_EPS)
        out_ref[rows, :] = (values * inv * gain_ref[...]).astype(BF16)
        return carry
    lax.fori_loop(0, TOKENS // 32, body, 0)


def pair_gates(logits, id0, id1):
    lane = iota(logits.shape, 1)
    first = jnp.sum(jnp.where(lane == id0, logits, 0.0), axis=1, keepdims=True)
    second = jnp.sum(jnp.where(lane == id1, logits, 0.0), axis=1, keepdims=True)
    top = jnp.maximum(first, second)
    e0 = jnp.exp(first - top)
    e1 = jnp.exp(second - top)
    total = e0 + e1
    return e0 / total, e1 / total


def attend_kernel(pos_ref, x_ref, gain_ref, cos_ref, sin_ref, ids_ref, router_ref, wkv_hbm, wq_hbm, kc_hbm, vc_hbm,
                  ko_hbm, vo_hbm, o_ref, gates_ref,
                  hid, wkv, wq, kbuf, vbuf, qsel, qrow, knew, vnew, orow,
                  wkv_sem, wq_sem, kin_sem, vin_sem, kout_sem, vout_sem):
    def block_of(ref, b):
        return ref.at[pl.ds(pl.multiple_of(b * BLOCK, BLOCK), BLOCK)]

    def load(b):
        slot = lax.rem(b, RING)
        return (pltpu.make_async_copy(block_of(kc_hbm, b), kbuf.at[slot], kin_sem.at[slot]),
                pltpu.make_async_copy(block_of(vc_hbm, b), vbuf.at[slot], vin_sem.at[slot]))

    def save(b):
        slot = lax.rem(b, RING)
        return (pltpu.make_async_copy(kbuf.at[slot], block_of(ko_hbm, b), kout_sem.at[slot]),
                pltpu.make_async_copy(vbuf.at[slot], block_of(vo_hbm, b), vout_sem.at[slot]))

    def load_wq(e):
        slot = lax.rem(e, WQ_RING)
        return pltpu.make_async_copy(wq_hbm.at[e], wq.at[slot], wq_sem.at[slot])

    kv_copy = pltpu.make_async_copy(wkv_hbm, wkv, wkv_sem)
    kv_copy.start()
    for e in range(WQ_RING):
        load_wq(jnp.int32(e)).start()
    for b in range(RING):
        for copy in load(jnp.int32(b)):
            copy.start()

    norm_rows(x_ref, gain_ref, hid)
    id0 = ids_ref[:, 0:1]
    id1 = ids_ref[:, 1:2]
    logits = dot(hid[...], router_ref[...])
    g0, g1 = pair_gates(logits, id0, id1)
    lane8 = iota((TOKENS, EXPERTS), 1)
    gates_ref[...] = jnp.where(lane8 == id0, g0, 0.0) + jnp.where(lane8 == id1, g1, 0.0)

    kv_copy.wait()

    def kv_body(m, carry):
        rows = pl.ds(pl.multiple_of(m * ROWS, ROWS), ROWS)
        kv = dot(hid[rows, :], wkv[...])
        cos = cos_ref[rows, :]
        sin = sin_ref[rows, :]
        for h in range(HEADS):
            k = kv[:, h * 256:h * 256 + 128]
            v = kv[:, h * 256 + 128:h * 256 + 256]
            k = k * cos + pltpu.roll(k, 64, 1) * sin
            knew[rows, h, :] = k
            knew[rows, h + 4, :] = k
            vnew[rows, h, :] = v
            vnew[rows, h + 4, :] = v
        return carry
    lax.fori_loop(0, TOKENS // ROWS, kv_body, 0)

    def q_body(e, carry):
        load_wq(e).wait()
        slot = lax.rem(e, WQ_RING)

        def m_body(m, c):
            rows = pl.ds(pl.multiple_of(m * ROWS, ROWS), ROWS)
            q = dot(hid[rows, :], wq[slot])
            for k in range(2):
                picked = ids_ref[rows, k:k + 1] == e
                qsel[k, rows, :] = jnp.where(picked, q, qsel[k, rows, :])
            return c
        lax.fori_loop(0, TOKENS // ROWS, m_body, 0)

        @pl.when(e + WQ_RING < EXPERTS)
        def _():
            load_wq(e + WQ_RING).start()
        return carry
    lax.fori_loop(0, EXPERTS, q_body, 0)

    def rope_body(m, carry):
        rows = pl.ds(pl.multiple_of(m * 128, 128), 128)
        cos = cos_ref[rows, :]
        sin = sin_ref[rows, :]
        for k in range(2):
            for h in range(HEADS):
                q = qsel[k, rows, h * 128:(h + 1) * 128]
                qrow[rows, k * HEADS + h, :] = q * cos + pltpu.roll(q, 64, 1) * sin
        return carry
    lax.fori_loop(0, TOKENS // 128, rope_body, 0)

    scale = HEAD_DIM ** -0.5
    sub16 = iota((16, HEAD_DIM), 0) >> 2
    row8 = iota((8, 128), 0)
    lane = iota((8, 128), 1)
    same_head = (lane & 3) == (row8 & 3)
    slot_of = lane >> 2

    def block_body(b, carry):
        slot = lax.rem(b, RING)
        for copy in load(b):
            copy.wait()

        def group_body(g, c):
            local = [g * GROUP + j for j in range(GROUP)]
            tokens = [b * BLOCK + t for t in local]
            places = [pos_ref[t] for t in tokens]
            for j in range(GROUP):
                rows = pl.ds(pl.multiple_of((places[j] >> 2) * 16, 16), 16)
                put = sub16 == (places[j] & 3)
                for new, buf in ((knew, kbuf), (vnew, vbuf)):
                    n8 = new[tokens[j]]
                    n16 = jnp.concatenate([n8, n8], axis=0)
                    old = buf[slot, local[j], rows, :].astype(F32)
                    buf[slot, local[j], rows, :] = jnp.where(put, n16, old).astype(BF16)
            probs = []
            for j in range(GROUP):
                q = qrow[tokens[j]].astype(BF16)
                s = lax.dot_general(q, kbuf[slot, local[j]], (((1,), (1,)), ((), ())), preferred_element_type=F32) * scale
                s = jnp.where(same_head & (slot_of <= places[j]), s, NEG)
                e = jnp.exp(s - jnp.max(s, axis=1, keepdims=True))
                probs.append((e / jnp.sum(e, axis=1, keepdims=True)).astype(BF16))
            for j in range(GROUP):
                orow[local[j]] = dot(probs[j], vbuf[slot, local[j]])
            return c
        lax.fori_loop(0, BLOCK // GROUP, group_body, 0)
        rows = pl.ds(pl.multiple_of(b * BLOCK, BLOCK), BLOCK)
        for r in range(8):
            o_ref[rows, r * 128:(r + 1) * 128] = orow[:, r, :].astype(BF16)
        for copy in save(b):
            copy.start()

        @pl.when(b >= 2)
        def _():
            for copy in save(b - 2):
                copy.wait()

            @pl.when(b - 2 + RING < BLOCKS)
            def _():
                for copy in load(b - 2 + RING):
                    copy.start()
        return carry
    lax.fori_loop(0, BLOCKS, block_body, 0)
    for b in (BLOCKS - 2, BLOCKS - 1):
        for copy in save(jnp.int32(b)):
            copy.wait()


def attend(positions, x, gain, cos, sin, ids, router, w_kv, w_query, k_cache, v_cache):
    any_spec = pl.BlockSpec(memory_space=pl.ANY)
    vmem = pl.BlockSpec(memory_space=pltpu.VMEM)
    smem = pl.BlockSpec(memory_space=pltpu.SMEM)
    cache = jax.ShapeDtypeStruct(k_cache.shape, BF16)
    return pl.pallas_call(
        attend_kernel,
        name='attend',
        out_shape=(cache, cache, jax.ShapeDtypeStruct((TOKENS, 2 * QUERY_COLS), BF16), jax.ShapeDtypeStruct((TOKENS, EXPERTS), F32)),
        in_specs=[smem] + [vmem] * 6 + [any_spec] * 4,
        out_specs=(any_spec, any_spec, vmem, vmem),
        scratch_shapes=[
            pltpu.VMEM((TOKENS, HIDDEN), BF16),
            pltpu.VMEM((HIDDEN, HEADS * 256), BF16),
            pltpu.VMEM((WQ_RING, HIDDEN, QUERY_COLS), BF16),
            pltpu.VMEM((RING, BLOCK, SLOTS * HEADS, HEAD_DIM), BF16),
            pltpu.VMEM((RING, BLOCK, SLOTS * HEADS, HEAD_DIM), BF16),
            pltpu.VMEM((2, TOKENS, QUERY_COLS), F32),
            pltpu.VMEM((TOKENS, 8, HEAD_DIM), F32),
            pltpu.VMEM((TOKENS, 8, HEAD_DIM), F32),
            pltpu.VMEM((TOKENS, 8, HEAD_DIM), F32),
            pltpu.VMEM((BLOCK, 8, HEAD_DIM), F32),
            pltpu.SemaphoreType.DMA,
            pltpu.SemaphoreType.DMA((WQ_RING,)),
            pltpu.SemaphoreType.DMA((RING,)),
            pltpu.SemaphoreType.DMA((RING,)),
            pltpu.SemaphoreType.DMA((RING,)),
            pltpu.SemaphoreType.DMA((RING,)),
        ],
        compiler_params=pltpu.CompilerParams(vmem_limit_bytes=VMEM_LIMIT),
    )(positions, x, gain, cos, sin, ids, router, w_kv, w_query, k_cache, v_cache)


def reduce_columns(load_step, wait_step, partial, base_ref, out_ref, send1, recv1, own, recv2, fin, recv3, s1, r1, s2, r2, s3, r3):
    me = lax.axis_index('tp')
    core = lax.rem(me, 2)
    sibling = me + 1 - 2 * core
    partner = lax.rem(me + 2, 4)
    barrier = pltpu.get_barrier_semaphore()
    for peer in (sibling, partner):
        pl.semaphore_signal(barrier, inc=1, device_id={'tp': peer}, device_id_type=MESH)
    pl.semaphore_wait(barrier, 2)

    def column(s):
        half = lax.rem(core + 1 + s, 2)
        return pl.multiple_of((half * (STEPS // 2) + lax.div(s, 2)) * COL, COL)

    def remote(src, dst, c, send, recv, peer):
        return pltpu.make_async_remote_copy(src_ref=src.at[c], dst_ref=dst.at[c], send_sem=send.at[c], recv_sem=recv.at[c],
                                            device_id={'tp': peer}, device_id_type=MESH)

    def to_sibling(c):
        return remote(send1, recv1, c, s1, r1, sibling)

    def to_partner(c):
        return remote(own, recv2, c, s2, r2, partner)

    def share(c):
        return remote(fin, recv3, c, s3, r3, sibling)

    def step_body(i, carry):
        for parity in range(2):
            s = 2 * i + parity
            wait_step(s, column(s))

            def row_body(m, c):
                rows = pl.ds(pl.multiple_of(m * ROWS, ROWS), ROWS)
                chunk = 2 * i + m
                acc = partial(s, rows)
                if parity == 0:
                    send1[chunk] = acc.astype(BF16)
                    to_sibling(chunk).start()
                else:
                    to_sibling(chunk).wait_recv()
                    own[chunk] = (acc + recv1[chunk].astype(F32)).astype(BF16)
                    to_partner(chunk).start()
                return c
            lax.fori_loop(0, TOKENS // ROWS, row_body, 0)
            load_step(s, column)
        return carry
    lax.fori_loop(0, STEPS // 2, step_body, 0)

    def place(c, half):
        rows = pl.ds(pl.multiple_of(lax.rem(c, 2) * ROWS, ROWS), ROWS)
        cols = pl.ds(pl.multiple_of((half * (STEPS // 2) + lax.div(c, 2)) * COL, COL), COL)
        return rows, cols

    def final_body(c, carry):
        to_partner(c).wait_recv()
        rows, cols = place(c, core)
        total = own[c].astype(F32) + recv2[c].astype(F32)
        value = (base_ref[rows, cols].astype(F32) + total).astype(BF16)
        fin[c] = value
        out_ref[rows, cols] = value
        share(c).start()
        return carry
    lax.fori_loop(0, CHUNKS, final_body, 0)

    def gather_body(c, carry):
        share(c).wait_recv()
        rows, cols = place(c, 1 - core)
        out_ref[rows, cols] = recv3[c]
        return carry
    lax.fori_loop(0, CHUNKS, gather_body, 0)

    def drain_body(c, carry):
        to_sibling(c).wait_send()
        to_partner(c).wait_send()
        share(c).wait_send()
        return carry
    lax.fori_loop(0, CHUNKS, drain_body, 0)


CHUNK_SCRATCH = [pltpu.VMEM((CHUNKS, ROWS, COL), BF16)] * 6 + [pltpu.SemaphoreType.DMA((CHUNKS,))] * 6
OUT_RING = 3


def out_kernel(o_ref, ids_ref, gates_ref, x_ref, w_hbm, out_ref, spread, wbuf, w_sem, *chunk_refs):
    me = lax.axis_index('tp')
    core = lax.rem(me, 2)

    def copy_of(s, col):
        slot = lax.rem(s, OUT_RING)
        return pltpu.make_async_copy(w_hbm.at[:, :, pl.ds(col, COL)], wbuf.at[slot], w_sem.at[slot])

    for s in range(OUT_RING):
        half = lax.rem(core + 1 + s, 2)
        copy_of(jnp.int32(s), pl.multiple_of((half * (STEPS // 2) + s // 2) * COL, COL)).start()

    def spread_body(m, carry):
        rows = pl.ds(pl.multiple_of(m * 128, 128), 128)
        first = o_ref[rows, :QUERY_COLS].astype(F32)
        second = o_ref[rows, QUERY_COLS:].astype(F32)
        for e in range(EXPERTS):
            picked = jnp.where(ids_ref[rows, 0:1] == e, first, 0.0)
            picked = jnp.where(ids_ref[rows, 1:2] == e, second, picked)
            spread[e, rows, :] = picked.astype(BF16)
        return carry
    lax.fori_loop(0, TOKENS // 128, spread_body, 0)

    def load_step(s, column):
        @pl.when(s + OUT_RING < STEPS)
        def _():
            copy_of(s + OUT_RING, column(s + OUT_RING)).start()

    def wait_step(s, col):
        copy_of(s, col).wait()

    def partial(s, rows):
        slot = lax.rem(s, OUT_RING)
        acc = jnp.zeros((ROWS, COL), F32)
        for e in range(EXPERTS):
            acc = acc + gates_ref[rows, e:e + 1] * dot(spread[e, rows, :], wbuf[slot, e])
        return acc

    reduce_columns(load_step, wait_step, partial, x_ref, out_ref, *chunk_refs)


def out_project(o, ids, gates, x, w_out):
    vmem = pl.BlockSpec(memory_space=pltpu.VMEM)
    return pl.pallas_call(
        out_kernel,
        name='out_project',
        out_shape=jax.ShapeDtypeStruct((TOKENS, HIDDEN), BF16),
        in_specs=[vmem] * 4 + [pl.BlockSpec(memory_space=pl.ANY)],
        out_specs=vmem,
        scratch_shapes=[
            pltpu.VMEM((EXPERTS, TOKENS, QUERY_COLS), BF16),
            pltpu.VMEM((OUT_RING, EXPERTS, QUERY_COLS, COL), BF16),
            pltpu.SemaphoreType.DMA((OUT_RING,)),
        ] + CHUNK_SCRATCH,
        compiler_params=pltpu.CompilerParams(vmem_limit_bytes=VMEM_LIMIT, collective_id=0, has_side_effects=True),
    )(o, ids, gates, x, w_out)


def gate_up_kernel(x_ref, gain_ref, router_ref, ids_ref, idst_ref, wg_hbm, wu_hbm, a_hbm, gates_ref,
                   unorm, picked, scatter, gathered, wg, wu, act, abuf, wg_sem, wu_sem, a_sem):
    first_id = lax.axis_index('tp') * LOCAL

    def load(s):
        e = lax.div(s, F_TILES)
        cols = pl.ds(pl.multiple_of(lax.rem(s, F_TILES) * FT, FT), FT)
        slot = lax.rem(s, W_RING)
        return (pltpu.make_async_copy(wg_hbm.at[e, :, cols], wg.at[slot], wg_sem.at[slot]),
                pltpu.make_async_copy(wu_hbm.at[e, :, cols], wu.at[slot], wu_sem.at[slot]))

    def save(s):
        e = lax.div(s, F_TILES)
        cols = pl.ds(pl.multiple_of(lax.rem(s, F_TILES) * FT, FT), FT)
        slot = lax.rem(s, 2)
        return pltpu.make_async_copy(abuf.at[slot], a_hbm.at[e, :, cols], a_sem.at[slot])

    for s in range(W_RING):
        for copy in load(jnp.int32(s)):
            copy.start()

    norm_rows(x_ref, gain_ref, unorm)
    id0 = ids_ref[:, 0:1]
    id1 = ids_ref[:, 1:2]
    logits = dot(unorm[...], router_ref[...])
    g0, g1 = pair_gates(logits, id0, id1)
    lane8 = iota((TOKENS, EXPERTS), 1)
    local8 = lane8 + first_id
    gates_ref[...] = jnp.where(local8 == id0, g0, 0.0) + jnp.where(local8 == id1, g1, 0.0)

    before = iota((TOKENS, TOKENS), 0)
    after = iota((TOKENS, TOKENS), 1)
    lower = jnp.where(after < before, 1.0, 0.0).astype(BF16)
    upper = jnp.where(before < after, 1.0, 0.0).astype(BF16)
    lane_id = iota((TOKENS, 128), 1) + first_id
    mask_col = jnp.where((lane_id == id0) | (lane_id == id1), 1.0, 0.0)
    rank_col = dot(lower, mask_col.astype(BF16))
    sub_id = iota((8, TOKENS), 0) + first_id
    mask_row = jnp.where((sub_id == idst_ref[0:1, :]) | (sub_id == idst_ref[1:2, :]), 1.0, 0.0)
    rank_row = dot(mask_row.astype(BF16), upper)
    counts = []
    for e in range(LOCAL):
        counts.append(jnp.sum(mask_row[e:e + 1, :]).astype(jnp.int32))
        where_col = jnp.where(mask_col[:, e:e + 1] > 0.0, rank_col[:, e:e + 1], -1.0)
        where_row = jnp.where(mask_row[e:e + 1, :] > 0.0, rank_row[e:e + 1, :], -1.0)
        scatter[e] = jnp.where(after.astype(F32) == where_col, 1.0, 0.0).astype(BF16)
        picked[e] = jnp.where(before.astype(F32) == where_row, 1.0, 0.0).astype(BF16)
    blocks = [lax.div(n + (RB - 1), RB) for n in counts]

    for e in range(LOCAL):
        def gather_body(rb, carry):
            rows = pl.ds(pl.multiple_of(rb * RB, RB), RB)
            gathered[e, rows, :] = dot(picked[e, rows, :], unorm[...]).astype(BF16)
            return carry
        lax.fori_loop(0, blocks[e], gather_body, 0)
    act[...] = jnp.zeros_like(act)

    def step_body(s, carry):
        e = lax.div(s, F_TILES)
        slot = lax.rem(s, W_RING)
        for copy in load(s):
            copy.wait()

        def row_body(rb, c):
            rows = pl.ds(pl.multiple_of(rb * RB, RB), RB)
            gate = dot(gathered[e, rows, :], wg[slot])
            up = dot(gathered[e, rows, :], wu[slot])
            act[rows, :] = (gate * (1.0 / (1.0 + jnp.exp(-gate))) * up).astype(BF16)
            return c
        lax.fori_loop(0, jnp.where(e == 0, blocks[0], blocks[1]), row_body, 0)

        @pl.when(s + W_RING < MLP_STEPS)
        def _():
            for copy in load(s + W_RING):
                copy.start()

        @pl.when(s >= 2)
        def _():
            save(s - 2).wait()
        out_slot = lax.rem(s, 2)

        def scatter_body(m, c):
            rows = pl.ds(pl.multiple_of(m * ROWS, ROWS), ROWS)
            abuf[out_slot, rows, :] = dot(scatter[e, rows, :], act[...]).astype(BF16)
            return c
        lax.fori_loop(0, TOKENS // ROWS, scatter_body, 0)
        save(s).start()
        return carry
    lax.fori_loop(0, MLP_STEPS, step_body, 0)
    for s in (MLP_STEPS - 2, MLP_STEPS - 1):
        save(jnp.int32(s)).wait()


def gate_up(x_mid, gain, router, ids, ids_t, w_gate, w_up):
    any_spec = pl.BlockSpec(memory_space=pl.ANY)
    vmem = pl.BlockSpec(memory_space=pltpu.VMEM)
    return pl.pallas_call(
        gate_up_kernel,
        name='gate_up',
        out_shape=(jax.ShapeDtypeStruct((LOCAL, TOKENS, FFN), BF16), jax.ShapeDtypeStruct((TOKENS, EXPERTS), F32)),
        in_specs=[vmem] * 5 + [any_spec] * 2,
        out_specs=(any_spec, vmem),
        scratch_shapes=[
            pltpu.VMEM((TOKENS, HIDDEN), BF16),
            pltpu.VMEM((LOCAL, TOKENS, TOKENS), BF16),
            pltpu.VMEM((LOCAL, TOKENS, TOKENS), BF16),
            pltpu.VMEM((LOCAL, TOKENS, HIDDEN), BF16),
            pltpu.VMEM((W_RING, HIDDEN, FT), BF16),
            pltpu.VMEM((W_RING, HIDDEN, FT), BF16),
            pltpu.VMEM((TOKENS, FT), BF16),
            pltpu.VMEM((2, TOKENS, FT), BF16),
            pltpu.SemaphoreType.DMA((W_RING,)),
            pltpu.SemaphoreType.DMA((W_RING,)),
            pltpu.SemaphoreType.DMA((2,)),
        ],
        compiler_params=pltpu.CompilerParams(vmem_limit_bytes=VMEM_LIMIT),
    )(x_mid, gain, router, ids, ids_t, w_gate, w_up)


DOWN_RING = 2


def down_kernel(gates_ref, x_ref, a_hbm, w_hbm, out_ref, abuf, wbuf, a_sem, w_sem, *chunk_refs):
    me = lax.axis_index('tp')
    core = lax.rem(me, 2)

    def copies(s, col):
        slot = lax.rem(s, DOWN_RING)
        return [pltpu.make_async_copy(w_hbm.at[e, :, pl.ds(col, COL)], wbuf.at[slot, e], w_sem.at[slot, e]) for e in range(LOCAL)]

    a_copies = [pltpu.make_async_copy(a_hbm.at[e], abuf.at[e], a_sem.at[e]) for e in range(LOCAL)]
    for copy in a_copies:
        copy.start()
    for s in range(DOWN_RING):
        half = lax.rem(core + 1 + s, 2)
        for copy in copies(jnp.int32(s), pl.multiple_of((half * (STEPS // 2) + s // 2) * COL, COL)):
            copy.start()
    for copy in a_copies:
        copy.wait()

    def load_step(s, column):
        @pl.when(s + DOWN_RING < STEPS)
        def _():
            for copy in copies(s + DOWN_RING, column(s + DOWN_RING)):
                copy.start()

    def wait_step(s, col):
        for copy in copies(s, col):
            copy.wait()

    def partial(s, rows):
        slot = lax.rem(s, DOWN_RING)
        acc = gates_ref[rows, 0:1] * dot(abuf[0, rows, :], wbuf[slot, 0])
        return acc + gates_ref[rows, 1:2] * dot(abuf[1, rows, :], wbuf[slot, 1])

    reduce_columns(load_step, wait_step, partial, x_ref, out_ref, *chunk_refs)


def down_project(gates, x_mid, act, w_down):
    vmem = pl.BlockSpec(memory_space=pltpu.VMEM)
    any_spec = pl.BlockSpec(memory_space=pl.ANY)
    return pl.pallas_call(
        down_kernel,
        name='down_project',
        out_shape=jax.ShapeDtypeStruct((TOKENS, HIDDEN), BF16),
        in_specs=[vmem] * 2 + [any_spec] * 2,
        out_specs=vmem,
        scratch_shapes=[
            pltpu.VMEM((LOCAL, TOKENS, FFN), BF16),
            pltpu.VMEM((DOWN_RING, LOCAL, FFN, COL), BF16),
            pltpu.SemaphoreType.DMA((LOCAL,)),
            pltpu.SemaphoreType.DMA((DOWN_RING, LOCAL)),
        ] + CHUNK_SCRATCH,
        compiler_params=pltpu.CompilerParams(vmem_limit_bytes=VMEM_LIMIT, collective_id=1, has_side_effects=True),
    )(gates, x_mid, act, w_down)


def rope_rows(positions):
    half = HEAD_DIM // 2
    inv_freq = ROPE_BASE ** (-(jnp.arange(half, dtype=F32) * 2.0 / HEAD_DIM))
    inv_freq = jnp.concatenate([inv_freq, inv_freq])
    sign = jnp.concatenate([-jnp.ones(half, F32), jnp.ones(half, F32)])
    angles = positions.astype(F32)[:, None] * inv_freq[None, :]
    return jnp.cos(angles), jnp.sin(angles) * sign


def solution(mesh):
    def local_step(x, k_cache, v_cache, positions, att_ids, mlp_ids, norm_att, w_kv, router_att, w_query, w_out, norm_mlp, router_mlp, w_gate, w_up, w_down):
        cos, sin = rope_rows(positions)
        flat = (TOKENS, SLOTS * HEADS, HEAD_DIM)
        k_new, v_new, o, att_gates = attend(
            positions, x, norm_att.reshape(1, HIDDEN), cos, sin, att_ids, router_att,
            w_kv.reshape(HIDDEN, HEADS * 256), w_query, k_cache.reshape(flat), v_cache.reshape(flat))
        x_mid = out_project(o, att_ids, att_gates, x, w_out)
        act, mlp_gates = gate_up(x_mid, norm_mlp.reshape(1, HIDDEN), router_mlp, mlp_ids, mlp_ids.T, w_gate, w_up)
        x_out = down_project(mlp_gates, x_mid, act, w_down)
        return x_out, k_new.reshape(k_cache.shape), v_new.reshape(v_cache.shape)

    token_spec = P('dp', None)
    cache_spec = P('dp', None, 'tp', None)
    expert_spec = P('tp', None, None)
    in_specs = (token_spec, cache_spec, cache_spec, P('dp'), token_spec, token_spec, P(), P(None, 'tp', None), P(), P(None, None, 'tp'), P(None, 'tp', None), P(), P(), expert_spec, expert_spec, expert_spec)
    out_specs = (token_spec, cache_spec, cache_spec)
    return jax.shard_map(local_step, mesh=mesh, in_specs=in_specs, out_specs=out_specs, check_vma=False)
```

time: 384 us -> 220 us (0.57)
  Pallas kernels: 0 us -> 199 us
  matrix products: 166 us -> 0 us
  waiting for transfers between devices: 93.6 us -> 0 us
  other arithmetic: 53.6 us -> 3.24 us
  local copies, waits for them, and re-layouts: 50.8 us -> 14.9 us
  between operations: 14.9 us -> 0.67 us
    pallas_call x0 -> x4, Pallas kernels: none -> 199 us  [the longest x1 68.1 us: attend(): pl.pallas_call(attend_kernel, name='attend', out_shape=(cache, cache, jax...]
    dot_general x10 -> x0, matrix products: 166 us -> none  [the longest x1 34.2 us: expert_part(): jnp.einsum('bef,efd->bed', activation, w_down, preferred_element_type=jnp...]
    psum x2 -> x0, waiting for transfers between devices: 93.6 us -> none  [the longest x1 47.7 us: local_step(): att_sum = lax.psum(att_part.astype(jnp.bfloat16), 'tp').astype(jnp.float32)]
    gather x12 -> x0, local copies, waits for them, and re-layouts: 36 us -> none  [the longest x2 21.2 us: attention_part(): jnp.take_along_axis(query_all, att_ids[:, :, None], axis=1)]
    select_n x2 -> x0, other arithmetic: 30.3 us -> none  [the longest x1 26.3 us: attention_part(): keys_all = jnp.where(at_slot, key_new[:, None, :, :], k_cache)]
    unnamed x34 -> x6, local copies, waits for them, and re-layouts: 1.39 us -> 14.9 us
    dot_general x1 -> x0, local copies, waits for them, and re-layouts: 8.25 us -> none  [attention_part(): jnp.einsum('bd,edc->bec', hidden, w_query, preferred_element_type=jnp.flo...]
    convert_element_type x4 -> x1, other arithmetic: 6.69 us -> 0.69 us  [rope_rows(): angles = positions.astype(F32)[:, None] * inv_freq[None, :]]
  transfers between devices with their start and end apart: 2 -> 0, of which waited for: 2 -> 0; matrix products, arithmetic and copies ran while one was open for 0% -> 0% of each run, Pallas kernels for 0% -> 0%
where the time goes in v1:
time: 220 us; the launch traced here: 218 us
  Pallas kernels  199 us (90%)
  local copies, waits for them, and re-layouts  14.9 us (7%)
  other arithmetic  3.24 us (1%)
    pallas_call x1, Pallas kernels, attend(): pl.pallas_call(attend_kernel, name='attend', out_shape=(cache, cache, jax...  68.1 us
    pallas_call x1, Pallas kernels, down_project(): pl.pallas_call(down_kernel, name='down_project', out_shape=jax.ShapeDtype...  57.5 us
    pallas_call x1, Pallas kernels, gate_up(): pl.pallas_call(gate_up_kernel, name='gate_up', out_shape=(jax.ShapeDtypeS...  37.9 us
    pallas_call x1, Pallas kernels, out_project(): pl.pallas_call(out_kernel, name='out_project', out_shape=jax.ShapeDtypeSt...  36 us
    unnamed x6, local copies, waits for them, and re-layouts  14.9 us

profile of v1, /device:TPU:0, one launch (start us, length us, event | category | flops | bytes accessed | tf_op | source)
XLA Modules:
  0.0 218.2 jit_solution(8795193003057015501)
XLA Ops:
  0.6 0.1 pad_maximum_fusion
  0.7 0.7 convert_element_type.3
  1.4 1.5 copy.19.ids_ref
  2.9 1.5 copy.23.ids_ref
  4.5 2.5 %fusion = (f32[512,128]{1,0:T(8,128)}, f32[512,128]{1,0:T(8,128)}) fusion(f32[128]{0:T(128)} %constant.9.clone.1, f32[128]{0:T(128)S(1)} %pad_maximum_fusion, f32[512]{0:T(512)S(1)} %convert_element_type.3), kind=kLoop, calls=%fused_computation.2 | loop fusion | flops 131072 | bytes 527360 | tf_op jit(solution)/shard_map/mul | solution.py:575
  6.9 1.8 copy.20.router_ref
  8.7 1.7 copy.22.router_ref
  10.4 5.2 %copy.24 = bf16[256,8,4,256]{3,1,2,0:T(8,128)(2,1)} copy(bf16[256,8,4,256]{3,2,1,0:T(4,128)(2,1)} %bitcast.12) | data formatting | bytes 8388608
  15.6 68.1 %attend.1 = (bf16[512,128,128]{2,1,0:T(8,128)(2,1)}, bf16[512,128,128]{2,1,0:T(8,128)(2,1)}, bf16[512,1024]{1,0:T(8,128)(2,1)}, f32[512,8]{1,0:T(8,128)}) custom-call(s32[512]{0:T(512)} %pos_ref.1, bf16[512,2048]{1,0:T(8,128)(2,1)} %x_ref.3, f32[1,2048]{1,0:T(1,128)} %bitcast.14, f32[512,128]{1,0:T(8,128)} %get-tuple-element.16.cos_ref, ...), custom_call_target="tpu_custom_call" | custom-call | tf_op jit(solution)/shard_map/attend/pallas_call | solution.py:222
  83.7 36.0 %out_project.1.x_ref = bf16[512,2048]{1,0:T(8,128)(2,1)} custom-call(bf16[512,1024]{1,0:T(8,128)(2,1)} %get-tuple-element.9.o_ref, s32[512,2]{1,0:T(8,128)} %copy.19.ids_ref, f32[512,8]{1,0:T(8,128)} %get-tuple-element.10.gates_ref, bf16[512,2048]{1,0:T(8,128)(2,1)} %x_ref.3, bf16[8,512,2048]{2,1,0:T(8,128)(2,1)} %w_hbm.2), custom_call_target="tpu_custom_call" | custom-call | tf_op jit(solution)/shard_map/out_project/pallas_call | solution.py:377
  119.7 37.9 %gate_up.1 = (bf16[2,512,5632]{2,1,0:T(8,128)(2,1)}, f32[512,8]{1,0:T(8,128)}) custom-call(bf16[512,2048]{1,0:T(8,128)(2,1)} %out_project.1.x_ref, f32[1,2048]{1,0:T(1,128)} %bitcast.15, bf16[2048,8]{1,0:T(8,128)(2,1)} %copy.22.router_ref, s32[512,2]{1,0:T(8,128)} %copy.23.ids_ref, s32[2,512]{1,0:T(2,128)} %bitcast.13, bf16[2,2048,5632]{2,1,0:T(8,128)(2,1)} %wg_hbm.1, ...), custom_call_target="tpu_custom_call" | custom-call | tf_op jit(solution)/shard_map/gate_up/pallas_call | solution.py:488
  157.6 57.5 %down_project.1 = bf16[512,2048]{1,0:T(8,128)(2,1)} custom-call(f32[512,8]{1,0:T(8,128)} %get-tuple-element.11.gates_ref, bf16[512,2048]{1,0:T(8,128)(2,1)} %out_project.1.x_ref, bf16[2,512,5632]{2,1,0:T(8,128)(2,1)} %get-tuple-element.12.a_hbm, bf16[2,5632,2048]{2,1,0:T(8,128)(2,1)} %w_hbm.3), custom_call_target="tpu_custom_call" | custom-call | tf_op jit(solution)/shard_map/down_project/pallas_call | solution.py:553
  215.0 3.2 %copy.26 = bf16[512,2048]{1,0:T(8,128)(2,1)} copy(bf16[512,2048]{1,0:T(8,128)(2,1)} %down_project.1) | data formatting | bytes 4194304
  (1 shorter events, 0.0 us)

commit v2 on v1

--- a/solution.py
+++ b/solution.py
@@ -2,6 +2,7 @@
 
 import jax
 import jax.numpy as jnp
+import numpy as np
 from jax import lax
 from jax.experimental import pallas as pl
 from jax.experimental.pallas import tpu as pltpu
@@ -39,7 +40,7 @@
 FT = 512
 F_TILES = FFN // FT
 MLP_STEPS = LOCAL * F_TILES
-W_RING = 4
+W_RING = 5
 RB = 128
 
 
@@ -72,9 +73,21 @@
     return e0 / total, e1 / total
 
 
-def attend_kernel(pos_ref, x_ref, gain_ref, cos_ref, sin_ref, ids_ref, router_ref, wkv_hbm, wq_hbm, kc_hbm, vc_hbm,
-                  ko_hbm, vo_hbm, o_ref, gates_ref,
-                  hid, wkv, wq, kbuf, vbuf, qsel, qrow, knew, vnew, orow,
+def turn(rows):
+    sub = iota((8, TOKENS), 0)
+    stacked = jnp.zeros((8, TOKENS), F32)
+    for i, row in enumerate(rows):
+        stacked = jnp.where(sub == i, row.astype(F32), stacked)
+    return jnp.transpose(stacked).astype(jnp.int32)
+
+
+def dot_nt(a, b):
+    return lax.dot_general(a, b, (((1,), (1,)), ((), ())), preferred_element_type=F32)
+
+
+def attend_kernel(pos_ref, x_ref, gain_ref, table_ref, posrow_ref, idst_ref, router_ref, wkv_hbm, wq_hbm, kc_hbm, vc_hbm,
+                  ko_hbm, vo_hbm, o_ref, gates_ref, ids_ref,
+                  hid, wraw, wtmp, wkv, wq, kbuf, vbuf, qsel, qrow, knv, orow, probs, cos_s, sin_s,
                   wkv_sem, wq_sem, kin_sem, vin_sem, kout_sem, vout_sem):
     def block_of(ref, b):
         return ref.at[pl.ds(pl.multiple_of(b * BLOCK, BLOCK), BLOCK)]
@@ -93,41 +106,52 @@
         slot = lax.rem(e, WQ_RING)
         return pltpu.make_async_copy(wq_hbm.at[e], wq.at[slot], wq_sem.at[slot])
 
-    kv_copy = pltpu.make_async_copy(wkv_hbm, wkv, wkv_sem)
+    kv_copy = pltpu.make_async_copy(wkv_hbm, wraw, wkv_sem)
     kv_copy.start()
     for e in range(WQ_RING):
         load_wq(jnp.int32(e)).start()
-    for b in range(RING):
-        for copy in load(jnp.int32(b)):
-            copy.start()
 
     norm_rows(x_ref, gain_ref, hid)
-    id0 = ids_ref[:, 0:1]
-    id1 = ids_ref[:, 1:2]
-    logits = dot(hid[...], router_ref[...])
+    ids = turn((idst_ref[0:1, :], idst_ref[1:2, :], posrow_ref[...]))
+    ids_ref[...] = ids
+    id0 = ids[:, 0:1]
+    id1 = ids[:, 1:2]
+    lane128 = iota((TOKENS, 128), 1)
+    chosen = ((lane128 & 31) == ids[:, 2:3]) & (lane128 < 3 * SLOTS)
+    trig = dot(jnp.where(chosen, 1.0, 0.0).astype(BF16), table_ref[...])
+    cos_s[...] = trig[:, :HEAD_DIM]
+    sin_s[...] = trig[:, HEAD_DIM:]
+    logits = dot_nt(hid[...], router_ref[...])
     g0, g1 = pair_gates(logits, id0, id1)
     lane8 = iota((TOKENS, EXPERTS), 1)
     gates_ref[...] = jnp.where(lane8 == id0, g0, 0.0) + jnp.where(lane8 == id1, g1, 0.0)
 
     kv_copy.wait()
 
+    def sort_body(i, carry):
+        raw = wraw[pl.ds(pl.multiple_of(i * 1024, 1024), 1024), :].astype(F32)
+        wtmp[...] = raw.reshape(128, 8, 128)
+        rows = pl.ds(pl.multiple_of(i * 128, 128), 128)
+        for j in range(8):
+            wkv[rows, j * 128:(j + 1) * 128] = wtmp[:, j, :].astype(BF16)
+        return carry
+    lax.fori_loop(0, HIDDEN // 128, sort_body, 0)
+
     def kv_body(m, carry):
         rows = pl.ds(pl.multiple_of(m * ROWS, ROWS), ROWS)
         kv = dot(hid[rows, :], wkv[...])
-        cos = cos_ref[rows, :]
-        sin = sin_ref[rows, :]
+        cos = cos_s[rows, :]
+        sin = sin_s[rows, :]
         for h in range(HEADS):
-            k = kv[:, h * 256:h * 256 + 128]
-            v = kv[:, h * 256 + 128:h * 256 + 256]
-            k = k * cos + pltpu.roll(k, 64, 1) * sin
-            knew[rows, h, :] = k
-            knew[rows, h + 4, :] = k
-            vnew[rows, h, :] = v
-            vnew[rows, h + 4, :] = v
+            k = kv[:, h * 128:(h + 1) * 128]
+            knv[rows, h, :] = k * cos + pltpu.roll(k, 64, 1) * sin
+            knv[rows, h + 4, :] = kv[:, (h + 4) * 128:(h + 5) * 128]
         return carry
     lax.fori_loop(0, TOKENS // ROWS, kv_body, 0)
 
     def q_body(e, carry):
+        for copy in load(e):
+            copy.start()
         load_wq(e).wait()
         slot = lax.rem(e, WQ_RING)
 
@@ -148,8 +172,8 @@
 
     def rope_body(m, carry):
         rows = pl.ds(pl.multiple_of(m * 128, 128), 128)
-        cos = cos_ref[rows, :]
-        sin = sin_ref[rows, :]
+        cos = cos_s[rows, :]
+        sin = sin_s[rows, :]
         for k in range(2):
             for h in range(HEADS):
                 q = qsel[k, rows, h * 128:(h + 1) * 128]
@@ -161,60 +185,82 @@
     sub16 = iota((16, HEAD_DIM), 0) >> 2
     row8 = iota((8, 128), 0)
     lane = iota((8, 128), 1)
+    low = row8 < 4
     same_head = (lane & 3) == (row8 & 3)
     slot_of = lane >> 2
 
-    def block_body(b, carry):
+    def block_body(i, carry):
+        b = jnp.minimum(i, BLOCKS - 1)
+        prev = jnp.maximum(i - 1, 0)
         slot = lax.rem(b, RING)
-        for copy in load(b):
-            copy.wait()
-
-        def group_body(g, c):
-            local = [g * GROUP + j for j in range(GROUP)]
-            tokens = [b * BLOCK + t for t in local]
-            places = [pos_ref[t] for t in tokens]
-            for j in range(GROUP):
-                rows = pl.ds(pl.multiple_of((places[j] >> 2) * 16, 16), 16)
-                put = sub16 == (places[j] & 3)
-                for new, buf in ((knew, kbuf), (vnew, vbuf)):
-                    n8 = new[tokens[j]]
-                    n16 = jnp.concatenate([n8, n8], axis=0)
-                    old = buf[slot, local[j], rows, :].astype(F32)
-                    buf[slot, local[j], rows, :] = jnp.where(put, n16, old).astype(BF16)
-            probs = []
-            for j in range(GROUP):
-                q = qrow[tokens[j]].astype(BF16)
-                s = lax.dot_general(q, kbuf[slot, local[j]], (((1,), (1,)), ((), ())), preferred_element_type=F32) * scale
-                s = jnp.where(same_head & (slot_of <= places[j]), s, NEG)
-                e = jnp.exp(s - jnp.max(s, axis=1, keepdims=True))
-                probs.append((e / jnp.sum(e, axis=1, keepdims=True)).astype(BF16))
-            for j in range(GROUP):
-                orow[local[j]] = dot(probs[j], vbuf[slot, local[j]])
-            return c
-        lax.fori_loop(0, BLOCK // GROUP, group_body, 0)
-        rows = pl.ds(pl.multiple_of(b * BLOCK, BLOCK), BLOCK)
+        prev_slot = lax.rem(prev, RING)
+        side = lax.rem(i, 2)
+
+        @pl.when(i < BLOCKS)
+        def _():
+            for copy in load(b):
+                copy.wait()
+        places = [pos_ref[b * BLOCK + t] for t in range(BLOCK)]
+
+        def patch(t):
+            rows = pl.ds(pl.multiple_of((places[t] >> 2) * 16, 16), 16)
+            put = sub16 == (places[t] & 3)
+            both = knv[b * BLOCK + t]
+            swapped = pltpu.roll(both, 4, 0)
+            for n8, buf in ((jnp.where(low, both, swapped), kbuf), (jnp.where(low, swapped, both), vbuf)):
+                n16 = jnp.concatenate([n8, n8], axis=0)
+                old = buf[slot, t, rows, :].astype(F32)
+                buf[slot, t, rows, :] = jnp.where(put, n16, old).astype(BF16)
+
+        def score(t):
+            s = dot_nt(qrow[b * BLOCK + t].astype(BF16), kbuf[slot, t]) * scale
+            s = jnp.where(same_head & (slot_of <= places[t]), s, NEG)
+            e = jnp.exp(s - jnp.max(s, axis=1, keepdims=True))
+            probs[side, t] = e / jnp.sum(e, axis=1, keepdims=True)
+
+        def mix(t):
+            orow[t] = dot(probs[1 - side, t].astype(BF16), vbuf[prev_slot, t])
+
+        half = BLOCK // 2
+        first, second = range(half), range(half, BLOCK)
+        for t in first:
+            patch(t)
+        for t in first:
+            score(t)
+        for t in second:
+            patch(t)
+        for t in first:
+            mix(t)
+        for t in second:
+            score(t)
+        for t in second:
+            mix(t)
+        rows = pl.ds(pl.multiple_of(prev * BLOCK, BLOCK), BLOCK)
         for r in range(8):
             o_ref[rows, r * 128:(r + 1) * 128] = orow[:, r, :].astype(BF16)
-        for copy in save(b):
-            copy.start()
-
-        @pl.when(b >= 2)
-        def _():
-            for copy in save(b - 2):
+
+        @pl.when(i >= 1)
+        def _():
+            for copy in save(prev):
+                copy.start()
+
+        @pl.when(i >= 3)
+        def _():
+            for copy in save(i - 3):
                 copy.wait()
 
-            @pl.when(b - 2 + RING < BLOCKS)
+            @pl.when(i - 3 + RING < BLOCKS)
             def _():
-                for copy in load(b - 2 + RING):
+                for copy in load(i - 3 + RING):
                     copy.start()
         return carry
-    lax.fori_loop(0, BLOCKS, block_body, 0)
+    lax.fori_loop(0, BLOCKS + 1, block_body, 0)
     for b in (BLOCKS - 2, BLOCKS - 1):
         for copy in save(jnp.int32(b)):
             copy.wait()
 
 
-def attend(positions, x, gain, cos, sin, ids, router, w_kv, w_query, k_cache, v_cache):
+def attend(positions, x, gain, table, pos_row, ids_t, router_t, w_kv, w_query, k_cache, v_cache):
     any_spec = pl.BlockSpec(memory_space=pl.ANY)
     vmem = pl.BlockSpec(memory_space=pltpu.VMEM)
     smem = pl.BlockSpec(memory_space=pltpu.SMEM)
@@ -222,11 +268,14 @@
     return pl.pallas_call(
         attend_kernel,
         name='attend',
-        out_shape=(cache, cache, jax.ShapeDtypeStruct((TOKENS, 2 * QUERY_COLS), BF16), jax.ShapeDtypeStruct((TOKENS, EXPERTS), F32)),
+        out_shape=(cache, cache, jax.ShapeDtypeStruct((TOKENS, 2 * QUERY_COLS), BF16),
+                   jax.ShapeDtypeStruct((TOKENS, EXPERTS), F32), jax.ShapeDtypeStruct((TOKENS, EXPERTS), jnp.int32)),
         in_specs=[smem] + [vmem] * 6 + [any_spec] * 4,
-        out_specs=(any_spec, any_spec, vmem, vmem),
+        out_specs=(any_spec, any_spec, vmem, vmem, vmem),
         scratch_shapes=[
             pltpu.VMEM((TOKENS, HIDDEN), BF16),
+            pltpu.VMEM((HIDDEN * 8, 128), BF16),
+            pltpu.VMEM((128, 8, 128), F32),
             pltpu.VMEM((HIDDEN, HEADS * 256), BF16),
             pltpu.VMEM((WQ_RING, HIDDEN, QUERY_COLS), BF16),
             pltpu.VMEM((RING, BLOCK, SLOTS * HEADS, HEAD_DIM), BF16),
@@ -234,8 +283,10 @@
             pltpu.VMEM((2, TOKENS, QUERY_COLS), F32),
             pltpu.VMEM((TOKENS, 8, HEAD_DIM), F32),
             pltpu.VMEM((TOKENS, 8, HEAD_DIM), F32),
-            pltpu.VMEM((TOKENS, 8, HEAD_DIM), F32),
             pltpu.VMEM((BLOCK, 8, HEAD_DIM), F32),
+            pltpu.VMEM((2, BLOCK, 8, HEAD_DIM), F32),
+            pltpu.VMEM((TOKENS, HEAD_DIM), F32),
+            pltpu.VMEM((TOKENS, HEAD_DIM), F32),
             pltpu.SemaphoreType.DMA,
             pltpu.SemaphoreType.DMA((WQ_RING,)),
             pltpu.SemaphoreType.DMA((RING,)),
@@ -244,14 +295,16 @@
             pltpu.SemaphoreType.DMA((RING,)),
         ],
         compiler_params=pltpu.CompilerParams(vmem_limit_bytes=VMEM_LIMIT),
-    )(positions, x, gain, cos, sin, ids, router, w_kv, w_query, k_cache, v_cache)
-
-
-def reduce_columns(load_step, wait_step, partial, base_ref, out_ref, send1, recv1, own, recv2, fin, recv3, s1, r1, s2, r2, s3, r3):
+    )(positions, x, gain, table, pos_row, ids_t, router_t, w_kv, w_query, k_cache, v_cache)
+
+
+def reduce_columns(load_step, wait_step, partial, base_hbm, out_ref, base_ref, base_sem, send1, recv1, own, recv2, fin, recv3, s1, r1, s2, r2, s3, r3):
     me = lax.axis_index('tp')
     core = lax.rem(me, 2)
     sibling = me + 1 - 2 * core
     partner = lax.rem(me + 2, 4)
+    base_copy = pltpu.make_async_copy(base_hbm, base_ref, base_sem)
+    base_copy.start()
     barrier = pltpu.get_barrier_semaphore()
     for peer in (sibling, partner):
         pl.semaphore_signal(barrier, inc=1, device_id={'tp': peer}, device_id_type=MESH)
@@ -295,6 +348,7 @@
             load_step(s, column)
         return carry
     lax.fori_loop(0, STEPS // 2, step_body, 0)
+    base_copy.wait()
 
     def place(c, half):
         rows = pl.ds(pl.multiple_of(lax.rem(c, 2) * ROWS, ROWS), ROWS)
@@ -327,7 +381,7 @@
     lax.fori_loop(0, CHUNKS, drain_body, 0)
 
 
-CHUNK_SCRATCH = [pltpu.VMEM((CHUNKS, ROWS, COL), BF16)] * 6 + [pltpu.SemaphoreType.DMA((CHUNKS,))] * 6
+CHUNK_SCRATCH = [pltpu.VMEM((TOKENS, HIDDEN), BF16), pltpu.SemaphoreType.DMA] + [pltpu.VMEM((CHUNKS, ROWS, COL), BF16)] * 6 + [pltpu.SemaphoreType.DMA((CHUNKS,))] * 6
 OUT_RING = 3
 
 
@@ -378,7 +432,7 @@
         out_kernel,
         name='out_project',
         out_shape=jax.ShapeDtypeStruct((TOKENS, HIDDEN), BF16),
-        in_specs=[vmem] * 4 + [pl.BlockSpec(memory_space=pl.ANY)],
+        in_specs=[vmem] * 3 + [pl.BlockSpec(memory_space=pl.ANY)] * 2,
         out_specs=vmem,
         scratch_shapes=[
             pltpu.VMEM((EXPERTS, TOKENS, QUERY_COLS), BF16),
@@ -389,7 +443,7 @@
     )(o, ids, gates, x, w_out)
 
 
-def gate_up_kernel(x_ref, gain_ref, router_ref, ids_ref, idst_ref, wg_hbm, wu_hbm, a_hbm, gates_ref,
+def gate_up_kernel(x_ref, gain_ref, router_ref, idst_ref, wg_hbm, wu_hbm, a_hbm, gates_ref,
                    unorm, picked, scatter, gathered, wg, wu, act, abuf, wg_sem, wu_sem, a_sem):
     first_id = lax.axis_index('tp') * LOCAL
 
@@ -411,9 +465,10 @@
             copy.start()
 
     norm_rows(x_ref, gain_ref, unorm)
-    id0 = ids_ref[:, 0:1]
-    id1 = ids_ref[:, 1:2]
-    logits = dot(unorm[...], router_ref[...])
+    ids = turn((idst_ref[0:1, :], idst_ref[1:2, :]))
+    id0 = ids[:, 0:1]
+    id1 = ids[:, 1:2]
+    logits = dot_nt(unorm[...], router_ref[...])
     g0, g1 = pair_gates(logits, id0, id1)
     lane8 = iota((TOKENS, EXPERTS), 1)
     local8 = lane8 + first_id
@@ -444,37 +499,36 @@
             gathered[e, rows, :] = dot(picked[e, rows, :], unorm[...]).astype(BF16)
             return carry
         lax.fori_loop(0, blocks[e], gather_body, 0)
-    act[...] = jnp.zeros_like(act)
 
     def step_body(s, carry):
         e = lax.div(s, F_TILES)
         slot = lax.rem(s, W_RING)
+        out_slot = lax.rem(s, 2)
         for copy in load(s):
             copy.wait()
 
-        def row_body(rb, c):
-            rows = pl.ds(pl.multiple_of(rb * RB, RB), RB)
-            gate = dot(gathered[e, rows, :], wg[slot])
-            up = dot(gathered[e, rows, :], wu[slot])
-            act[rows, :] = (gate * (1.0 / (1.0 + jnp.exp(-gate))) * up).astype(BF16)
-            return c
-        lax.fori_loop(0, jnp.where(e == 0, blocks[0], blocks[1]), row_body, 0)
+        @pl.when(s >= 2)
+        def _():
+            save(s - 2).wait()
+
+        def run(count):
+            for n in range(FT // COL):
+                cols = slice(n * COL, (n + 1) * COL)
+                gate = dot(gathered[e, :count, :], wg[slot, :, cols])
+                up = dot(gathered[e, :count, :], wu[slot, :, cols])
+                act[:count, cols] = (gate * (1.0 / (1.0 + jnp.exp(-gate))) * up).astype(BF16)
+            for m in range(TOKENS // ROWS):
+                rows = slice(m * ROWS, (m + 1) * ROWS)
+                abuf[out_slot, rows, :] = dot(scatter[e, rows, :count], act[:count, :]).astype(BF16)
+
+        n_blocks = jnp.where(e == 0, blocks[0], blocks[1])
+        for k in range(1, TOKENS // RB + 1):
+            pl.when(n_blocks == k)(functools.partial(run, k * RB))
 
         @pl.when(s + W_RING < MLP_STEPS)
         def _():
             for copy in load(s + W_RING):
                 copy.start()
-
-        @pl.when(s >= 2)
-        def _():
-            save(s - 2).wait()
-        out_slot = lax.rem(s, 2)
-
-        def scatter_body(m, c):
-            rows = pl.ds(pl.multiple_of(m * ROWS, ROWS), ROWS)
-            abuf[out_slot, rows, :] = dot(scatter[e, rows, :], act[...]).astype(BF16)
-            return c
-        lax.fori_loop(0, TOKENS // ROWS, scatter_body, 0)
         save(s).start()
         return carry
     lax.fori_loop(0, MLP_STEPS, step_body, 0)
@@ -482,14 +536,14 @@
         save(jnp.int32(s)).wait()
 
 
-def gate_up(x_mid, gain, router, ids, ids_t, w_gate, w_up):
+def gate_up(x_mid, gain, router_t, ids_t, w_gate, w_up):
     any_spec = pl.BlockSpec(memory_space=pl.ANY)
     vmem = pl.BlockSpec(memory_space=pltpu.VMEM)
     return pl.pallas_call(
         gate_up_kernel,
         name='gate_up',
         out_shape=(jax.ShapeDtypeStruct((LOCAL, TOKENS, FFN), BF16), jax.ShapeDtypeStruct((TOKENS, EXPERTS), F32)),
-        in_specs=[vmem] * 5 + [any_spec] * 2,
+        in_specs=[vmem] * 4 + [any_spec] * 2,
         out_specs=(any_spec, vmem),
         scratch_shapes=[
             pltpu.VMEM((TOKENS, HIDDEN), BF16),
@@ -505,7 +559,7 @@
             pltpu.SemaphoreType.DMA((2,)),
         ],
         compiler_params=pltpu.CompilerParams(vmem_limit_bytes=VMEM_LIMIT),
-    )(x_mid, gain, router, ids, ids_t, w_gate, w_up)
+    )(x_mid, gain, router_t, ids_t, w_gate, w_up)
 
 
 DOWN_RING = 2
@@ -554,7 +608,7 @@
         down_kernel,
         name='down_project',
         out_shape=jax.ShapeDtypeStruct((TOKENS, HIDDEN), BF16),
-        in_specs=[vmem] * 2 + [any_spec] * 2,
+        in_specs=[vmem] + [any_spec] * 3,
         out_specs=vmem,
         scratch_shapes=[
             pltpu.VMEM((LOCAL, TOKENS, FFN), BF16),
@@ -566,24 +620,33 @@
     )(gates, x_mid, act, w_down)
 
 
-def rope_rows(positions):
+def rope_table():
     half = HEAD_DIM // 2
-    inv_freq = ROPE_BASE ** (-(jnp.arange(half, dtype=F32) * 2.0 / HEAD_DIM))
-    inv_freq = jnp.concatenate([inv_freq, inv_freq])
-    sign = jnp.concatenate([-jnp.ones(half, F32), jnp.ones(half, F32)])
-    angles = positions.astype(F32)[:, None] * inv_freq[None, :]
-    return jnp.cos(angles), jnp.sin(angles) * sign
+    inv_freq = np.float32(ROPE_BASE) ** (-(np.arange(half, dtype=np.float32) * np.float32(2.0) / np.float32(HEAD_DIM)))
+    angles = np.arange(SLOTS, dtype=np.float32)[:, None] * inv_freq[None, :].astype(np.float32)
+    cos = np.cos(angles.astype(np.float64))
+    sin = np.sin(angles.astype(np.float64))
+    full = np.concatenate([cos, cos, -sin, sin], axis=1).astype(np.float32)
+    parts = []
+    for _ in range(3):
+        part = full.astype(BF16)
+        parts.append(part)
+        full = full - part.astype(np.float32)
+    parts.append(np.zeros_like(parts[0]))
+    return np.concatenate(parts, axis=0)
 
 
 def solution(mesh):
+    table = rope_table()
+
     def local_step(x, k_cache, v_cache, positions, att_ids, mlp_ids, norm_att, w_kv, router_att, w_query, w_out, norm_mlp, router_mlp, w_gate, w_up, w_down):
-        cos, sin = rope_rows(positions)
         flat = (TOKENS, SLOTS * HEADS, HEAD_DIM)
-        k_new, v_new, o, att_gates = attend(
-            positions, x, norm_att.reshape(1, HIDDEN), cos, sin, att_ids, router_att,
-            w_kv.reshape(HIDDEN, HEADS * 256), w_query, k_cache.reshape(flat), v_cache.reshape(flat))
-        x_mid = out_project(o, att_ids, att_gates, x, w_out)
-        act, mlp_gates = gate_up(x_mid, norm_mlp.reshape(1, HIDDEN), router_mlp, mlp_ids, mlp_ids.T, w_gate, w_up)
+        kv_rows = w_kv.reshape(HIDDEN, HEADS, 2, HEAD_DIM).transpose(0, 2, 1, 3).reshape(HIDDEN * 8, HEAD_DIM)
+        k_new, v_new, o, att_gates, att_cols = attend(
+            positions, x, norm_att.reshape(1, HIDDEN), jnp.asarray(table), positions.reshape(1, TOKENS), att_ids.T, router_att.T,
+            kv_rows, w_query, k_cache.reshape(flat), v_cache.reshape(flat))
+        x_mid = out_project(o, att_cols, att_gates, x, w_out)
+        act, mlp_gates = gate_up(x_mid, norm_mlp.reshape(1, HIDDEN), router_mlp.T, mlp_ids.T, w_gate, w_up)
         x_out = down_project(mlp_gates, x_mid, act, w_down)
         return x_out, k_new.reshape(k_cache.shape), v_new.reshape(v_cache.shape)
 

time: 220 us -> 185 us (0.84); the launches traced: 218 us -> 185 us
  Pallas kernels: 199 us -> 182 us
  local copies, waits for them, and re-layouts: 14.9 us -> 3.16 us
  other arithmetic: 3.24 us -> 0 us
    unnamed x6 -> x1, local copies, waits for them, and re-layouts: 14.9 us -> 3.16 us
    pallas_call x1, Pallas kernels: 68.1 us -> 58.2 us  [attend(): pl.pallas_call(attend_kernel, name='attend', out_shape=(cache, cache, jax...]
    pallas_call x1, Pallas kernels: 57.5 us -> 51.8 us  [down_project(): pl.pallas_call(down_kernel, name='down_project', out_shape=jax.ShapeDtype...]
    mul x1 -> x0, other arithmetic: 2.46 us -> none  [rope_rows(): return (jnp.cos(angles), jnp.sin(angles) * sign)]
where the time goes in v2:
time: 185 us
  Pallas kernels  182 us (98%)
  local copies, waits for them, and re-layouts  3.16 us (2%)
    pallas_call x1, Pallas kernels, attend(): pl.pallas_call(attend_kernel, name='attend', out_shape=(cache, cache, jax...  58.2 us
    pallas_call x1, Pallas kernels, down_project(): pl.pallas_call(down_kernel, name='down_project', out_shape=jax.ShapeDtype...  51.8 us
    pallas_call x1, Pallas kernels, gate_up(): pl.pallas_call(gate_up_kernel, name='gate_up', out_shape=(jax.ShapeDtypeS...  36.3 us
    pallas_call x1, Pallas kernels, out_project(): pl.pallas_call(out_kernel, name='out_project', out_shape=jax.ShapeDtypeSt...  35.2 us

profile of v2, /device:TPU:0, one launch (start us, length us, event | category | flops | bytes accessed | tf_op | source)
XLA Modules:
  0.0 185.4 jit_solution(17148155142282657484)
XLA Ops:
  0.6 58.2 %attend.1 = (bf16[512,128,128]{2,1,0:T(8,128)(2,1)}, bf16[512,128,128]{2,1,0:T(8,128)(2,1)}, bf16[512,1024]{1,0:T(8,128)(2,1)}, f32[512,8]{1,0:T(8,128)}, s32[512,8]{1,0:T(8,128)}) custom-call(s32[512]{0:T(512)} %pos_ref.1, bf16[512,2048]{1,0:T(8,128)(2,1)} %x_ref.3, f32[1,2048]{1,0:T(1,128)} %bitcast.21, bf16[128,256]{1,0:T(8,128)(2,1)} %constant.2.clone.table_ref, ...), custom_call_target="tpu_custom_call" | custom-call | tf_op jit(solution)/shard_map/attend/pallas_call | solution.py:268
  58.9 35.2 %out_project.1.x_ref = bf16[512,2048]{1,0:T(8,128)(2,1)} custom-call(bf16[512,1024]{1,0:T(8,128)(2,1)} %get-tuple-element.10.o_ref, s32[512,8]{1,0:T(8,128)} %get-tuple-element.11.ids_ref, f32[512,8]{1,0:T(8,128)} %get-tuple-element.12.gates_ref, bf16[512,2048]{1,0:T(8,128)(2,1)} %x_ref.3, bf16[8,512,2048]{2,1,0:T(8,128)(2,1)} %w_hbm.2), custom_call_target="tpu_custom_call" | custom-call | tf_op jit(solution)/shard_map/out_project/pallas_call | solution.py:431
  94.1 36.3 %gate_up.1 = (bf16[2,512,5632]{2,1,0:T(8,128)(2,1)}, f32[512,8]{1,0:T(8,128)}) custom-call(bf16[512,2048]{1,0:T(8,128)(2,1)} %out_project.1.x_ref, f32[1,2048]{1,0:T(1,128)} %bitcast.22, bf16[8,2048]{1,0:T(8,128)(2,1)} %bitcast.20, s32[2,512]{1,0:T(2,128)} %bitcast.25, bf16[2,2048,5632]{2,1,0:T(8,128)(2,1)} %wg_hbm.1, bf16[2,2048,5632]{2,1,0:T(8,128)(2,1)} %wu_hbm.1), custom_call_target="tpu_custom_call" | custom-call | tf_op jit(solution)/shard_map/gate_up/pallas_call | solution.py:542
  130.5 51.8 %down_project.1 = bf16[512,2048]{1,0:T(8,128)(2,1)} custom-call(f32[512,8]{1,0:T(8,128)} %get-tuple-element.13.gates_ref, bf16[512,2048]{1,0:T(8,128)(2,1)} %out_project.1.x_ref, bf16[2,512,5632]{2,1,0:T(8,128)(2,1)} %get-tuple-element.14.a_hbm, bf16[2,5632,2048]{2,1,0:T(8,128)(2,1)} %w_hbm.3), custom_call_target="tpu_custom_call" | custom-call | tf_op jit(solution)/shard_map/down_project/pallas_call | solution.py:607
  182.3 3.2 %copy.22 = bf16[512,2048]{1,0:T(8,128)(2,1)} copy(bf16[512,2048]{1,0:T(8,128)(2,1)} %down_project.1) | data formatting | bytes 4194304

commit v3 on v2

--- a/solution.py
+++ b/solution.py
@@ -85,10 +85,10 @@
     return lax.dot_general(a, b, (((1,), (1,)), ((), ())), preferred_element_type=F32)
 
 
-def attend_kernel(pos_ref, x_ref, gain_ref, table_ref, posrow_ref, idst_ref, router_ref, wkv_hbm, wq_hbm, kc_hbm, vc_hbm,
-                  ko_hbm, vo_hbm, o_ref, gates_ref, ids_ref,
-                  hid, wraw, wtmp, wkv, wq, kbuf, vbuf, qsel, qrow, knv, orow, probs, cos_s, sin_s,
-                  wkv_sem, wq_sem, kin_sem, vin_sem, kout_sem, vout_sem):
+def project_kernel(pos_ref, x_ref, gain_ref, table_ref, posrow_ref, idst_ref, router_ref, wkv_hbm, wq_hbm, kc_hbm, vc_hbm,
+                   ko_hbm, vo_hbm, qrow, gates_ref, ids_ref,
+                   hid, wraw, wtmp, wkv, wq, kbuf, vbuf, qsel, knv, cos_s, sin_s,
+                   wkv_sem, wq_sem, kin_sem, vin_sem, kout_sem, vout_sem):
     def block_of(ref, b):
         return ref.at[pl.ds(pl.multiple_of(b * BLOCK, BLOCK), BLOCK)]
 
@@ -121,19 +121,16 @@
     trig = dot(jnp.where(chosen, 1.0, 0.0).astype(BF16), table_ref[...])
     cos_s[...] = trig[:, :HEAD_DIM]
     sin_s[...] = trig[:, HEAD_DIM:]
-    logits = dot_nt(hid[...], router_ref[...])
-    g0, g1 = pair_gates(logits, id0, id1)
-    lane8 = iota((TOKENS, EXPERTS), 1)
-    gates_ref[...] = jnp.where(lane8 == id0, g0, 0.0) + jnp.where(lane8 == id1, g1, 0.0)
-
+    for b in range(RING):
+        for copy in load(jnp.int32(b)):
+            copy.start()
     kv_copy.wait()
 
     def sort_body(i, carry):
-        raw = wraw[pl.ds(pl.multiple_of(i * 1024, 1024), 1024), :].astype(F32)
-        wtmp[...] = raw.reshape(128, 8, 128)
+        wtmp[...] = wraw[pl.ds(pl.multiple_of(i * 1024, 1024), 1024), :].astype(F32)
         rows = pl.ds(pl.multiple_of(i * 128, 128), 128)
         for j in range(8):
-            wkv[rows, j * 128:(j + 1) * 128] = wtmp[:, j, :].astype(BF16)
+            wkv[rows, j * 128:(j + 1) * 128] = wtmp[pl.ds(j, 128, stride=8), :].astype(BF16)
         return carry
     lax.fori_loop(0, HIDDEN // 128, sort_body, 0)
 
@@ -144,31 +141,63 @@
         sin = sin_s[rows, :]
         for h in range(HEADS):
             k = kv[:, h * 128:(h + 1) * 128]
-            knv[rows, h, :] = k * cos + pltpu.roll(k, 64, 1) * sin
-            knv[rows, h + 4, :] = kv[:, (h + 4) * 128:(h + 5) * 128]
+            knv[pl.ds(m * (ROWS * 8) + h, ROWS, stride=8), :] = k * cos + pltpu.roll(k, 64, 1) * sin
+            knv[pl.ds(m * (ROWS * 8) + h + 4, ROWS, stride=8), :] = kv[:, (h + 4) * 128:(h + 5) * 128]
         return carry
     lax.fori_loop(0, TOKENS // ROWS, kv_body, 0)
 
-    def q_body(e, carry):
-        for copy in load(e):
+    sub16 = iota((16, HEAD_DIM), 0) >> 2
+    low = iota((8, 128), 0) < 4
+
+    def block_body(b, carry):
+        e = lax.div(b, 2)
+        m = lax.rem(b, 2)
+        slot = lax.rem(b, RING)
+        wslot = lax.rem(e, WQ_RING)
+
+        @pl.when(m == 0)
+        def _():
+            load_wq(e).wait()
+        for copy in load(b):
+            copy.wait()
+        rows = pl.ds(pl.multiple_of(m * ROWS, ROWS), ROWS)
+        q = dot(hid[rows, :], wq[wslot])
+        for t in range(BLOCK):
+            place = pos_ref[b * BLOCK + t]
+            lines = pl.ds(pl.multiple_of((place >> 2) * 16, 16), 16)
+            put = sub16 == (place & 3)
+            both = knv[pl.ds(pl.multiple_of((b * BLOCK + t) * 8, 8), 8), :]
+            swapped = pltpu.roll(both, 4, 0)
+            for n8, buf in ((jnp.where(low, both, swapped), kbuf), (jnp.where(low, swapped, both), vbuf)):
+                n16 = jnp.concatenate([n8, n8], axis=0)
+                old = buf[slot, t, lines, :].astype(F32)
+                buf[slot, t, lines, :] = jnp.where(put, n16, old).astype(BF16)
+        for k in range(2):
+            picked = ids_ref[rows, k:k + 1] == e
+            qsel[k, rows, :] = jnp.where(picked, q, qsel[k, rows, :])
+        for copy in save(b):
             copy.start()
-        load_wq(e).wait()
-        slot = lax.rem(e, WQ_RING)
-
-        def m_body(m, c):
-            rows = pl.ds(pl.multiple_of(m * ROWS, ROWS), ROWS)
-            q = dot(hid[rows, :], wq[slot])
-            for k in range(2):
-                picked = ids_ref[rows, k:k + 1] == e
-                qsel[k, rows, :] = jnp.where(picked, q, qsel[k, rows, :])
-            return c
-        lax.fori_loop(0, TOKENS // ROWS, m_body, 0)
-
-        @pl.when(e + WQ_RING < EXPERTS)
+
+        @pl.when((m == 1) & (e + WQ_RING < EXPERTS))
         def _():
             load_wq(e + WQ_RING).start()
-        return carry
-    lax.fori_loop(0, EXPERTS, q_body, 0)
+
+        @pl.when(b >= 2)
+        def _():
+            for copy in save(b - 2):
+                copy.wait()
+
+            @pl.when(b - 2 + RING < BLOCKS)
+            def _():
+                for copy in load(b - 2 + RING):
+                    copy.start()
+        return carry
+    lax.fori_loop(0, BLOCKS, block_body, 0)
+
+    logits = dot_nt(hid[...], router_ref[...])
+    g0, g1 = pair_gates(logits, id0, id1)
+    lane8 = iota((TOKENS, EXPERTS), 1)
+    gates_ref[...] = jnp.where(lane8 == id0, g0, 0.0) + jnp.where(lane8 == id1, g1, 0.0)
 
     def rope_body(m, carry):
         rows = pl.ds(pl.multiple_of(m * 128, 128), 128)
@@ -177,114 +206,36 @@
         for k in range(2):
             for h in range(HEADS):
                 q = qsel[k, rows, h * 128:(h + 1) * 128]
-                qrow[rows, k * HEADS + h, :] = q * cos + pltpu.roll(q, 64, 1) * sin
+                qrow[pl.ds(m * 1024 + k * HEADS + h, 128, stride=8), :] = q * cos + pltpu.roll(q, 64, 1) * sin
         return carry
     lax.fori_loop(0, TOKENS // 128, rope_body, 0)
-
-    scale = HEAD_DIM ** -0.5
-    sub16 = iota((16, HEAD_DIM), 0) >> 2
-    row8 = iota((8, 128), 0)
-    lane = iota((8, 128), 1)
-    low = row8 < 4
-    same_head = (lane & 3) == (row8 & 3)
-    slot_of = lane >> 2
-
-    def block_body(i, carry):
-        b = jnp.minimum(i, BLOCKS - 1)
-        prev = jnp.maximum(i - 1, 0)
-        slot = lax.rem(b, RING)
-        prev_slot = lax.rem(prev, RING)
-        side = lax.rem(i, 2)
-
-        @pl.when(i < BLOCKS)
-        def _():
-            for copy in load(b):
-                copy.wait()
-        places = [pos_ref[b * BLOCK + t] for t in range(BLOCK)]
-
-        def patch(t):
-            rows = pl.ds(pl.multiple_of((places[t] >> 2) * 16, 16), 16)
-            put = sub16 == (places[t] & 3)
-            both = knv[b * BLOCK + t]
-            swapped = pltpu.roll(both, 4, 0)
-            for n8, buf in ((jnp.where(low, both, swapped), kbuf), (jnp.where(low, swapped, both), vbuf)):
-                n16 = jnp.concatenate([n8, n8], axis=0)
-                old = buf[slot, t, rows, :].astype(F32)
-                buf[slot, t, rows, :] = jnp.where(put, n16, old).astype(BF16)
-
-        def score(t):
-            s = dot_nt(qrow[b * BLOCK + t].astype(BF16), kbuf[slot, t]) * scale
-            s = jnp.where(same_head & (slot_of <= places[t]), s, NEG)
-            e = jnp.exp(s - jnp.max(s, axis=1, keepdims=True))
-            probs[side, t] = e / jnp.sum(e, axis=1, keepdims=True)
-
-        def mix(t):
-            orow[t] = dot(probs[1 - side, t].astype(BF16), vbuf[prev_slot, t])
-
-        half = BLOCK // 2
-        first, second = range(half), range(half, BLOCK)
-        for t in first:
-            patch(t)
-        for t in first:
-            score(t)
-        for t in second:
-            patch(t)
-        for t in first:
-            mix(t)
-        for t in second:
-            score(t)
-        for t in second:
-            mix(t)
-        rows = pl.ds(pl.multiple_of(prev * BLOCK, BLOCK), BLOCK)
-        for r in range(8):
-            o_ref[rows, r * 128:(r + 1) * 128] = orow[:, r, :].astype(BF16)
-
-        @pl.when(i >= 1)
-        def _():
-            for copy in save(prev):
-                copy.start()
-
-        @pl.when(i >= 3)
-        def _():
-            for copy in save(i - 3):
-                copy.wait()
-
-            @pl.when(i - 3 + RING < BLOCKS)
-            def _():
-                for copy in load(i - 3 + RING):
-                    copy.start()
-        return carry
-    lax.fori_loop(0, BLOCKS + 1, block_body, 0)
     for b in (BLOCKS - 2, BLOCKS - 1):
         for copy in save(jnp.int32(b)):
             copy.wait()
 
 
-def attend(positions, x, gain, table, pos_row, ids_t, router_t, w_kv, w_query, k_cache, v_cache):
+def project(positions, x, gain, table, pos_row, ids_t, router_t, w_kv, w_query, k_cache, v_cache):
     any_spec = pl.BlockSpec(memory_space=pl.ANY)
     vmem = pl.BlockSpec(memory_space=pltpu.VMEM)
     smem = pl.BlockSpec(memory_space=pltpu.SMEM)
     cache = jax.ShapeDtypeStruct(k_cache.shape, BF16)
     return pl.pallas_call(
-        attend_kernel,
-        name='attend',
-        out_shape=(cache, cache, jax.ShapeDtypeStruct((TOKENS, 2 * QUERY_COLS), BF16),
+        project_kernel,
+        name='project',
+        out_shape=(cache, cache, jax.ShapeDtypeStruct((TOKENS * 8, HEAD_DIM), F32),
                    jax.ShapeDtypeStruct((TOKENS, EXPERTS), F32), jax.ShapeDtypeStruct((TOKENS, EXPERTS), jnp.int32)),
         in_specs=[smem] + [vmem] * 6 + [any_spec] * 4,
         out_specs=(any_spec, any_spec, vmem, vmem, vmem),
         scratch_shapes=[
             pltpu.VMEM((TOKENS, HIDDEN), BF16),
             pltpu.VMEM((HIDDEN * 8, 128), BF16),
-            pltpu.VMEM((128, 8, 128), F32),
+            pltpu.VMEM((1024, 128), F32),
             pltpu.VMEM((HIDDEN, HEADS * 256), BF16),
             pltpu.VMEM((WQ_RING, HIDDEN, QUERY_COLS), BF16),
             pltpu.VMEM((RING, BLOCK, SLOTS * HEADS, HEAD_DIM), BF16),
             pltpu.VMEM((RING, BLOCK, SLOTS * HEADS, HEAD_DIM), BF16),
             pltpu.VMEM((2, TOKENS, QUERY_COLS), F32),
-            pltpu.VMEM((TOKENS, 8, HEAD_DIM), F32),
-            pltpu.VMEM((TOKENS, 8, HEAD_DIM), F32),
-            pltpu.VMEM((BLOCK, 8, HEAD_DIM), F32),
-            pltpu.VMEM((2, BLOCK, 8, HEAD_DIM), F32),
+            pltpu.VMEM((TOKENS * 8, HEAD_DIM), F32),
             pltpu.VMEM((TOKENS, HEAD_DIM), F32),
             pltpu.VMEM((TOKENS, HEAD_DIM), F32),
             pltpu.SemaphoreType.DMA,
@@ -298,7 +249,7 @@
     )(positions, x, gain, table, pos_row, ids_t, router_t, w_kv, w_query, k_cache, v_cache)
 
 
-def reduce_columns(load_step, wait_step, partial, base_hbm, out_ref, base_ref, base_sem, send1, recv1, own, recv2, fin, recv3, s1, r1, s2, r2, s3, r3):
+def reduce_columns(drive, partial, base_hbm, out_ref, base_ref, base_sem, send1, recv1, own, recv2, fin, recv3, s1, r1, s2, r2, s3, r3):
     me = lax.axis_index('tp')
     core = lax.rem(me, 2)
     sibling = me + 1 - 2 * core
@@ -327,27 +278,20 @@
     def share(c):
         return remote(fin, recv3, c, s3, r3, sibling)
 
-    def step_body(i, carry):
-        for parity in range(2):
-            s = 2 * i + parity
-            wait_step(s, column(s))
-
-            def row_body(m, c):
-                rows = pl.ds(pl.multiple_of(m * ROWS, ROWS), ROWS)
-                chunk = 2 * i + m
-                acc = partial(s, rows)
-                if parity == 0:
-                    send1[chunk] = acc.astype(BF16)
-                    to_sibling(chunk).start()
-                else:
-                    to_sibling(chunk).wait_recv()
-                    own[chunk] = (acc + recv1[chunk].astype(F32)).astype(BF16)
-                    to_partner(chunk).start()
-                return c
-            lax.fori_loop(0, TOKENS // ROWS, row_body, 0)
-            load_step(s, column)
-        return carry
-    lax.fori_loop(0, STEPS // 2, step_body, 0)
+    def chunk_step(i, parity, m):
+        s = 2 * i + parity
+        rows = pl.ds(pl.multiple_of(m * ROWS, ROWS), ROWS)
+        chunk = 2 * i + m
+        acc = partial(s, rows, column(s))
+        if parity == 0:
+            send1[chunk] = acc.astype(BF16)
+            to_sibling(chunk).start()
+        else:
+            to_sibling(chunk).wait_recv()
+            own[chunk] = (acc + recv1[chunk].astype(F32)).astype(BF16)
+            to_partner(chunk).start()
+
+    drive(chunk_step, column)
     base_copy.wait()
 
     def place(c, half):
@@ -382,65 +326,142 @@
 
 
 CHUNK_SCRATCH = [pltpu.VMEM((TOKENS, HIDDEN), BF16), pltpu.SemaphoreType.DMA] + [pltpu.VMEM((CHUNKS, ROWS, COL), BF16)] * 6 + [pltpu.SemaphoreType.DMA((CHUNKS,))] * 6
-OUT_RING = 3
-
-
-def out_kernel(o_ref, ids_ref, gates_ref, x_ref, w_hbm, out_ref, spread, wbuf, w_sem, *chunk_refs):
-    me = lax.axis_index('tp')
-    core = lax.rem(me, 2)
-
-    def copy_of(s, col):
-        slot = lax.rem(s, OUT_RING)
-        return pltpu.make_async_copy(w_hbm.at[:, :, pl.ds(col, COL)], wbuf.at[slot], w_sem.at[slot])
-
-    for s in range(OUT_RING):
-        half = lax.rem(core + 1 + s, 2)
-        copy_of(jnp.int32(s), pl.multiple_of((half * (STEPS // 2) + s // 2) * COL, COL)).start()
-
-    def spread_body(m, carry):
-        rows = pl.ds(pl.multiple_of(m * 128, 128), 128)
-        first = o_ref[rows, :QUERY_COLS].astype(F32)
-        second = o_ref[rows, QUERY_COLS:].astype(F32)
-        for e in range(EXPERTS):
-            picked = jnp.where(ids_ref[rows, 0:1] == e, first, 0.0)
-            picked = jnp.where(ids_ref[rows, 1:2] == e, second, picked)
-            spread[e, rows, :] = picked.astype(BF16)
-        return carry
-    lax.fori_loop(0, TOKENS // 128, spread_body, 0)
-
-    def load_step(s, column):
-        @pl.when(s + OUT_RING < STEPS)
-        def _():
-            copy_of(s + OUT_RING, column(s + OUT_RING)).start()
-
-    def wait_step(s, col):
-        copy_of(s, col).wait()
-
-    def partial(s, rows):
-        slot = lax.rem(s, OUT_RING)
+A_RING = 8
+HALF_BLOCKS = ROWS // BLOCK
+
+
+def attend_kernel(pos_ref, ids_ref, gates_ref, q_hbm, kc_hbm, vc_hbm, w_hbm, x_hbm, out_ref,
+                  qrow, kbuf, vbuf, probs, orow, mixed, spread, wbuf, q_sem, k_sem, v_sem, w_sem, *chunk_refs):
+    def load(b):
+        slot = lax.rem(b, A_RING)
+        rows = pl.ds(pl.multiple_of(b * BLOCK, BLOCK), BLOCK)
+        return (pltpu.make_async_copy(kc_hbm.at[rows], kbuf.at[slot], k_sem.at[slot]),
+                pltpu.make_async_copy(vc_hbm.at[rows], vbuf.at[slot], v_sem.at[slot]))
+
+    q_copy = pltpu.make_async_copy(q_hbm, qrow, q_sem)
+    q_copy.start()
+    for b in range(A_RING):
+        for copy in load(jnp.int32(b)):
+            copy.start()
+    w_copies = [pltpu.make_async_copy(w_hbm.at[e], wbuf.at[e], w_sem.at[e]) for e in range(EXPERTS)]
+    for copy in w_copies:
+        copy.start()
+
+    scale = HEAD_DIM ** -0.5
+    row8 = iota((8, 128), 0)
+    lane = iota((8, 128), 1)
+    same_head = (lane & 3) == (row8 & 3)
+    slot_of = lane >> 2
+
+    def attend_rows(m):
+        def block_body(i, carry):
+            b = m * HALF_BLOCKS + jnp.minimum(i, HALF_BLOCKS - 1)
+            before = jnp.maximum(i - 1, 0)
+            prev = m * HALF_BLOCKS + before
+            slot = lax.rem(b, A_RING)
+            prev_slot = lax.rem(prev, A_RING)
+            side = lax.rem(i, 2)
+
+            @pl.when(i < HALF_BLOCKS)
+            def _():
+                for copy in load(b):
+                    copy.wait()
+
+            def score(t):
+                q = qrow[pl.ds(pl.multiple_of((b * BLOCK + t) * 8, 8), 8), :].astype(BF16)
+                s = dot_nt(q, kbuf[slot, t]) * scale
+                s = jnp.where(same_head & (slot_of <= pos_ref[b * BLOCK + t]), s, NEG)
+                e = jnp.exp(s - jnp.max(s, axis=1, keepdims=True))
+                probs[side, t] = e / jnp.sum(e, axis=1, keepdims=True)
+
+            def mix(t):
+                orow[t * 8:(t + 1) * 8, :] = dot(probs[1 - side, t].astype(BF16), vbuf[prev_slot, t])
+
+            half = BLOCK // 2
+            for t in range(half):
+                score(t)
+            for t in range(half):
+                mix(t)
+            for t in range(half, BLOCK):
+                score(t)
+            for t in range(half, BLOCK):
+                mix(t)
+            rows = pl.ds(pl.multiple_of(before * BLOCK, BLOCK), BLOCK)
+            for r in range(8):
+                mixed[rows, r * 128:(r + 1) * 128] = orow[pl.ds(r, BLOCK, stride=8), :].astype(BF16)
+
+            @pl.when((i >= 1) & (prev + A_RING < BLOCKS))
+            def _():
+                for copy in load(prev + A_RING):
+                    copy.start()
+            return carry
+        lax.fori_loop(0, HALF_BLOCKS + 1, block_body, 0)
+
+        def spread_body(n, carry):
+            rows = pl.ds(pl.multiple_of(n * 64, 64), 64)
+            from_rows = pl.ds(pl.multiple_of(m * ROWS + n * 64, 64), 64)
+            first = mixed[rows, :QUERY_COLS].astype(F32)
+            second = mixed[rows, QUERY_COLS:].astype(F32)
+            for e in range(EXPERTS):
+                picked = jnp.where(ids_ref[from_rows, 0:1] == e, first, 0.0)
+                picked = jnp.where(ids_ref[from_rows, 1:2] == e, second, picked)
+                spread[e, rows, :] = picked.astype(BF16)
+            return carry
+        lax.fori_loop(0, ROWS // 64, spread_body, 0)
+
+    def partial(s, rows, col):
         acc = jnp.zeros((ROWS, COL), F32)
         for e in range(EXPERTS):
-            acc = acc + gates_ref[rows, e:e + 1] * dot(spread[e, rows, :], wbuf[slot, e])
+            acc = acc + gates_ref[rows, e:e + 1] * dot(spread[e], wbuf[e, :, pl.ds(col, COL)])
         return acc
 
-    reduce_columns(load_step, wait_step, partial, x_ref, out_ref, *chunk_refs)
-
-
-def out_project(o, ids, gates, x, w_out):
+    def drive(chunk_step, column):
+        q_copy.wait()
+
+        def half_body(m, carry):
+            attend_rows(m)
+
+            @pl.when(m == 0)
+            def _():
+                for copy in w_copies:
+                    copy.wait()
+
+            def col_body(i, c):
+                for parity in range(2):
+                    chunk_step(i, parity, m)
+                return c
+            lax.fori_loop(0, STEPS // 2, col_body, 0)
+            return carry
+        lax.fori_loop(0, TOKENS // ROWS, half_body, 0)
+
+    reduce_columns(drive, partial, x_hbm, out_ref, *chunk_refs)
+
+
+def attend(positions, ids, gates, q, k_cache, v_cache, w_out, x):
     vmem = pl.BlockSpec(memory_space=pltpu.VMEM)
+    any_spec = pl.BlockSpec(memory_space=pl.ANY)
     return pl.pallas_call(
-        out_kernel,
-        name='out_project',
+        attend_kernel,
+        name='attend',
         out_shape=jax.ShapeDtypeStruct((TOKENS, HIDDEN), BF16),
-        in_specs=[vmem] * 3 + [pl.BlockSpec(memory_space=pl.ANY)] * 2,
+        in_specs=[pl.BlockSpec(memory_space=pltpu.SMEM)] + [vmem] * 2 + [any_spec] * 5,
         out_specs=vmem,
         scratch_shapes=[
-            pltpu.VMEM((EXPERTS, TOKENS, QUERY_COLS), BF16),
-            pltpu.VMEM((OUT_RING, EXPERTS, QUERY_COLS, COL), BF16),
-            pltpu.SemaphoreType.DMA((OUT_RING,)),
+            pltpu.VMEM((TOKENS * 8, HEAD_DIM), F32),
+            pltpu.VMEM((A_RING, BLOCK, SLOTS * HEADS, HEAD_DIM), BF16),
+            pltpu.VMEM((A_RING, BLOCK, SLOTS * HEADS, HEAD_DIM), BF16),
+            pltpu.VMEM((2, BLOCK, 8, HEAD_DIM), F32),
+            pltpu.VMEM((BLOCK * 8, HEAD_DIM), F32),
+            pltpu.VMEM((ROWS, 2 * QUERY_COLS), BF16),
+            pltpu.VMEM((EXPERTS, ROWS, QUERY_COLS), BF16),
+            pltpu.VMEM((EXPERTS, QUERY_COLS, HIDDEN), BF16),
+            pltpu.SemaphoreType.DMA,
+            pltpu.SemaphoreType.DMA((A_RING,)),
+            pltpu.SemaphoreType.DMA((A_RING,)),
+            pltpu.SemaphoreType.DMA((EXPERTS,)),
         ] + CHUNK_SCRATCH,
         compiler_params=pltpu.CompilerParams(vmem_limit_bytes=VMEM_LIMIT, collective_id=0, has_side_effects=True),
-    )(o, ids, gates, x, w_out)
+    )(positions, ids, gates, q, k_cache, v_cache, w_out, x)
 
 
 def gate_up_kernel(x_ref, gain_ref, router_ref, idst_ref, wg_hbm, wu_hbm, a_hbm, gates_ref,
@@ -583,22 +604,31 @@
     for copy in a_copies:
         copy.wait()
 
-    def load_step(s, column):
-        @pl.when(s + DOWN_RING < STEPS)
-        def _():
-            for copy in copies(s + DOWN_RING, column(s + DOWN_RING)):
-                copy.start()
-
-    def wait_step(s, col):
-        for copy in copies(s, col):
-            copy.wait()
-
-    def partial(s, rows):
+    def partial(s, rows, col):
         slot = lax.rem(s, DOWN_RING)
         acc = gates_ref[rows, 0:1] * dot(abuf[0, rows, :], wbuf[slot, 0])
         return acc + gates_ref[rows, 1:2] * dot(abuf[1, rows, :], wbuf[slot, 1])
 
-    reduce_columns(load_step, wait_step, partial, x_ref, out_ref, *chunk_refs)
+    def drive(chunk_step, column):
+        def col_body(i, carry):
+            for parity in range(2):
+                s = 2 * i + parity
+                for copy in copies(s, column(s)):
+                    copy.wait()
+
+                def row_body(m, c):
+                    chunk_step(i, parity, m)
+                    return c
+                lax.fori_loop(0, TOKENS // ROWS, row_body, 0)
+
+                @pl.when(s + DOWN_RING < STEPS)
+                def _():
+                    for copy in copies(s + DOWN_RING, column(s + DOWN_RING)):
+                        copy.start()
+            return carry
+        lax.fori_loop(0, STEPS // 2, col_body, 0)
+
+    reduce_columns(drive, partial, x_ref, out_ref, *chunk_refs)
 
 
 def down_project(gates, x_mid, act, w_down):
@@ -642,10 +672,10 @@
     def local_step(x, k_cache, v_cache, positions, att_ids, mlp_ids, norm_att, w_kv, router_att, w_query, w_out, norm_mlp, router_mlp, w_gate, w_up, w_down):
         flat = (TOKENS, SLOTS * HEADS, HEAD_DIM)
         kv_rows = w_kv.reshape(HIDDEN, HEADS, 2, HEAD_DIM).transpose(0, 2, 1, 3).reshape(HIDDEN * 8, HEAD_DIM)
-        k_new, v_new, o, att_gates, att_cols = attend(
+        k_new, v_new, q, att_gates, att_cols = project(
             positions, x, norm_att.reshape(1, HIDDEN), jnp.asarray(table), positions.reshape(1, TOKENS), att_ids.T, router_att.T,
             kv_rows, w_query, k_cache.reshape(flat), v_cache.reshape(flat))
-        x_mid = out_project(o, att_cols, att_gates, x, w_out)
+        x_mid = attend(positions, att_cols, att_gates, q, k_new, v_new, w_out, x)
         act, mlp_gates = gate_up(x_mid, norm_mlp.reshape(1, HIDDEN), router_mlp.T, mlp_ids.T, w_gate, w_up)
         x_out = down_project(mlp_gates, x_mid, act, w_down)
         return x_out, k_new.reshape(k_cache.shape), v_new.reshape(v_cache.shape)

time: 185 us -> 188 us (1.016)
    pallas_call x2, Pallas kernels: 93.5 us -> 97.2 us  [the longest x1 63.5 us: attend(): pl.pallas_call(attend_kernel, name='attend', out_shape=jax.ShapeDtypeStru...]
    pallas_call x1, Pallas kernels: 51.8 us -> 49.3 us  [down_project(): pl.pallas_call(down_kernel, name='down_project', out_shape=jax.ShapeDtype...]
where the time goes in v3:
time: 188 us; the launch traced here: 187 us
  Pallas kernels  183 us (97%)
  local copies, waits for them, and re-layouts  3.16 us (2%)
    pallas_call x1, Pallas kernels, attend(): pl.pallas_call(attend_kernel, name='attend', out_shape=jax.ShapeDtypeStru...  63.5 us
    pallas_call x1, Pallas kernels, down_project(): pl.pallas_call(down_kernel, name='down_project', out_shape=jax.ShapeDtype...  49.3 us
    pallas_call x1, Pallas kernels, gate_up(): pl.pallas_call(gate_up_kernel, name='gate_up', out_shape=(jax.ShapeDtypeS...  36.3 us
    pallas_call x1, Pallas kernels, project(): pl.pallas_call(project_kernel, name='project', out_shape=(cache, cache, j...  33.7 us

profile of v3, /device:TPU:0, one launch (start us, length us, event | category | flops | bytes accessed | tf_op | source)
XLA Modules:
  0.0 186.6 jit_solution(6201820443442369013)
XLA Ops:
  0.6 33.7 %project.1 = (bf16[512,128,128]{2,1,0:T(8,128)(2,1)}, bf16[512,128,128]{2,1,0:T(8,128)(2,1)}, f32[4096,128]{1,0:T(8,128)}, f32[512,8]{1,0:T(8,128)}, s32[512,8]{1,0:T(8,128)}) custom-call(s32[512]{0:T(512)} %pos_ref.3, bf16[512,2048]{1,0:T(8,128)(2,1)} %x_hbm.1, f32[1,2048]{1,0:T(1,128)} %bitcast.24, bf16[128,256]{1,0:T(8,128)(2,1)} %constant.2.clone.table_ref, ...), custom_call_target="tpu_custom_call" | custom-call | tf_op jit(solution)/shard_map/project/pallas_call | solution.py:222
  34.4 63.5 %attend.1.x_ref = bf16[512,2048]{1,0:T(8,128)(2,1)} custom-call(s32[512]{0:T(512)} %pos_ref.3, s32[512,8]{1,0:T(8,128)} %get-tuple-element.10.ids_ref, f32[512,8]{1,0:T(8,128)} %get-tuple-element.11.gates_ref, f32[4096,128]{1,0:T(8,128)} %get-tuple-element.12.q_hbm, bf16[512,128,128]{2,1,0:T(8,128)(2,1)} %get-tuple-element.13.kc_hbm, ...), custom_call_target="tpu_custom_call" | custom-call | tf_op jit(solution)/shard_map/attend/pallas_call | solution.py:443
  97.9 36.3 %gate_up.1 = (bf16[2,512,5632]{2,1,0:T(8,128)(2,1)}, f32[512,8]{1,0:T(8,128)}) custom-call(bf16[512,2048]{1,0:T(8,128)(2,1)} %attend.1.x_ref, f32[1,2048]{1,0:T(1,128)} %bitcast.25, bf16[8,2048]{1,0:T(8,128)(2,1)} %bitcast.22, s32[2,512]{1,0:T(2,128)} %bitcast.27, bf16[2,2048,5632]{2,1,0:T(8,128)(2,1)} %wg_hbm.1, bf16[2,2048,5632]{2,1,0:T(8,128)(2,1)} %wu_hbm.1), custom_call_target="tpu_custom_call" | custom-call | tf_op jit(solution)/shard_map/gate_up/pallas_call | solution.py:563
  134.2 49.3 %down_project.1 = bf16[512,2048]{1,0:T(8,128)(2,1)} custom-call(f32[512,8]{1,0:T(8,128)} %get-tuple-element.15.gates_ref, bf16[512,2048]{1,0:T(8,128)(2,1)} %attend.1.x_ref, bf16[2,512,5632]{2,1,0:T(8,128)(2,1)} %get-tuple-element.16.a_hbm, bf16[2,5632,2048]{2,1,0:T(8,128)(2,1)} %w_hbm.3), custom_call_target="tpu_custom_call" | custom-call | tf_op jit(solution)/shard_map/down_project/pallas_call | solution.py:637
  183.5 3.2 %copy.22 = bf16[512,2048]{1,0:T(8,128)(2,1)} copy(bf16[512,2048]{1,0:T(8,128)(2,1)} %down_project.1) | data formatting | bytes 4194304

commit v4 on v3

--- a/solution.py
+++ b/solution.py
@@ -86,8 +86,8 @@
 
 
 def project_kernel(pos_ref, x_ref, gain_ref, table_ref, posrow_ref, idst_ref, router_ref, wkv_hbm, wq_hbm, kc_hbm, vc_hbm,
-                   ko_hbm, vo_hbm, qrow, gates_ref, ids_ref,
-                   hid, wraw, wtmp, wkv, wq, kbuf, vbuf, qsel, knv, cos_s, sin_s,
+                   ko_hbm, vo_hbm, q_ref, gates_ref, ids_ref,
+                   hid, wraw, wtmp, wkv, wq, kbuf, vbuf, qsel, qrow, knv, cos_s, sin_s,
                    wkv_sem, wq_sem, kin_sem, vin_sem, kout_sem, vout_sem):
     def block_of(ref, b):
         return ref.at[pl.ds(pl.multiple_of(b * BLOCK, BLOCK), BLOCK)]
@@ -206,7 +206,12 @@
         for k in range(2):
             for h in range(HEADS):
                 q = qsel[k, rows, h * 128:(h + 1) * 128]
-                qrow[pl.ds(m * 1024 + k * HEADS + h, 128, stride=8), :] = q * cos + pltpu.roll(q, 64, 1) * sin
+                qrow[pl.ds(k * HEADS + h, 128, stride=8), :] = q * cos + pltpu.roll(q, 64, 1) * sin
+        q = qrow[...]
+        even = (iota((1024, HEAD_DIM), 0) & 8) == 0
+        lines = pl.ds(pl.multiple_of(m * 1024, 1024), 1024)
+        q_ref[lines, :HEAD_DIM] = jnp.where(even, q, 0.0).astype(BF16)
+        q_ref[lines, HEAD_DIM:] = jnp.where(even, 0.0, q).astype(BF16)
         return carry
     lax.fori_loop(0, TOKENS // 128, rope_body, 0)
     for b in (BLOCKS - 2, BLOCKS - 1):
@@ -222,7 +227,7 @@
     return pl.pallas_call(
         project_kernel,
         name='project',
-        out_shape=(cache, cache, jax.ShapeDtypeStruct((TOKENS * 8, HEAD_DIM), F32),
+        out_shape=(cache, cache, jax.ShapeDtypeStruct((TOKENS * 8, 2 * HEAD_DIM), BF16),
                    jax.ShapeDtypeStruct((TOKENS, EXPERTS), F32), jax.ShapeDtypeStruct((TOKENS, EXPERTS), jnp.int32)),
         in_specs=[smem] + [vmem] * 6 + [any_spec] * 4,
         out_specs=(any_spec, any_spec, vmem, vmem, vmem),
@@ -235,6 +240,7 @@
             pltpu.VMEM((RING, BLOCK, SLOTS * HEADS, HEAD_DIM), BF16),
             pltpu.VMEM((RING, BLOCK, SLOTS * HEADS, HEAD_DIM), BF16),
             pltpu.VMEM((2, TOKENS, QUERY_COLS), F32),
+            pltpu.VMEM((1024, HEAD_DIM), F32),
             pltpu.VMEM((TOKENS * 8, HEAD_DIM), F32),
             pltpu.VMEM((TOKENS, HEAD_DIM), F32),
             pltpu.VMEM((TOKENS, HEAD_DIM), F32),
@@ -250,12 +256,13 @@
 
 
 def reduce_columns(drive, partial, base_hbm, out_ref, base_ref, base_sem, send1, recv1, own, recv2, fin, recv3, s1, r1, s2, r2, s3, r3):
+    chunks, height, width = send1.shape
+    per = TOKENS // height
+    half_width = HIDDEN // 2
     me = lax.axis_index('tp')
     core = lax.rem(me, 2)
     sibling = me + 1 - 2 * core
     partner = lax.rem(me + 2, 4)
-    base_copy = pltpu.make_async_copy(base_hbm, base_ref, base_sem)
-    base_copy.start()
     barrier = pltpu.get_barrier_semaphore()
     for peer in (sibling, partner):
         pl.semaphore_signal(barrier, inc=1, device_id={'tp': peer}, device_id_type=MESH)
@@ -263,7 +270,7 @@
 
     def column(s):
         half = lax.rem(core + 1 + s, 2)
-        return pl.multiple_of((half * (STEPS // 2) + lax.div(s, 2)) * COL, COL)
+        return pl.multiple_of(half * half_width + lax.div(s, 2) * width, width)
 
     def remote(src, dst, c, send, recv, peer):
         return pltpu.make_async_remote_copy(src_ref=src.at[c], dst_ref=dst.at[c], send_sem=send.at[c], recv_sem=recv.at[c],
@@ -280,8 +287,8 @@
 
     def chunk_step(i, parity, m):
         s = 2 * i + parity
-        rows = pl.ds(pl.multiple_of(m * ROWS, ROWS), ROWS)
-        chunk = 2 * i + m
+        rows = pl.ds(pl.multiple_of(m * height, height), height)
+        chunk = per * i + m
         acc = partial(s, rows, column(s))
         if parity == 0:
             send1[chunk] = acc.astype(BF16)
@@ -291,115 +298,130 @@
             own[chunk] = (acc + recv1[chunk].astype(F32)).astype(BF16)
             to_partner(chunk).start()
 
-    drive(chunk_step, column)
-    base_copy.wait()
-
     def place(c, half):
-        rows = pl.ds(pl.multiple_of(lax.rem(c, 2) * ROWS, ROWS), ROWS)
-        cols = pl.ds(pl.multiple_of((half * (STEPS // 2) + lax.div(c, 2)) * COL, COL), COL)
+        rows = pl.ds(pl.multiple_of(lax.rem(c, per) * height, height), height)
+        cols = pl.ds(pl.multiple_of(half * half_width + lax.div(c, per) * width, width), width)
         return rows, cols
 
-    def final_body(c, carry):
+    def finish(c):
         to_partner(c).wait_recv()
         rows, cols = place(c, core)
         total = own[c].astype(F32) + recv2[c].astype(F32)
         value = (base_ref[rows, cols].astype(F32) + total).astype(BF16)
         fin[c] = value
+        share(c).start()
         out_ref[rows, cols] = value
-        share(c).start()
-        return carry
-    lax.fori_loop(0, CHUNKS, final_body, 0)
+
+    base_copy = pltpu.make_async_copy(base_hbm, base_ref, base_sem)
+    finished = drive(chunk_step, column, finish, base_copy)
+
+    def final_body(c, carry):
+        finish(c)
+        return carry
+    lax.fori_loop(finished, chunks, final_body, 0)
 
     def gather_body(c, carry):
         share(c).wait_recv()
         rows, cols = place(c, 1 - core)
         out_ref[rows, cols] = recv3[c]
         return carry
-    lax.fori_loop(0, CHUNKS, gather_body, 0)
+    lax.fori_loop(0, chunks, gather_body, 0)
 
     def drain_body(c, carry):
         to_sibling(c).wait_send()
         to_partner(c).wait_send()
         share(c).wait_send()
         return carry
-    lax.fori_loop(0, CHUNKS, drain_body, 0)
-
-
-CHUNK_SCRATCH = [pltpu.VMEM((TOKENS, HIDDEN), BF16), pltpu.SemaphoreType.DMA] + [pltpu.VMEM((CHUNKS, ROWS, COL), BF16)] * 6 + [pltpu.SemaphoreType.DMA((CHUNKS,))] * 6
-A_RING = 8
-HALF_BLOCKS = ROWS // BLOCK
+    lax.fori_loop(0, chunks, drain_body, 0)
+
+
+def chunk_scratch(height, width):
+    chunks = TOKENS * HIDDEN // 2 // (height * width)
+    return ([pltpu.VMEM((TOKENS, HIDDEN), BF16), pltpu.SemaphoreType.DMA]
+            + [pltpu.VMEM((chunks, height, width), BF16)] * 6 + [pltpu.SemaphoreType.DMA((chunks,))] * 6)
+
+
+A_RING = 6
+A_AHEAD = 4
+A_ROWS = 128
+PARTS = TOKENS // A_ROWS
+PART_BLOCKS = A_ROWS // BLOCK
 
 
 def attend_kernel(pos_ref, ids_ref, gates_ref, q_hbm, kc_hbm, vc_hbm, w_hbm, x_hbm, out_ref,
-                  qrow, kbuf, vbuf, probs, orow, mixed, spread, wbuf, q_sem, k_sem, v_sem, w_sem, *chunk_refs):
+                  qbuf, kbuf, vbuf, probs, orow, mixed, spread, wbuf, q_sem, k_sem, v_sem, w_sem, *chunk_refs):
     def load(b):
         slot = lax.rem(b, A_RING)
         rows = pl.ds(pl.multiple_of(b * BLOCK, BLOCK), BLOCK)
         return (pltpu.make_async_copy(kc_hbm.at[rows], kbuf.at[slot], k_sem.at[slot]),
                 pltpu.make_async_copy(vc_hbm.at[rows], vbuf.at[slot], v_sem.at[slot]))
 
-    q_copy = pltpu.make_async_copy(q_hbm, qrow, q_sem)
+    q_copy = pltpu.make_async_copy(q_hbm, qbuf, q_sem)
     q_copy.start()
-    for b in range(A_RING):
+    for b in range(A_AHEAD):
         for copy in load(jnp.int32(b)):
             copy.start()
     w_copies = [pltpu.make_async_copy(w_hbm.at[e], wbuf.at[e], w_sem.at[e]) for e in range(EXPERTS)]
-    for copy in w_copies:
-        copy.start()
 
     scale = HEAD_DIM ** -0.5
-    row8 = iota((8, 128), 0)
-    lane = iota((8, 128), 1)
-    same_head = (lane & 3) == (row8 & 3)
+    row16 = iota((16, 128), 0)
+    lane = iota((16, 128), 1)
+    upper = row16 < 8
+    same_head = (lane & 3) == (row16 & 3)
     slot_of = lane >> 2
 
     def attend_rows(m):
         def block_body(i, carry):
-            b = m * HALF_BLOCKS + jnp.minimum(i, HALF_BLOCKS - 1)
+            b = m * PART_BLOCKS + jnp.minimum(i, PART_BLOCKS - 1)
             before = jnp.maximum(i - 1, 0)
-            prev = m * HALF_BLOCKS + before
+            prev = m * PART_BLOCKS + before
             slot = lax.rem(b, A_RING)
             prev_slot = lax.rem(prev, A_RING)
             side = lax.rem(i, 2)
 
-            @pl.when(i < HALF_BLOCKS)
+            @pl.when(i < PART_BLOCKS)
             def _():
                 for copy in load(b):
                     copy.wait()
 
-            def score(t):
-                q = qrow[pl.ds(pl.multiple_of((b * BLOCK + t) * 8, 8), 8), :].astype(BF16)
-                s = dot_nt(q, kbuf[slot, t]) * scale
-                s = jnp.where(same_head & (slot_of <= pos_ref[b * BLOCK + t]), s, NEG)
+            def score(j):
+                t = b * BLOCK + 2 * j
+                q = qbuf[pl.ds(pl.multiple_of(t * 8, 16), 16), :]
+                keys = jnp.concatenate([kbuf[slot, 2 * j], kbuf[slot, 2 * j + 1]], axis=1)
+                s = dot_nt(q, keys) * scale
+                s = jnp.where(same_head & (slot_of <= jnp.where(upper, pos_ref[t], pos_ref[t + 1])), s, NEG)
                 e = jnp.exp(s - jnp.max(s, axis=1, keepdims=True))
-                probs[side, t] = e / jnp.sum(e, axis=1, keepdims=True)
-
-            def mix(t):
-                orow[t * 8:(t + 1) * 8, :] = dot(probs[1 - side, t].astype(BF16), vbuf[prev_slot, t])
-
-            half = BLOCK // 2
-            for t in range(half):
-                score(t)
-            for t in range(half):
-                mix(t)
-            for t in range(half, BLOCK):
-                score(t)
-            for t in range(half, BLOCK):
-                mix(t)
+                probs[side, j] = (e / jnp.sum(e, axis=1, keepdims=True)).astype(BF16)
+
+            def mix(j):
+                values = jnp.concatenate([vbuf[prev_slot, 2 * j], vbuf[prev_slot, 2 * j + 1]], axis=1)
+                o = dot(probs[1 - side, j], values)
+                orow[j * 16:j * 16 + 8, :] = o[:8, :HEAD_DIM]
+                orow[j * 16 + 8:j * 16 + 16, :] = o[8:, HEAD_DIM:]
+
+            pairs = BLOCK // 2
+            for j in range(pairs // 2):
+                score(j)
+            for j in range(pairs // 2):
+                mix(j)
+            for j in range(pairs // 2, pairs):
+                score(j)
+            for j in range(pairs // 2, pairs):
+                mix(j)
             rows = pl.ds(pl.multiple_of(before * BLOCK, BLOCK), BLOCK)
             for r in range(8):
                 mixed[rows, r * 128:(r + 1) * 128] = orow[pl.ds(r, BLOCK, stride=8), :].astype(BF16)
 
-            @pl.when((i >= 1) & (prev + A_RING < BLOCKS))
+            @pl.when((i < PART_BLOCKS) & (b + A_AHEAD < BLOCKS))
             def _():
-                for copy in load(prev + A_RING):
+                for copy in load(b + A_AHEAD):
                     copy.start()
             return carry
-        lax.fori_loop(0, HALF_BLOCKS + 1, block_body, 0)
+        lax.fori_loop(0, PART_BLOCKS + 1, block_body, 0)
 
         def spread_body(n, carry):
             rows = pl.ds(pl.multiple_of(n * 64, 64), 64)
-            from_rows = pl.ds(pl.multiple_of(m * ROWS + n * 64, 64), 64)
+            from_rows = pl.ds(pl.multiple_of(m * A_ROWS + n * 64, 64), 64)
             first = mixed[rows, :QUERY_COLS].astype(F32)
             second = mixed[rows, QUERY_COLS:].astype(F32)
             for e in range(EXPERTS):
@@ -407,32 +429,40 @@
                 picked = jnp.where(ids_ref[from_rows, 1:2] == e, second, picked)
                 spread[e, rows, :] = picked.astype(BF16)
             return carry
-        lax.fori_loop(0, ROWS // 64, spread_body, 0)
+        lax.fori_loop(0, A_ROWS // 64, spread_body, 0)
 
     def partial(s, rows, col):
-        acc = jnp.zeros((ROWS, COL), F32)
+        acc = jnp.zeros((A_ROWS, HIDDEN // 2), F32)
         for e in range(EXPERTS):
-            acc = acc + gates_ref[rows, e:e + 1] * dot(spread[e], wbuf[e, :, pl.ds(col, COL)])
+            acc = acc + gates_ref[rows, e:e + 1] * dot(spread[e], wbuf[e, :, pl.ds(col, HIDDEN // 2)])
         return acc
 
-    def drive(chunk_step, column):
+    def drive(chunk_step, column, finish, base_copy):
         q_copy.wait()
-
-        def half_body(m, carry):
+        for copy in w_copies:
+            copy.start()
+
+        def part_body(m, carry):
             attend_rows(m)
 
             @pl.when(m == 0)
             def _():
+                base_copy.start()
                 for copy in w_copies:
                     copy.wait()
-
-            def col_body(i, c):
-                for parity in range(2):
-                    chunk_step(i, parity, m)
-                return c
-            lax.fori_loop(0, STEPS // 2, col_body, 0)
+            for parity in range(2):
+                chunk_step(0, parity, m)
+
+            @pl.when(m == 1)
+            def _():
+                base_copy.wait()
+
+            @pl.when(m >= 2)
+            def _():
+                finish(m - 2)
             return carry
-        lax.fori_loop(0, TOKENS // ROWS, half_body, 0)
+        lax.fori_loop(0, PARTS, part_body, 0)
+        return PARTS - 2
 
     reduce_columns(drive, partial, x_hbm, out_ref, *chunk_refs)
 
@@ -447,19 +477,19 @@
         in_specs=[pl.BlockSpec(memory_space=pltpu.SMEM)] + [vmem] * 2 + [any_spec] * 5,
         out_specs=vmem,
         scratch_shapes=[
-            pltpu.VMEM((TOKENS * 8, HEAD_DIM), F32),
+            pltpu.VMEM((TOKENS * 8, 2 * HEAD_DIM), BF16),
             pltpu.VMEM((A_RING, BLOCK, SLOTS * HEADS, HEAD_DIM), BF16),
             pltpu.VMEM((A_RING, BLOCK, SLOTS * HEADS, HEAD_DIM), BF16),
-            pltpu.VMEM((2, BLOCK, 8, HEAD_DIM), F32),
+            pltpu.VMEM((2, BLOCK // 2, 16, HEAD_DIM), BF16),
             pltpu.VMEM((BLOCK * 8, HEAD_DIM), F32),
-            pltpu.VMEM((ROWS, 2 * QUERY_COLS), BF16),
-            pltpu.VMEM((EXPERTS, ROWS, QUERY_COLS), BF16),
+            pltpu.VMEM((A_ROWS, 2 * QUERY_COLS), BF16),
+            pltpu.VMEM((EXPERTS, A_ROWS, QUERY_COLS), BF16),
             pltpu.VMEM((EXPERTS, QUERY_COLS, HIDDEN), BF16),
             pltpu.SemaphoreType.DMA,
             pltpu.SemaphoreType.DMA((A_RING,)),
             pltpu.SemaphoreType.DMA((A_RING,)),
             pltpu.SemaphoreType.DMA((EXPERTS,)),
-        ] + CHUNK_SCRATCH,
+        ] + chunk_scratch(A_ROWS, HIDDEN // 2),
         compiler_params=pltpu.CompilerParams(vmem_limit_bytes=VMEM_LIMIT, collective_id=0, has_side_effects=True),
     )(positions, ids, gates, q, k_cache, v_cache, w_out, x)
 
@@ -586,35 +616,45 @@
 DOWN_RING = 2
 
 
-def down_kernel(gates_ref, x_ref, a_hbm, w_hbm, out_ref, abuf, wbuf, a_sem, w_sem, *chunk_refs):
+def down_kernel(gates_ref, x_hbm, a_hbm, w_hbm, out_ref, abuf, wbuf, first_part, a_sem, w_sem, *chunk_refs):
     me = lax.axis_index('tp')
     core = lax.rem(me, 2)
 
-    def copies(s, col):
+    def copy_of(s, col, e):
         slot = lax.rem(s, DOWN_RING)
-        return [pltpu.make_async_copy(w_hbm.at[e, :, pl.ds(col, COL)], wbuf.at[slot, e], w_sem.at[slot, e]) for e in range(LOCAL)]
+        return pltpu.make_async_copy(w_hbm.at[e, :, pl.ds(col, COL)], wbuf.at[slot, e], w_sem.at[slot, e])
+
+    def early(s, e):
+        half = lax.rem(core + 1 + s, 2)
+        return copy_of(jnp.int32(s), pl.multiple_of((half * (STEPS // 2) + s // 2) * COL, COL), e)
 
     a_copies = [pltpu.make_async_copy(a_hbm.at[e], abuf.at[e], a_sem.at[e]) for e in range(LOCAL)]
-    for copy in a_copies:
-        copy.start()
-    for s in range(DOWN_RING):
-        half = lax.rem(core + 1 + s, 2)
-        for copy in copies(jnp.int32(s), pl.multiple_of((half * (STEPS // 2) + s // 2) * COL, COL)):
-            copy.start()
-    for copy in a_copies:
-        copy.wait()
+    for e in range(LOCAL):
+        a_copies[e].start()
+        early(0, e).start()
 
     def partial(s, rows, col):
-        slot = lax.rem(s, DOWN_RING)
-        acc = gates_ref[rows, 0:1] * dot(abuf[0, rows, :], wbuf[slot, 0])
-        return acc + gates_ref[rows, 1:2] * dot(abuf[1, rows, :], wbuf[slot, 1])
-
-    def drive(chunk_step, column):
+        return first_part[rows, :] + gates_ref[rows, 1:2] * dot(abuf[1, rows, :], wbuf[lax.rem(s, DOWN_RING), 1])
+
+    def drive(chunk_step, column, finish, base_copy):
         def col_body(i, carry):
             for parity in range(2):
                 s = 2 * i + parity
-                for copy in copies(s, column(s)):
-                    copy.wait()
+                slot = lax.rem(s, DOWN_RING)
+                copy_of(s, column(s), 0).wait()
+                if parity == 0:
+                    @pl.when(i == 0)
+                    def _():
+                        a_copies[0].wait()
+                        for e in range(LOCAL):
+                            early(1, e).start()
+                        base_copy.start()
+                first_part[...] = gates_ref[:, 0:1] * dot(abuf[0], wbuf[slot, 0])
+                if parity == 0:
+                    @pl.when(i == 0)
+                    def _():
+                        a_copies[1].wait()
+                copy_of(s, column(s), 1).wait()
 
                 def row_body(m, c):
                     chunk_step(i, parity, m)
@@ -623,12 +663,22 @@
 
                 @pl.when(s + DOWN_RING < STEPS)
                 def _():
-                    for copy in copies(s + DOWN_RING, column(s + DOWN_RING)):
-                        copy.start()
+                    for e in range(LOCAL):
+                        copy_of(s + DOWN_RING, column(s + DOWN_RING), e).start()
+
+            @pl.when(i == 1)
+            def _():
+                base_copy.wait()
+
+            @pl.when(i >= 2)
+            def _():
+                finish(2 * (i - 2))
+                finish(2 * (i - 2) + 1)
             return carry
         lax.fori_loop(0, STEPS // 2, col_body, 0)
-
-    reduce_columns(drive, partial, x_ref, out_ref, *chunk_refs)
+        return CHUNKS // 2
+
+    reduce_columns(drive, partial, x_hbm, out_ref, *chunk_refs)
 
 
 def down_project(gates, x_mid, act, w_down):
@@ -643,9 +693,10 @@
         scratch_shapes=[
             pltpu.VMEM((LOCAL, TOKENS, FFN), BF16),
             pltpu.VMEM((DOWN_RING, LOCAL, FFN, COL), BF16),
+            pltpu.VMEM((TOKENS, COL), F32),
             pltpu.SemaphoreType.DMA((LOCAL,)),
             pltpu.SemaphoreType.DMA((DOWN_RING, LOCAL)),
-        ] + CHUNK_SCRATCH,
+        ] + chunk_scratch(ROWS, COL),
         compiler_params=pltpu.CompilerParams(vmem_limit_bytes=VMEM_LIMIT, collective_id=1, has_side_effects=True),
     )(gates, x_mid, act, w_down)
 

time: 188 us -> 174 us (0.926)
  Pallas kernels: 183 us -> 170 us
    pallas_call x1, Pallas kernels: 63.5 us -> 50.3 us  [attend(): pl.pallas_call(attend_kernel, name='attend', out_shape=jax.ShapeDtypeStru...]
where the time goes in v4:
time: 174 us; the launch traced here: 173 us
  Pallas kernels  170 us (98%)
  local copies, waits for them, and re-layouts  3.16 us (2%)
    pallas_call x1, Pallas kernels, attend(): pl.pallas_call(attend_kernel, name='attend', out_shape=jax.ShapeDtypeStru...  50.3 us
    pallas_call x1, Pallas kernels, down_project(): pl.pallas_call(down_kernel, name='down_project', out_shape=jax.ShapeDtype...  49 us
    pallas_call x1, Pallas kernels, gate_up(): pl.pallas_call(gate_up_kernel, name='gate_up', out_shape=(jax.ShapeDtypeS...  36.3 us
    pallas_call x1, Pallas kernels, project(): pl.pallas_call(project_kernel, name='project', out_shape=(cache, cache, j...  34 us

profile of v4, /device:TPU:0, one launch (start us, length us, event | category | flops | bytes accessed | tf_op | source)
XLA Modules:
  0.0 173.5 jit_solution(17021677436648642811)
XLA Ops:
  0.6 34.0 %project.1 = (bf16[512,128,128]{2,1,0:T(8,128)(2,1)}, bf16[512,128,128]{2,1,0:T(8,128)(2,1)}, bf16[4096,256]{1,0:T(8,128)(2,1)}, f32[512,8]{1,0:T(8,128)}, s32[512,8]{1,0:T(8,128)}) custom-call(s32[512]{0:T(512)} %pos_ref.3, bf16[512,2048]{1,0:T(8,128)(2,1)} %x_hbm.1, f32[1,2048]{1,0:T(1,128)} %bitcast.24, bf16[128,256]{1,0:T(8,128)(2,1)} %constant.2.clone.table_ref, ...), custom_call_target="tpu_custom_call" | custom-call | tf_op jit(solution)/shard_map/project/pallas_call | solution.py:227
  34.6 50.3 %attend.1.x_ref.x_hbm = bf16[512,2048]{1,0:T(8,128)(2,1)} custom-call(s32[512]{0:T(512)} %pos_ref.3, s32[512,8]{1,0:T(8,128)} %get-tuple-element.10.ids_ref, f32[512,8]{1,0:T(8,128)} %get-tuple-element.11.gates_ref, bf16[4096,256]{1,0:T(8,128)(2,1)} %get-tuple-element.12.q_hbm, bf16[512,128,128]{2,1,0:T(8,128)(2,1)} %get-tuple-element.13.kc_hbm, ...), custom_call_target="tpu_custom_call" | custom-call | tf_op jit(solution)/shard_map/attend/pallas_call | solution.py:473
  85.0 36.3 %gate_up.1 = (bf16[2,512,5632]{2,1,0:T(8,128)(2,1)}, f32[512,8]{1,0:T(8,128)}) custom-call(bf16[512,2048]{1,0:T(8,128)(2,1)} %attend.1.x_ref.x_hbm, f32[1,2048]{1,0:T(1,128)} %bitcast.25, bf16[8,2048]{1,0:T(8,128)(2,1)} %bitcast.22, s32[2,512]{1,0:T(2,128)} %bitcast.27, bf16[2,2048,5632]{2,1,0:T(8,128)(2,1)} %wg_hbm.1, bf16[2,2048,5632]{2,1,0:T(8,128)(2,1)} %wu_hbm.1), custom_call_target="tpu_custom_call" | custom-call | tf_op jit(solution)/shard_map/gate_up/pallas_call | solution.py:593
  121.3 49.0 %down_project.1 = bf16[512,2048]{1,0:T(8,128)(2,1)} custom-call(f32[512,8]{1,0:T(8,128)} %get-tuple-element.15.gates_ref, bf16[512,2048]{1,0:T(8,128)(2,1)} %attend.1.x_ref.x_hbm, bf16[2,512,5632]{2,1,0:T(8,128)(2,1)} %get-tuple-element.16.a_hbm, bf16[2,5632,2048]{2,1,0:T(8,128)(2,1)} %w_hbm.3), custom_call_target="tpu_custom_call" | custom-call | tf_op jit(solution)/shard_map/down_project/pallas_call | solution.py:687
  170.3 3.2 %copy.22 = bf16[512,2048]{1,0:T(8,128)(2,1)} copy(bf16[512,2048]{1,0:T(8,128)(2,1)} %down_project.1) | data formatting | bytes 4194304

commit v5 on v4

--- a/solution.py
+++ b/solution.py
@@ -108,10 +108,17 @@
 
     kv_copy = pltpu.make_async_copy(wkv_hbm, wraw, wkv_sem)
     kv_copy.start()
-    for e in range(WQ_RING):
+    for b in range(3):
+        for copy in load(jnp.int32(b)):
+            copy.start()
+    load_wq(jnp.int32(0)).start()
+
+    norm_rows(x_ref, gain_ref, hid)
+    for e in range(1, WQ_RING):
         load_wq(jnp.int32(e)).start()
-
-    norm_rows(x_ref, gain_ref, hid)
+    for b in range(3, RING):
+        for copy in load(jnp.int32(b)):
+            copy.start()
     ids = turn((idst_ref[0:1, :], idst_ref[1:2, :], posrow_ref[...]))
     ids_ref[...] = ids
     id0 = ids[:, 0:1]
@@ -121,9 +128,10 @@
     trig = dot(jnp.where(chosen, 1.0, 0.0).astype(BF16), table_ref[...])
     cos_s[...] = trig[:, :HEAD_DIM]
     sin_s[...] = trig[:, HEAD_DIM:]
-    for b in range(RING):
-        for copy in load(jnp.int32(b)):
-            copy.start()
+    logits = dot_nt(hid[...], router_ref[...])
+    g0, g1 = pair_gates(logits, id0, id1)
+    lane8 = iota((TOKENS, EXPERTS), 1)
+    gates_ref[...] = jnp.where(lane8 == id0, g0, 0.0) + jnp.where(lane8 == id1, g1, 0.0)
     kv_copy.wait()
 
     def sort_body(i, carry):
@@ -193,11 +201,6 @@
                     copy.start()
         return carry
     lax.fori_loop(0, BLOCKS, block_body, 0)
-
-    logits = dot_nt(hid[...], router_ref[...])
-    g0, g1 = pair_gates(logits, id0, id1)
-    lane8 = iota((TOKENS, EXPERTS), 1)
-    gates_ref[...] = jnp.where(lane8 == id0, g0, 0.0) + jnp.where(lane8 == id1, g1, 0.0)
 
     def rope_body(m, carry):
         rows = pl.ds(pl.multiple_of(m * 128, 128), 128)
@@ -494,16 +497,23 @@
     )(positions, ids, gates, q, k_cache, v_cache, w_out, x)
 
 
-def gate_up_kernel(x_ref, gain_ref, router_ref, idst_ref, wg_hbm, wu_hbm, a_hbm, gates_ref,
-                   unorm, picked, scatter, gathered, wg, wu, act, abuf, wg_sem, wu_sem, a_sem):
+def gate_up_kernel(x_ref, gain_ref, router_ref, idst_ref, wg_hbm, wu_hbm, wd_hbm, a_hbm, gates_ref, early_ref,
+                   unorm, picked, scatter, gathered, wg, wu, wd, act, abuf, early_rows, wg_sem, wu_sem, wd_sem, a_sem):
     first_id = lax.axis_index('tp') * LOCAL
+    core = lax.rem(lax.axis_index('tp'), 2)
 
     def load(s):
         e = lax.div(s, F_TILES)
         cols = pl.ds(pl.multiple_of(lax.rem(s, F_TILES) * FT, FT), FT)
         slot = lax.rem(s, W_RING)
         return (pltpu.make_async_copy(wg_hbm.at[e, :, cols], wg.at[slot], wg_sem.at[slot]),
-                pltpu.make_async_copy(wu_hbm.at[e, :, cols], wu.at[slot], wu_sem.at[slot]))
+                pltpu.make_async_copy(wu_hbm.at[e, :, cols], wu.at[slot], wu_sem.at[slot]),
+                down_of(e, cols, slot, 0), down_of(e, cols, slot, 1))
+
+    def down_of(e, rows, slot, j):
+        half = lax.rem(core + 1 + j, 2)
+        cols = pl.ds(pl.multiple_of(half * (HIDDEN // 2), HIDDEN // 2), COL)
+        return pltpu.make_async_copy(wd_hbm.at[e, rows, cols], wd.at[slot, j], wd_sem.at[slot, j])
 
     def save(s):
         e = lax.div(s, F_TILES)
@@ -551,6 +561,8 @@
             return carry
         lax.fori_loop(0, blocks[e], gather_body, 0)
 
+    early_rows[...] = jnp.zeros_like(early_rows)
+
     def step_body(s, carry):
         e = lax.div(s, F_TILES)
         slot = lax.rem(s, W_RING)
@@ -568,13 +580,17 @@
                 gate = dot(gathered[e, :count, :], wg[slot, :, cols])
                 up = dot(gathered[e, :count, :], wu[slot, :, cols])
                 act[:count, cols] = (gate * (1.0 / (1.0 + jnp.exp(-gate))) * up).astype(BF16)
+            for j in range(2):
+                cols = slice(j * COL, (j + 1) * COL)
+                early_rows[e, :count, cols] += dot(act[:count, :], wd[slot, j])
             for m in range(TOKENS // ROWS):
                 rows = slice(m * ROWS, (m + 1) * ROWS)
                 abuf[out_slot, rows, :] = dot(scatter[e, rows, :count], act[:count, :]).astype(BF16)
 
-        n_blocks = jnp.where(e == 0, blocks[0], blocks[1])
-        for k in range(1, TOKENS // RB + 1):
-            pl.when(n_blocks == k)(functools.partial(run, k * RB))
+        n_rows = jnp.where(e == 0, counts[0], counts[1])
+        n_steps = jnp.maximum(lax.div(n_rows + 63, 64), 2)
+        for k in range(2, TOKENS // 64 + 1):
+            pl.when(n_steps == k)(functools.partial(run, k * 64))
 
         @pl.when(s + W_RING < MLP_STEPS)
         def _():
@@ -583,19 +599,34 @@
         save(s).start()
         return carry
     lax.fori_loop(0, MLP_STEPS, step_body, 0)
+
+    def early_body(m, carry):
+        rows = pl.ds(pl.multiple_of(m * ROWS, ROWS), ROWS)
+        for j in range(2):
+            total = jnp.zeros((ROWS, COL), F32)
+            for e in range(LOCAL):
+                z = early_rows[e, :, j * COL:(j + 1) * COL]
+                high = z.astype(BF16)
+                rest = (z - high.astype(F32)).astype(BF16)
+                mine = dot(scatter[e, rows, :], high) + dot(scatter[e, rows, :], rest)
+                total = total + gates_ref[rows, e:e + 1] * mine
+            early_ref[j, rows, :] = total
+        return carry
+    lax.fori_loop(0, TOKENS // ROWS, early_body, 0)
     for s in (MLP_STEPS - 2, MLP_STEPS - 1):
         save(jnp.int32(s)).wait()
 
 
-def gate_up(x_mid, gain, router_t, ids_t, w_gate, w_up):
+def gate_up(x_mid, gain, router_t, ids_t, w_gate, w_up, w_down):
     any_spec = pl.BlockSpec(memory_space=pl.ANY)
     vmem = pl.BlockSpec(memory_space=pltpu.VMEM)
     return pl.pallas_call(
         gate_up_kernel,
         name='gate_up',
-        out_shape=(jax.ShapeDtypeStruct((LOCAL, TOKENS, FFN), BF16), jax.ShapeDtypeStruct((TOKENS, EXPERTS), F32)),
-        in_specs=[vmem] * 4 + [any_spec] * 2,
-        out_specs=(any_spec, vmem),
+        out_shape=(jax.ShapeDtypeStruct((LOCAL, TOKENS, FFN), BF16), jax.ShapeDtypeStruct((TOKENS, EXPERTS), F32),
+                   jax.ShapeDtypeStruct((2, TOKENS, COL), F32)),
+        in_specs=[vmem] * 4 + [any_spec] * 3,
+        out_specs=(any_spec, vmem, vmem),
         scratch_shapes=[
             pltpu.VMEM((TOKENS, HIDDEN), BF16),
             pltpu.VMEM((LOCAL, TOKENS, TOKENS), BF16),
@@ -603,20 +634,23 @@
             pltpu.VMEM((LOCAL, TOKENS, HIDDEN), BF16),
             pltpu.VMEM((W_RING, HIDDEN, FT), BF16),
             pltpu.VMEM((W_RING, HIDDEN, FT), BF16),
+            pltpu.VMEM((W_RING, 2, FT, COL), BF16),
             pltpu.VMEM((TOKENS, FT), BF16),
             pltpu.VMEM((2, TOKENS, FT), BF16),
+            pltpu.VMEM((LOCAL, TOKENS, 2 * COL), F32),
             pltpu.SemaphoreType.DMA((W_RING,)),
             pltpu.SemaphoreType.DMA((W_RING,)),
+            pltpu.SemaphoreType.DMA((W_RING, 2)),
             pltpu.SemaphoreType.DMA((2,)),
         ],
         compiler_params=pltpu.CompilerParams(vmem_limit_bytes=VMEM_LIMIT),
-    )(x_mid, gain, router_t, ids_t, w_gate, w_up)
+    )(x_mid, gain, router_t, ids_t, w_gate, w_up, w_down)
 
 
 DOWN_RING = 2
 
 
-def down_kernel(gates_ref, x_hbm, a_hbm, w_hbm, out_ref, abuf, wbuf, first_part, a_sem, w_sem, *chunk_refs):
+def down_kernel(gates_ref, early_ref, x_hbm, a_hbm, w_hbm, out_ref, abuf, wbuf, first_part, a_sem, w_sem, *chunk_refs):
     me = lax.axis_index('tp')
     core = lax.rem(me, 2)
 
@@ -624,34 +658,37 @@
         slot = lax.rem(s, DOWN_RING)
         return pltpu.make_async_copy(w_hbm.at[e, :, pl.ds(col, COL)], wbuf.at[slot, e], w_sem.at[slot, e])
 
-    def early(s, e):
+    def ahead(s, e):
         half = lax.rem(core + 1 + s, 2)
         return copy_of(jnp.int32(s), pl.multiple_of((half * (STEPS // 2) + s // 2) * COL, COL), e)
 
     a_copies = [pltpu.make_async_copy(a_hbm.at[e], abuf.at[e], a_sem.at[e]) for e in range(LOCAL)]
     for e in range(LOCAL):
         a_copies[e].start()
-        early(0, e).start()
+        ahead(2, e).start()
 
     def partial(s, rows, col):
+        if isinstance(s, int):
+            return early_ref[s, rows, :]
         return first_part[rows, :] + gates_ref[rows, 1:2] * dot(abuf[1, rows, :], wbuf[lax.rem(s, DOWN_RING), 1])
 
     def drive(chunk_step, column, finish, base_copy):
+        for m in range(TOKENS // ROWS):
+            for parity in range(2):
+                chunk_step(0, parity, m)
+        a_copies[0].wait()
+        for e in range(LOCAL):
+            ahead(3, e).start()
+        base_copy.start()
+
         def col_body(i, carry):
             for parity in range(2):
                 s = 2 * i + parity
                 slot = lax.rem(s, DOWN_RING)
                 copy_of(s, column(s), 0).wait()
-                if parity == 0:
-                    @pl.when(i == 0)
-                    def _():
-                        a_copies[0].wait()
-                        for e in range(LOCAL):
-                            early(1, e).start()
-                        base_copy.start()
                 first_part[...] = gates_ref[:, 0:1] * dot(abuf[0], wbuf[slot, 0])
                 if parity == 0:
-                    @pl.when(i == 0)
+                    @pl.when(i == 1)
                     def _():
                         a_copies[1].wait()
                 copy_of(s, column(s), 1).wait()
@@ -675,20 +712,20 @@
                 finish(2 * (i - 2))
                 finish(2 * (i - 2) + 1)
             return carry
-        lax.fori_loop(0, STEPS // 2, col_body, 0)
+        lax.fori_loop(1, STEPS // 2, col_body, 0)
         return CHUNKS // 2
 
     reduce_columns(drive, partial, x_hbm, out_ref, *chunk_refs)
 
 
-def down_project(gates, x_mid, act, w_down):
+def down_project(gates, early, x_mid, act, w_down):
     vmem = pl.BlockSpec(memory_space=pltpu.VMEM)
     any_spec = pl.BlockSpec(memory_space=pl.ANY)
     return pl.pallas_call(
         down_kernel,
         name='down_project',
         out_shape=jax.ShapeDtypeStruct((TOKENS, HIDDEN), BF16),
-        in_specs=[vmem] + [any_spec] * 3,
+        in_specs=[vmem] * 2 + [any_spec] * 3,
         out_specs=vmem,
         scratch_shapes=[
             pltpu.VMEM((LOCAL, TOKENS, FFN), BF16),
@@ -698,7 +735,37 @@
             pltpu.SemaphoreType.DMA((DOWN_RING, LOCAL)),
         ] + chunk_scratch(ROWS, COL),
         compiler_params=pltpu.CompilerParams(vmem_limit_bytes=VMEM_LIMIT, collective_id=1, has_side_effects=True),
-    )(gates, x_mid, act, w_down)
+    )(gates, early, x_mid, act, w_down)
+
+
+PIECES = 8
+
+
+def hand_over_kernel(x_hbm, out_hbm, buf, in_sem, out_sem):
+    def rows(i):
+        return pl.ds(i * (TOKENS // PIECES), TOKENS // PIECES)
+    reads = [pltpu.make_async_copy(x_hbm.at[rows(i)], buf.at[i], in_sem.at[i]) for i in range(PIECES)]
+    writes = [pltpu.make_async_copy(buf.at[i], out_hbm.at[rows(i)], out_sem.at[i]) for i in range(PIECES)]
+    for copy in reads:
+        copy.start()
+    for read, write in zip(reads, writes):
+        read.wait()
+        write.start()
+    for copy in writes:
+        copy.wait()
+
+
+def hand_over(x):
+    any_spec = pl.BlockSpec(memory_space=pl.ANY)
+    return pl.pallas_call(
+        hand_over_kernel,
+        name='hand_over',
+        out_shape=jax.ShapeDtypeStruct(x.shape, x.dtype),
+        in_specs=[any_spec],
+        out_specs=any_spec,
+        scratch_shapes=[pltpu.VMEM((PIECES, TOKENS // PIECES, HIDDEN), BF16), pltpu.SemaphoreType.DMA((PIECES,)), pltpu.SemaphoreType.DMA((PIECES,))],
+        compiler_params=pltpu.CompilerParams(vmem_limit_bytes=VMEM_LIMIT),
+    )(x)
 
 
 def rope_table():
@@ -727,8 +794,8 @@
             positions, x, norm_att.reshape(1, HIDDEN), jnp.asarray(table), positions.reshape(1, TOKENS), att_ids.T, router_att.T,
             kv_rows, w_query, k_cache.reshape(flat), v_cache.reshape(flat))
         x_mid = attend(positions, att_cols, att_gates, q, k_new, v_new, w_out, x)
-        act, mlp_gates = gate_up(x_mid, norm_mlp.reshape(1, HIDDEN), router_mlp.T, mlp_ids.T, w_gate, w_up)
-        x_out = down_project(mlp_gates, x_mid, act, w_down)
+        act, mlp_gates, early = gate_up(x_mid, norm_mlp.reshape(1, HIDDEN), router_mlp.T, mlp_ids.T, w_gate, w_up, w_down)
+        x_out = hand_over(down_project(mlp_gates, early, x_mid, act, w_down))
         return x_out, k_new.reshape(k_cache.shape), v_new.reshape(v_cache.shape)
 
     token_spec = P('dp', None)

time: 174 us -> 170 us (0.977)
  local copies, waits for them, and re-layouts: 3.16 us -> 0 us
  Pallas kernels: 170 us -> 168 us
    pallas_call x1, Pallas kernels: 49 us -> 34.7 us  [down_project(): pl.pallas_call(down_kernel, name='down_project', out_shape=jax.ShapeDtype...]
    pallas_call x1, Pallas kernels: 36.3 us -> 46.7 us  [gate_up(): pl.pallas_call(gate_up_kernel, name='gate_up', out_shape=(jax.ShapeDtypeS...]
    unnamed x1 -> x0, local copies, waits for them, and re-layouts: 3.16 us -> none
    pallas_call x0 -> x1, Pallas kernels: none -> 2.39 us  [hand_over(): pl.pallas_call(hand_over_kernel, name='hand_over', out_shape=jax.ShapeDty...]
where the time goes in v5:
time: 170 us; the launch traced here: 168 us
  Pallas kernels  168 us (99%)
    pallas_call x1, Pallas kernels, attend(): pl.pallas_call(attend_kernel, name='attend', out_shape=jax.ShapeDtypeStru...  50.3 us
    pallas_call x1, Pallas kernels, gate_up(): pl.pallas_call(gate_up_kernel, name='gate_up', out_shape=(jax.ShapeDtypeS...  46.7 us
    pallas_call x1, Pallas kernels, down_project(): pl.pallas_call(down_kernel, name='down_project', out_shape=jax.ShapeDtype...  34.7 us
    pallas_call x1, Pallas kernels, project(): pl.pallas_call(project_kernel, name='project', out_shape=(cache, cache, j...  33.4 us

profile of v5, /device:TPU:0, one launch (start us, length us, event | category | flops | bytes accessed | tf_op | source)
XLA Modules:
  0.0 168.4 jit_solution(17295570985470200044)
XLA Ops:
  0.6 33.4 %project.1 = (bf16[512,128,128]{2,1,0:T(8,128)(2,1)}, bf16[512,128,128]{2,1,0:T(8,128)(2,1)}, bf16[4096,256]{1,0:T(8,128)(2,1)}, f32[512,8]{1,0:T(8,128)}, s32[512,8]{1,0:T(8,128)}) custom-call(s32[512]{0:T(512)} %pos_ref.3, bf16[512,2048]{1,0:T(8,128)(2,1)} %x_hbm.1, f32[1,2048]{1,0:T(1,128)} %bitcast.24, bf16[128,256]{1,0:T(8,128)(2,1)} %constant.2.clone.table_ref, ...), custom_call_target="tpu_custom_call" | custom-call | tf_op jit(solution)/shard_map/project/pallas_call | solution.py:230
  34.0 50.3 %attend.1.x_ref.x_hbm = bf16[512,2048]{1,0:T(8,128)(2,1)} custom-call(s32[512]{0:T(512)} %pos_ref.3, s32[512,8]{1,0:T(8,128)} %get-tuple-element.11.ids_ref, f32[512,8]{1,0:T(8,128)} %get-tuple-element.12.gates_ref, bf16[4096,256]{1,0:T(8,128)(2,1)} %get-tuple-element.13.q_hbm, bf16[512,128,128]{2,1,0:T(8,128)(2,1)} %get-tuple-element.14.kc_hbm, ...), custom_call_target="tpu_custom_call" | custom-call | tf_op jit(solution)/shard_map/attend/pallas_call | solution.py:476
  84.3 46.7 %gate_up.1 = (bf16[2,512,5632]{2,1,0:T(8,128)(2,1)}, f32[512,8]{1,0:T(8,128)}, f32[2,512,256]{2,1,0:T(8,128)}) custom-call(bf16[512,2048]{1,0:T(8,128)(2,1)} %attend.1.x_ref.x_hbm, f32[1,2048]{1,0:T(1,128)} %bitcast.25, bf16[8,2048]{1,0:T(8,128)(2,1)} %bitcast.22, s32[2,512]{1,0:T(2,128)} %bitcast.27, bf16[2,2048,5632]{2,1,0:T(8,128)(2,1)} %wg_hbm.1, ...), custom_call_target="tpu_custom_call" | custom-call | tf_op jit(solution)/shard_map/gate_up/pallas_call | solution.py:623
  131.1 34.7 %down_project.1.x_hbm = bf16[512,2048]{1,0:T(8,128)(2,1)} custom-call(f32[512,8]{1,0:T(8,128)} %get-tuple-element.16.gates_ref, f32[2,512,256]{2,1,0:T(8,128)} %get-tuple-element.17.early_ref, bf16[512,2048]{1,0:T(8,128)(2,1)} %attend.1.x_ref.x_hbm, bf16[2,512,5632]{2,1,0:T(8,128)(2,1)} %get-tuple-element.18.a_hbm, bf16[2,5632,2048]{2,1,0:T(8,128)(2,1)} %w_hbm.3), custom_call_target="tpu_custom_call" | custom-call | tf_op jit(solution)/shard_map/down_project/pallas_call | solution.py:724
  165.8 2.4 %hand_over.1 = bf16[512,2048]{1,0:T(8,128)(2,1)} custom-call(bf16[512,2048]{1,0:T(8,128)(2,1)} %down_project.1.x_hbm), custom_call_target="tpu_custom_call" | custom-call | tf_op jit(solution)/shard_map/hand_over/pallas_call | solution.py:760

commit v6 on v5

--- a/solution.py
+++ b/solution.py
@@ -85,10 +85,10 @@
     return lax.dot_general(a, b, (((1,), (1,)), ((), ())), preferred_element_type=F32)
 
 
-def project_kernel(pos_ref, x_ref, gain_ref, table_ref, posrow_ref, idst_ref, router_ref, wkv_hbm, wq_hbm, kc_hbm, vc_hbm,
-                   ko_hbm, vo_hbm, q_ref, gates_ref, ids_ref,
-                   hid, wraw, wtmp, wkv, wq, kbuf, vbuf, qsel, qrow, knv, cos_s, sin_s,
-                   wkv_sem, wq_sem, kin_sem, vin_sem, kout_sem, vout_sem):
+def attend_kernel(pos_ref, x_ref, gain_ref, table_ref, posrow_ref, idst_ref, router_ref, wkv_hbm, wq_hbm, kc_hbm, vc_hbm,
+                  ko_hbm, vo_hbm, o_ref, gates_ref, ids_ref,
+                  hid, wraw, wtmp, wkv, wq, kbuf, vbuf, qsel, qrow, qdiag, knv, probs, orow, cos_s, sin_s,
+                  wkv_sem, wq_sem, kin_sem, vin_sem, kout_sem, vout_sem):
     def block_of(ref, b):
         return ref.at[pl.ds(pl.multiple_of(b * BLOCK, BLOCK), BLOCK)]
 
@@ -116,9 +116,6 @@
     norm_rows(x_ref, gain_ref, hid)
     for e in range(1, WQ_RING):
         load_wq(jnp.int32(e)).start()
-    for b in range(3, RING):
-        for copy in load(jnp.int32(b)):
-            copy.start()
     ids = turn((idst_ref[0:1, :], idst_ref[1:2, :], posrow_ref[...]))
     ids_ref[...] = ids
     id0 = ids[:, 0:1]
@@ -154,53 +151,28 @@
         return carry
     lax.fori_loop(0, TOKENS // ROWS, kv_body, 0)
 
-    sub16 = iota((16, HEAD_DIM), 0) >> 2
-    low = iota((8, 128), 0) < 4
-
-    def block_body(b, carry):
-        e = lax.div(b, 2)
-        m = lax.rem(b, 2)
-        slot = lax.rem(b, RING)
-        wslot = lax.rem(e, WQ_RING)
-
-        @pl.when(m == 0)
+    def q_body(e, carry):
+        @pl.when(e + 3 < RING)
         def _():
-            load_wq(e).wait()
-        for copy in load(b):
-            copy.wait()
-        rows = pl.ds(pl.multiple_of(m * ROWS, ROWS), ROWS)
-        q = dot(hid[rows, :], wq[wslot])
-        for t in range(BLOCK):
-            place = pos_ref[b * BLOCK + t]
-            lines = pl.ds(pl.multiple_of((place >> 2) * 16, 16), 16)
-            put = sub16 == (place & 3)
-            both = knv[pl.ds(pl.multiple_of((b * BLOCK + t) * 8, 8), 8), :]
-            swapped = pltpu.roll(both, 4, 0)
-            for n8, buf in ((jnp.where(low, both, swapped), kbuf), (jnp.where(low, swapped, both), vbuf)):
-                n16 = jnp.concatenate([n8, n8], axis=0)
-                old = buf[slot, t, lines, :].astype(F32)
-                buf[slot, t, lines, :] = jnp.where(put, n16, old).astype(BF16)
-        for k in range(2):
-            picked = ids_ref[rows, k:k + 1] == e
-            qsel[k, rows, :] = jnp.where(picked, q, qsel[k, rows, :])
-        for copy in save(b):
-            copy.start()
-
-        @pl.when((m == 1) & (e + WQ_RING < EXPERTS))
+            for copy in load(e + 3):
+                copy.start()
+        load_wq(e).wait()
+        slot = lax.rem(e, WQ_RING)
+
+        def m_body(m, c):
+            rows = pl.ds(pl.multiple_of(m * ROWS, ROWS), ROWS)
+            q = dot(hid[rows, :], wq[slot])
+            for k in range(2):
+                picked = ids_ref[rows, k:k + 1] == e
+                qsel[k, rows, :] = jnp.where(picked, q, qsel[k, rows, :])
+            return c
+        lax.fori_loop(0, TOKENS // ROWS, m_body, 0)
+
+        @pl.when(e + WQ_RING < EXPERTS)
         def _():
             load_wq(e + WQ_RING).start()
-
-        @pl.when(b >= 2)
-        def _():
-            for copy in save(b - 2):
-                copy.wait()
-
-            @pl.when(b - 2 + RING < BLOCKS)
-            def _():
-                for copy in load(b - 2 + RING):
-                    copy.start()
-        return carry
-    lax.fori_loop(0, BLOCKS, block_body, 0)
+        return carry
+    lax.fori_loop(0, EXPERTS, q_body, 0)
 
     def rope_body(m, carry):
         rows = pl.ds(pl.multiple_of(m * 128, 128), 128)
@@ -213,24 +185,107 @@
         q = qrow[...]
         even = (iota((1024, HEAD_DIM), 0) & 8) == 0
         lines = pl.ds(pl.multiple_of(m * 1024, 1024), 1024)
-        q_ref[lines, :HEAD_DIM] = jnp.where(even, q, 0.0).astype(BF16)
-        q_ref[lines, HEAD_DIM:] = jnp.where(even, 0.0, q).astype(BF16)
+        qdiag[lines, :HEAD_DIM] = jnp.where(even, q, 0.0).astype(BF16)
+        qdiag[lines, HEAD_DIM:] = jnp.where(even, 0.0, q).astype(BF16)
         return carry
     lax.fori_loop(0, TOKENS // 128, rope_body, 0)
+
+    scale = HEAD_DIM ** -0.5
+    sub16 = iota((16, HEAD_DIM), 0) >> 2
+    low = iota((8, 128), 0) < 4
+    row16 = iota((16, 128), 0)
+    lane = iota((16, 128), 1)
+    upper = row16 < 8
+    same_head = (lane & 3) == (row16 & 3)
+    slot_of = lane >> 2
+
+    def block_body(i, carry):
+        b = jnp.minimum(i, BLOCKS - 1)
+        prev = jnp.maximum(i - 1, 0)
+        slot = lax.rem(b, RING)
+        prev_slot = lax.rem(prev, RING)
+        side = lax.rem(i, 2)
+
+        @pl.when(i < BLOCKS)
+        def _():
+            for copy in load(b):
+                copy.wait()
+        places = [pos_ref[b * BLOCK + t] for t in range(BLOCK)]
+
+        def patch(t):
+            rows = pl.ds(pl.multiple_of((places[t] >> 2) * 16, 16), 16)
+            put = sub16 == (places[t] & 3)
+            both = knv[pl.ds(pl.multiple_of((b * BLOCK + t) * 8, 8), 8), :]
+            swapped = pltpu.roll(both, 4, 0)
+            for n8, buf in ((jnp.where(low, both, swapped), kbuf), (jnp.where(low, swapped, both), vbuf)):
+                n16 = jnp.concatenate([n8, n8], axis=0)
+                old = buf[slot, t, rows, :].astype(F32)
+                buf[slot, t, rows, :] = jnp.where(put, n16, old).astype(BF16)
+
+        def score(j):
+            t = b * BLOCK + 2 * j
+            q = qdiag[pl.ds(pl.multiple_of(t * 8, 16), 16), :]
+            keys = jnp.concatenate([kbuf[slot, 2 * j], kbuf[slot, 2 * j + 1]], axis=1)
+            s = dot_nt(q, keys) * scale
+            s = jnp.where(same_head & (slot_of <= jnp.where(upper, places[2 * j], places[2 * j + 1])), s, NEG)
+            e = jnp.exp(s - jnp.max(s, axis=1, keepdims=True))
+            probs[side, j] = (e / jnp.sum(e, axis=1, keepdims=True)).astype(BF16)
+
+        def mix(j):
+            values = jnp.concatenate([vbuf[prev_slot, 2 * j], vbuf[prev_slot, 2 * j + 1]], axis=1)
+            o = dot(probs[1 - side, j], values)
+            orow[j * 16:j * 16 + 8, :] = o[:8, :HEAD_DIM]
+            orow[j * 16 + 8:j * 16 + 16, :] = o[8:, HEAD_DIM:]
+
+        half = BLOCK // 2
+        pairs = BLOCK // 2
+        first, second = range(pairs // 2), range(pairs // 2, pairs)
+        for t in range(half):
+            patch(t)
+        for j in first:
+            score(j)
+        for t in range(half, BLOCK):
+            patch(t)
+        for j in first:
+            mix(j)
+        for j in second:
+            score(j)
+        for j in second:
+            mix(j)
+        rows = pl.ds(pl.multiple_of(prev * BLOCK, BLOCK), BLOCK)
+        for r in range(8):
+            o_ref[rows, r * 128:(r + 1) * 128] = orow[pl.ds(r, BLOCK, stride=8), :].astype(BF16)
+
+        @pl.when(i >= 1)
+        def _():
+            for copy in save(prev):
+                copy.start()
+
+        @pl.when(i >= 3)
+        def _():
+            for copy in save(i - 3):
+                copy.wait()
+
+            @pl.when(i - 3 + RING < BLOCKS)
+            def _():
+                for copy in load(i - 3 + RING):
+                    copy.start()
+        return carry
+    lax.fori_loop(0, BLOCKS + 1, block_body, 0)
     for b in (BLOCKS - 2, BLOCKS - 1):
         for copy in save(jnp.int32(b)):
             copy.wait()
 
 
-def project(positions, x, gain, table, pos_row, ids_t, router_t, w_kv, w_query, k_cache, v_cache):
+def attend(positions, x, gain, table, pos_row, ids_t, router_t, w_kv, w_query, k_cache, v_cache):
     any_spec = pl.BlockSpec(memory_space=pl.ANY)
     vmem = pl.BlockSpec(memory_space=pltpu.VMEM)
     smem = pl.BlockSpec(memory_space=pltpu.SMEM)
     cache = jax.ShapeDtypeStruct(k_cache.shape, BF16)
     return pl.pallas_call(
-        project_kernel,
-        name='project',
-        out_shape=(cache, cache, jax.ShapeDtypeStruct((TOKENS * 8, 2 * HEAD_DIM), BF16),
+        attend_kernel,
+        name='attend',
+        out_shape=(cache, cache, jax.ShapeDtypeStruct((TOKENS, 2 * QUERY_COLS), BF16),
                    jax.ShapeDtypeStruct((TOKENS, EXPERTS), F32), jax.ShapeDtypeStruct((TOKENS, EXPERTS), jnp.int32)),
         in_specs=[smem] + [vmem] * 6 + [any_spec] * 4,
         out_specs=(any_spec, any_spec, vmem, vmem, vmem),
@@ -244,7 +299,10 @@
             pltpu.VMEM((RING, BLOCK, SLOTS * HEADS, HEAD_DIM), BF16),
             pltpu.VMEM((2, TOKENS, QUERY_COLS), F32),
             pltpu.VMEM((1024, HEAD_DIM), F32),
+            pltpu.VMEM((TOKENS * 8, 2 * HEAD_DIM), BF16),
             pltpu.VMEM((TOKENS * 8, HEAD_DIM), F32),
+            pltpu.VMEM((2, BLOCK // 2, 16, HEAD_DIM), BF16),
+            pltpu.VMEM((BLOCK * 8, HEAD_DIM), F32),
             pltpu.VMEM((TOKENS, HEAD_DIM), F32),
             pltpu.VMEM((TOKENS, HEAD_DIM), F32),
             pltpu.SemaphoreType.DMA,
@@ -344,157 +402,93 @@
             + [pltpu.VMEM((chunks, height, width), BF16)] * 6 + [pltpu.SemaphoreType.DMA((chunks,))] * 6)
 
 
-A_RING = 6
-A_AHEAD = 4
-A_ROWS = 128
-PARTS = TOKENS // A_ROWS
-PART_BLOCKS = A_ROWS // BLOCK
-
-
-def attend_kernel(pos_ref, ids_ref, gates_ref, q_hbm, kc_hbm, vc_hbm, w_hbm, x_hbm, out_ref,
-                  qbuf, kbuf, vbuf, probs, orow, mixed, spread, wbuf, q_sem, k_sem, v_sem, w_sem, *chunk_refs):
-    def load(b):
-        slot = lax.rem(b, A_RING)
-        rows = pl.ds(pl.multiple_of(b * BLOCK, BLOCK), BLOCK)
-        return (pltpu.make_async_copy(kc_hbm.at[rows], kbuf.at[slot], k_sem.at[slot]),
-                pltpu.make_async_copy(vc_hbm.at[rows], vbuf.at[slot], v_sem.at[slot]))
-
-    q_copy = pltpu.make_async_copy(q_hbm, qbuf, q_sem)
-    q_copy.start()
-    for b in range(A_AHEAD):
-        for copy in load(jnp.int32(b)):
-            copy.start()
-    w_copies = [pltpu.make_async_copy(w_hbm.at[e], wbuf.at[e], w_sem.at[e]) for e in range(EXPERTS)]
-
-    scale = HEAD_DIM ** -0.5
-    row16 = iota((16, 128), 0)
-    lane = iota((16, 128), 1)
-    upper = row16 < 8
-    same_head = (lane & 3) == (row16 & 3)
-    slot_of = lane >> 2
-
-    def attend_rows(m):
-        def block_body(i, carry):
-            b = m * PART_BLOCKS + jnp.minimum(i, PART_BLOCKS - 1)
-            before = jnp.maximum(i - 1, 0)
-            prev = m * PART_BLOCKS + before
-            slot = lax.rem(b, A_RING)
-            prev_slot = lax.rem(prev, A_RING)
-            side = lax.rem(i, 2)
-
-            @pl.when(i < PART_BLOCKS)
-            def _():
-                for copy in load(b):
-                    copy.wait()
-
-            def score(j):
-                t = b * BLOCK + 2 * j
-                q = qbuf[pl.ds(pl.multiple_of(t * 8, 16), 16), :]
-                keys = jnp.concatenate([kbuf[slot, 2 * j], kbuf[slot, 2 * j + 1]], axis=1)
-                s = dot_nt(q, keys) * scale
-                s = jnp.where(same_head & (slot_of <= jnp.where(upper, pos_ref[t], pos_ref[t + 1])), s, NEG)
-                e = jnp.exp(s - jnp.max(s, axis=1, keepdims=True))
-                probs[side, j] = (e / jnp.sum(e, axis=1, keepdims=True)).astype(BF16)
-
-            def mix(j):
-                values = jnp.concatenate([vbuf[prev_slot, 2 * j], vbuf[prev_slot, 2 * j + 1]], axis=1)
-                o = dot(probs[1 - side, j], values)
-                orow[j * 16:j * 16 + 8, :] = o[:8, :HEAD_DIM]
-                orow[j * 16 + 8:j * 16 + 16, :] = o[8:, HEAD_DIM:]
-
-            pairs = BLOCK // 2
-            for j in range(pairs // 2):
-                score(j)
-            for j in range(pairs // 2):
-                mix(j)
-            for j in range(pairs // 2, pairs):
-                score(j)
-            for j in range(pairs // 2, pairs):
-                mix(j)
-            rows = pl.ds(pl.multiple_of(before * BLOCK, BLOCK), BLOCK)
-            for r in range(8):
-                mixed[rows, r * 128:(r + 1) * 128] = orow[pl.ds(r, BLOCK, stride=8), :].astype(BF16)
-
-            @pl.when((i < PART_BLOCKS) & (b + A_AHEAD < BLOCKS))
-            def _():
-                for copy in load(b + A_AHEAD):
-                    copy.start()
-            return carry
-        lax.fori_loop(0, PART_BLOCKS + 1, block_body, 0)
-
+OUT_RING = 4
+
+
+def out_kernel(o_ref, ids_ref, gates_ref, w_hbm, x_hbm, out_ref, spread, wbuf, w_sem, *chunk_refs):
+    core = lax.rem(lax.axis_index('tp'), 2)
+
+    def load_w(s):
+        half = lax.rem(core + 1 + s, 2)
+        cols = pl.ds(pl.multiple_of((half * (STEPS // 2) + lax.div(s, 2)) * COL, COL), COL)
+        slot = lax.rem(s, OUT_RING)
+        return pltpu.make_async_copy(w_hbm.at[:, :, cols], wbuf.at[slot], w_sem.at[slot])
+
+    for s in range(OUT_RING):
+        load_w(jnp.int32(s)).start()
+
+    def spread_rows(m):
         def spread_body(n, carry):
-            rows = pl.ds(pl.multiple_of(n * 64, 64), 64)
-            from_rows = pl.ds(pl.multiple_of(m * A_ROWS + n * 64, 64), 64)
-            first = mixed[rows, :QUERY_COLS].astype(F32)
-            second = mixed[rows, QUERY_COLS:].astype(F32)
+            rows = pl.ds(pl.multiple_of(m * ROWS + n * 64, 64), 64)
+            first = o_ref[rows, :QUERY_COLS].astype(F32)
+            second = o_ref[rows, QUERY_COLS:].astype(F32)
             for e in range(EXPERTS):
-                picked = jnp.where(ids_ref[from_rows, 0:1] == e, first, 0.0)
-                picked = jnp.where(ids_ref[from_rows, 1:2] == e, second, picked)
+                picked = jnp.where(ids_ref[rows, 0:1] == e, first, 0.0)
+                picked = jnp.where(ids_ref[rows, 1:2] == e, second, picked)
                 spread[e, rows, :] = picked.astype(BF16)
             return carry
-        lax.fori_loop(0, A_ROWS // 64, spread_body, 0)
+        lax.fori_loop(0, ROWS // 64, spread_body, 0)
 
     def partial(s, rows, col):
-        acc = jnp.zeros((A_ROWS, HIDDEN // 2), F32)
+        slot = lax.rem(s, OUT_RING)
+        acc = jnp.zeros((ROWS, COL), F32)
         for e in range(EXPERTS):
-            acc = acc + gates_ref[rows, e:e + 1] * dot(spread[e], wbuf[e, :, pl.ds(col, HIDDEN // 2)])
+            acc = acc + gates_ref[rows, e:e + 1] * dot(spread[e, rows, :], wbuf[slot, e])
         return acc
 
     def drive(chunk_step, column, finish, base_copy):
-        q_copy.wait()
-        for copy in w_copies:
-            copy.start()
-
-        def part_body(m, carry):
-            attend_rows(m)
-
-            @pl.when(m == 0)
+        def col_body(i, carry):
+            for parity in range(2):
+                load_w(2 * i + parity).wait()
+
+            def row_body(m, c):
+                @pl.when(i == 0)
+                def _():
+                    spread_rows(m)
+                for parity in range(2):
+                    chunk_step(i, parity, m)
+                return c
+            lax.fori_loop(0, TOKENS // ROWS, row_body, 0)
+
+            @pl.when(2 * i + OUT_RING < STEPS)
+            def _():
+                for parity in range(2):
+                    load_w(2 * i + OUT_RING + parity).start()
+
+            @pl.when(i == 0)
             def _():
                 base_copy.start()
-                for copy in w_copies:
-                    copy.wait()
-            for parity in range(2):
-                chunk_step(0, parity, m)
-
-            @pl.when(m == 1)
+
+            @pl.when(i == 1)
             def _():
                 base_copy.wait()
 
-            @pl.when(m >= 2)
+            @pl.when(i >= 2)
             def _():
-                finish(m - 2)
+                finish(2 * (i - 2))
+                finish(2 * (i - 2) + 1)
             return carry
-        lax.fori_loop(0, PARTS, part_body, 0)
-        return PARTS - 2
+        lax.fori_loop(0, STEPS // 2, col_body, 0)
+        return CHUNKS // 2
 
     reduce_columns(drive, partial, x_hbm, out_ref, *chunk_refs)
 
 
-def attend(positions, ids, gates, q, k_cache, v_cache, w_out, x):
+def out_project(o, ids, gates, w_out, x):
     vmem = pl.BlockSpec(memory_space=pltpu.VMEM)
-    any_spec = pl.BlockSpec(memory_space=pl.ANY)
     return pl.pallas_call(
-        attend_kernel,
-        name='attend',
+        out_kernel,
+        name='out_project',
         out_shape=jax.ShapeDtypeStruct((TOKENS, HIDDEN), BF16),
-        in_specs=[pl.BlockSpec(memory_space=pltpu.SMEM)] + [vmem] * 2 + [any_spec] * 5,
+        in_specs=[vmem] * 3 + [pl.BlockSpec(memory_space=pl.ANY)] * 2,
         out_specs=vmem,
         scratch_shapes=[
-            pltpu.VMEM((TOKENS * 8, 2 * HEAD_DIM), BF16),
-            pltpu.VMEM((A_RING, BLOCK, SLOTS * HEADS, HEAD_DIM), BF16),
-            pltpu.VMEM((A_RING, BLOCK, SLOTS * HEADS, HEAD_DIM), BF16),
-            pltpu.VMEM((2, BLOCK // 2, 16, HEAD_DIM), BF16),
-            pltpu.VMEM((BLOCK * 8, HEAD_DIM), F32),
-            pltpu.VMEM((A_ROWS, 2 * QUERY_COLS), BF16),
-            pltpu.VMEM((EXPERTS, A_ROWS, QUERY_COLS), BF16),
-            pltpu.VMEM((EXPERTS, QUERY_COLS, HIDDEN), BF16),
-            pltpu.SemaphoreType.DMA,
-            pltpu.SemaphoreType.DMA((A_RING,)),
-            pltpu.SemaphoreType.DMA((A_RING,)),
-            pltpu.SemaphoreType.DMA((EXPERTS,)),
-        ] + chunk_scratch(A_ROWS, HIDDEN // 2),
+            pltpu.VMEM((EXPERTS, TOKENS, QUERY_COLS), BF16),
+            pltpu.VMEM((OUT_RING, EXPERTS, QUERY_COLS, COL), BF16),
+            pltpu.SemaphoreType.DMA((OUT_RING,)),
+        ] + chunk_scratch(ROWS, COL),
         compiler_params=pltpu.CompilerParams(vmem_limit_bytes=VMEM_LIMIT, collective_id=0, has_side_effects=True),
-    )(positions, ids, gates, q, k_cache, v_cache, w_out, x)
+    )(o, ids, gates, w_out, x)
 
 
 def gate_up_kernel(x_ref, gain_ref, router_ref, idst_ref, wg_hbm, wu_hbm, wd_hbm, a_hbm, gates_ref, early_ref,
@@ -790,10 +784,10 @@
     def local_step(x, k_cache, v_cache, positions, att_ids, mlp_ids, norm_att, w_kv, router_att, w_query, w_out, norm_mlp, router_mlp, w_gate, w_up, w_down):
         flat = (TOKENS, SLOTS * HEADS, HEAD_DIM)
         kv_rows = w_kv.reshape(HIDDEN, HEADS, 2, HEAD_DIM).transpose(0, 2, 1, 3).reshape(HIDDEN * 8, HEAD_DIM)
-        k_new, v_new, q, att_gates, att_cols = project(
+        k_new, v_new, o, att_gates, att_cols = attend(
             positions, x, norm_att.reshape(1, HIDDEN), jnp.asarray(table), positions.reshape(1, TOKENS), att_ids.T, router_att.T,
             kv_rows, w_query, k_cache.reshape(flat), v_cache.reshape(flat))
-        x_mid = attend(positions, att_cols, att_gates, q, k_new, v_new, w_out, x)
+        x_mid = out_project(o, att_cols, att_gates, w_out, x)
         act, mlp_gates, early = gate_up(x_mid, norm_mlp.reshape(1, HIDDEN), router_mlp.T, mlp_ids.T, w_gate, w_up, w_down)
         x_out = hand_over(down_project(mlp_gates, early, x_mid, act, w_down))
         return x_out, k_new.reshape(k_cache.shape), v_new.reshape(v_cache.shape)

time: 170 us -> 166 us (0.976)
  Pallas kernels: 168 us -> 164 us
    pallas_call x1, Pallas kernels: 46.7 us -> 41 us  [gate_up(): pl.pallas_call(gate_up_kernel, name='gate_up', out_shape=(jax.ShapeDtypeS...]
    pallas_call x1, Pallas kernels: 34.7 us -> 39.9 us  [down_project(): pl.pallas_call(down_kernel, name='down_project', out_shape=jax.ShapeDtype...]
    pallas_call x2, Pallas kernels: 83.7 us -> 80.6 us  [the longest x1 44.4 us: attend(): pl.pallas_call(attend_kernel, name='attend', out_shape=(cache, cache, jax...]
where the time goes in v6:
time: 166 us; the launch traced here: 165 us
  Pallas kernels  164 us (99%)
    pallas_call x1, Pallas kernels, attend(): pl.pallas_call(attend_kernel, name='attend', out_shape=(cache, cache, jax...  44.4 us
    pallas_call x1, Pallas kernels, gate_up(): pl.pallas_call(gate_up_kernel, name='gate_up', out_shape=(jax.ShapeDtypeS...  41 us
    pallas_call x1, Pallas kernels, down_project(): pl.pallas_call(down_kernel, name='down_project', out_shape=jax.ShapeDtype...  39.9 us
    pallas_call x1, Pallas kernels, out_project(): pl.pallas_call(out_kernel, name='out_project', out_shape=jax.ShapeDtypeSt...  36.2 us

profile of v6, /device:TPU:0, one launch (start us, length us, event | category | flops | bytes accessed | tf_op | source)
XLA Modules:
  0.0 164.7 jit_solution(1114976431671665720)
XLA Ops:
  0.6 44.4 %attend.1 = (bf16[512,128,128]{2,1,0:T(8,128)(2,1)}, bf16[512,128,128]{2,1,0:T(8,128)(2,1)}, bf16[512,1024]{1,0:T(8,128)(2,1)}, f32[512,8]{1,0:T(8,128)}, s32[512,8]{1,0:T(8,128)}) custom-call(s32[512]{0:T(512)} %pos_ref.1, bf16[512,2048]{1,0:T(8,128)(2,1)} %x_hbm.1, f32[1,2048]{1,0:T(1,128)} %bitcast.21, bf16[128,256]{1,0:T(8,128)(2,1)} %constant.2.clone.table_ref, ...), custom_call_target="tpu_custom_call" | custom-call | tf_op jit(solution)/shard_map/attend/pallas_call | solution.py:285
  45.1 36.2 %out_project.1.x_ref.x_hbm = bf16[512,2048]{1,0:T(8,128)(2,1)} custom-call(bf16[512,1024]{1,0:T(8,128)(2,1)} %get-tuple-element.11.o_ref, s32[512,8]{1,0:T(8,128)} %get-tuple-element.12.ids_ref, f32[512,8]{1,0:T(8,128)} %get-tuple-element.13.gates_ref, bf16[8,512,2048]{2,1,0:T(8,128)(2,1)} %w_hbm.2, bf16[512,2048]{1,0:T(8,128)(2,1)} %x_hbm.1), custom_call_target="tpu_custom_call" | custom-call | tf_op jit(solution)/shard_map/out_project/pallas_call | solution.py:479
  81.2 41.0 %gate_up.1 = (bf16[2,512,5632]{2,1,0:T(8,128)(2,1)}, f32[512,8]{1,0:T(8,128)}, f32[2,512,256]{2,1,0:T(8,128)}) custom-call(bf16[512,2048]{1,0:T(8,128)(2,1)} %out_project.1.x_ref.x_hbm, f32[1,2048]{1,0:T(1,128)} %bitcast.22, bf16[8,2048]{1,0:T(8,128)(2,1)} %bitcast.20, s32[2,512]{1,0:T(2,128)} %bitcast.25, bf16[2,2048,5632]{2,1,0:T(8,128)(2,1)} %wg_hbm.1, ...), custom_call_target="tpu_custom_call" | custom-call | tf_op jit(solution)/shard_map/gate_up/pallas_call | solution.py:617
  122.2 39.9 %down_project.1.x_hbm = bf16[512,2048]{1,0:T(8,128)(2,1)} custom-call(f32[512,8]{1,0:T(8,128)} %get-tuple-element.14.gates_ref, f32[2,512,256]{2,1,0:T(8,128)} %get-tuple-element.15.early_ref, bf16[512,2048]{1,0:T(8,128)(2,1)} %out_project.1.x_ref.x_hbm, bf16[2,512,5632]{2,1,0:T(8,128)(2,1)} %get-tuple-element.16.a_hbm, bf16[2,5632,2048]{2,1,0:T(8,128)(2,1)} %w_hbm.3), custom_call_target="tpu_custom_call" | custom-call | tf_op jit(solution)/shard_map/down_project/pallas_call | solution.py:718
  162.1 2.4 %hand_over.1 = bf16[512,2048]{1,0:T(8,128)(2,1)} custom-call(bf16[512,2048]{1,0:T(8,128)(2,1)} %down_project.1.x_hbm), custom_call_target="tpu_custom_call" | custom-call | tf_op jit(solution)/shard_map/hand_over/pallas_call | solution.py:754

commit v7 on v6

--- a/solution.py
+++ b/solution.py
@@ -139,17 +139,13 @@
         return carry
     lax.fori_loop(0, HIDDEN // 128, sort_body, 0)
 
-    def kv_body(m, carry):
-        rows = pl.ds(pl.multiple_of(m * ROWS, ROWS), ROWS)
-        kv = dot(hid[rows, :], wkv[...])
-        cos = cos_s[rows, :]
-        sin = sin_s[rows, :]
-        for h in range(HEADS):
-            k = kv[:, h * 128:(h + 1) * 128]
-            knv[pl.ds(m * (ROWS * 8) + h, ROWS, stride=8), :] = k * cos + pltpu.roll(k, 64, 1) * sin
-            knv[pl.ds(m * (ROWS * 8) + h + 4, ROWS, stride=8), :] = kv[:, (h + 4) * 128:(h + 5) * 128]
-        return carry
-    lax.fori_loop(0, TOKENS // ROWS, kv_body, 0)
+    keys_new = dot(hid[...], wkv[:, :QUERY_COLS])
+    for h in range(HEADS):
+        k = keys_new[:, h * 128:(h + 1) * 128]
+        knv[pl.ds(h, TOKENS, stride=8), :] = k * cos_s[...] + pltpu.roll(k, 64, 1) * sin_s[...]
+    values_new = dot(hid[...], wkv[:, QUERY_COLS:])
+    for h in range(HEADS):
+        knv[pl.ds(h + 4, TOKENS, stride=8), :] = values_new[:, h * 128:(h + 1) * 128]
 
     def q_body(e, carry):
         @pl.when(e + 3 < RING)
@@ -159,14 +155,9 @@
         load_wq(e).wait()
         slot = lax.rem(e, WQ_RING)
 
-        def m_body(m, c):
-            rows = pl.ds(pl.multiple_of(m * ROWS, ROWS), ROWS)
-            q = dot(hid[rows, :], wq[slot])
-            for k in range(2):
-                picked = ids_ref[rows, k:k + 1] == e
-                qsel[k, rows, :] = jnp.where(picked, q, qsel[k, rows, :])
-            return c
-        lax.fori_loop(0, TOKENS // ROWS, m_body, 0)
+        q = dot(hid[...], wq[slot])
+        for k in range(2):
+            qsel[k] = jnp.where(ids_ref[:, k:k + 1] == e, q, qsel[k])
 
         @pl.when(e + WQ_RING < EXPERTS)
         def _():

time: 166 us -> 166 us (level)
  no operation moved by 1% of the time
where the time goes in v7:
time: 166 us; the launch traced here: 164 us
  Pallas kernels  163 us (98%)
    pallas_call x1, Pallas kernels, attend(): pl.pallas_call(attend_kernel, name='attend', out_shape=(cache, cache, jax...  42.9 us
    pallas_call x1, Pallas kernels, gate_up(): pl.pallas_call(gate_up_kernel, name='gate_up', out_shape=(jax.ShapeDtypeS...  41 us
    pallas_call x1, Pallas kernels, down_project(): pl.pallas_call(down_kernel, name='down_project', out_shape=jax.ShapeDtype...  40.7 us
    pallas_call x1, Pallas kernels, out_project(): pl.pallas_call(out_kernel, name='out_project', out_shape=jax.ShapeDtypeSt...  36.2 us

profile of v7, /device:TPU:0, one launch (start us, length us, event | category | flops | bytes accessed | tf_op | source)
XLA Modules:
  0.0 164.0 jit_solution(13826095587752004662)
XLA Ops:
  0.6 42.9 %attend.1 = (bf16[512,128,128]{2,1,0:T(8,128)(2,1)}, bf16[512,128,128]{2,1,0:T(8,128)(2,1)}, bf16[512,1024]{1,0:T(8,128)(2,1)}, f32[512,8]{1,0:T(8,128)}, s32[512,8]{1,0:T(8,128)}) custom-call(s32[512]{0:T(512)} %pos_ref.1, bf16[512,2048]{1,0:T(8,128)(2,1)} %x_hbm.1, f32[1,2048]{1,0:T(1,128)} %bitcast.21, bf16[128,256]{1,0:T(8,128)(2,1)} %constant.2.clone.table_ref, ...), custom_call_target="tpu_custom_call" | custom-call | tf_op jit(solution)/shard_map/attend/pallas_call | solution.py:276
  43.6 36.2 %out_project.1.x_ref.x_hbm = bf16[512,2048]{1,0:T(8,128)(2,1)} custom-call(bf16[512,1024]{1,0:T(8,128)(2,1)} %get-tuple-element.11.o_ref, s32[512,8]{1,0:T(8,128)} %get-tuple-element.12.ids_ref, f32[512,8]{1,0:T(8,128)} %get-tuple-element.13.gates_ref, bf16[8,512,2048]{2,1,0:T(8,128)(2,1)} %w_hbm.2, bf16[512,2048]{1,0:T(8,128)(2,1)} %x_hbm.1), custom_call_target="tpu_custom_call" | custom-call | tf_op jit(solution)/shard_map/out_project/pallas_call | solution.py:470
  79.8 41.0 %gate_up.1 = (bf16[2,512,5632]{2,1,0:T(8,128)(2,1)}, f32[512,8]{1,0:T(8,128)}, f32[2,512,256]{2,1,0:T(8,128)}) custom-call(bf16[512,2048]{1,0:T(8,128)(2,1)} %out_project.1.x_ref.x_hbm, f32[1,2048]{1,0:T(1,128)} %bitcast.22, bf16[8,2048]{1,0:T(8,128)(2,1)} %bitcast.20, s32[2,512]{1,0:T(2,128)} %bitcast.25, bf16[2,2048,5632]{2,1,0:T(8,128)(2,1)} %wg_hbm.1, ...), custom_call_target="tpu_custom_call" | custom-call | tf_op jit(solution)/shard_map/gate_up/pallas_call | solution.py:608
  120.7 40.7 %down_project.1.x_hbm = bf16[512,2048]{1,0:T(8,128)(2,1)} custom-call(f32[512,8]{1,0:T(8,128)} %get-tuple-element.14.gates_ref, f32[2,512,256]{2,1,0:T(8,128)} %get-tuple-element.15.early_ref, bf16[512,2048]{1,0:T(8,128)(2,1)} %out_project.1.x_ref.x_hbm, bf16[2,512,5632]{2,1,0:T(8,128)(2,1)} %get-tuple-element.16.a_hbm, bf16[2,5632,2048]{2,1,0:T(8,128)(2,1)} %w_hbm.3), custom_call_target="tpu_custom_call" | custom-call | tf_op jit(solution)/shard_map/down_project/pallas_call | solution.py:709
  161.4 2.4 %hand_over.1 = bf16[512,2048]{1,0:T(8,128)(2,1)} custom-call(bf16[512,2048]{1,0:T(8,128)(2,1)} %down_project.1.x_hbm), custom_call_target="tpu_custom_call" | custom-call | tf_op jit(solution)/shard_map/hand_over/pallas_call | solution.py:745
